TPU v7x, 32 devices: a whole 2x2x4 slice. The times are simulated.
32 devices in a mesh: pole: 4 (over x, core), rows: 8 (over z, y).
Axes of the slice: x: 2, y: 2, z: 4, core: 2. Of those that a mesh axis runs over, the one named last changes fastest.
Arguments:
- subspace: float32 [2, 256, 4096], P(None, None, 'rows'), may hold values from -6 to 6
- pivots: float32 [4, 16, 2, 256, 256], P('pole', 'rows'), may hold values from -0.25 to 0.25
- lower_blocks: float32 [4, 16, 2, 256, 256], P('pole', 'rows'), may hold values from -1 to 1
- upper_blocks: float32 [4, 16, 2, 256, 256], P('pole', 'rows'), may hold values from -1 to 1
- pole_weights: float32 [4, 2], P('pole'), may hold values from -4 to 4
Outputs:
- rotated_basis: float32 [2, 256, 4096], P(None, 'pole', 'rows')
All inputs are finite; a program needn't handle non-finite values.
Results may differ from a plain program's by a relative error of at most 0.00018.
Values sent between devices are 32-bit elements; how exact they have to be, the bound alone decides.
No kernel may reach another device: no remote copies, remote signals or barrier semaphores. Data moves between devices by JAX's collectives and lax.ppermute only.
A program may use at most 128 MiB of HBM per device.

v0:
```python
import jax
import jax.numpy as jnp
from jax import lax
from jax.sharding import PartitionSpec as P

NS_ITERS = 2


HIGH = lax.Precision.HIGHEST


def prefix(part, axis, combine, identity, reverse):
    count = lax.axis_size(axis)
    place = lax.axis_index(axis)
    ahead = count - 1 - place if reverse else place
    gathered = jax.tree.map(lambda a: lax.all_gather(a, axis), part)
    state = jax.tree.map(lambda a, e: jnp.zeros_like(a) + jnp.asarray(e, a.dtype), part, identity)

    def one(lap, state):
        source = count - 1 - lap if reverse else lap
        return combine(
            state, jax.tree.map(lambda a: lax.dynamic_index_in_dim(a, source, 0, False), gathered)
        )

    return lax.fori_loop(0, ahead, one, state)


def real_dot(first, second, dims):
    return lax.dot_general(
        first, second, (dims, ((), ())), precision=HIGH, preferred_element_type=jnp.float32
    )


def times_trans(left, matrix):
    dims = ((1,), (1,))
    real = real_dot(left[0], matrix[0], dims) - real_dot(left[1], matrix[1], dims)
    imag = real_dot(left[0], matrix[1], dims) + real_dot(left[1], matrix[0], dims)
    return jnp.stack([real, imag])


def complex_dot(left, right):
    dims = ((1,), (0,))
    real = real_dot(left[0], right[0], dims) - real_dot(left[1], right[1], dims)
    imag = real_dot(left[0], right[1], dims) + real_dot(left[1], right[0], dims)
    return jnp.stack([real, imag])


def gram_matrix(basis):
    dims = ((1,), (1,))
    real = real_dot(basis[0], basis[0], dims) + real_dot(basis[1], basis[1], dims)
    imag = real_dot(basis[0], basis[1], dims) - real_dot(basis[1], basis[0], dims)
    return jnp.stack([real, imag])


def rotate(mixing, basis):
    dims = ((0,), (0,))
    real = real_dot(mixing[0], basis[0], dims) - real_dot(mixing[1], basis[1], dims)
    imag = real_dot(mixing[0], basis[1], dims) + real_dot(mixing[1], basis[0], dims)
    return jnp.stack([real, imag])


def unit_matrix(size):
    return jnp.stack([jnp.eye(size, dtype=jnp.float32), jnp.zeros((size, size), jnp.float32)])


def newton_schulz(gram):
    unit = unit_matrix(gram.shape[1])
    frob = jnp.sqrt(jnp.sum(gram * gram))
    current = gram / frob
    inverse_root = unit
    for sweep in range(NS_ITERS):
        scale_factor = 1.5 * unit - 0.5 * complex_dot(inverse_root, current)
        current = complex_dot(current, scale_factor)
        inverse_root = complex_dot(scale_factor, inverse_root)
    return (inverse_root, frob)


def chain(earlier, later):
    return (complex_dot(earlier[0], later[0]), complex_dot(earlier[1], later[0]) + later[1])


def shards(subspace, pivots, lower_blocks, upper_blocks, pole_weights):
    width = pivots.shape[-1]
    count = pivots.shape[1]
    vectors = subspace.shape[1]
    pivot = pivots[0]
    lower = lower_blocks[0]
    upper = upper_blocks[0]
    pieces = subspace.reshape(2, vectors, count, width)
    unit = unit_matrix(width)
    blank = jnp.zeros((2, vectors, width), jnp.float32)
    forward = []
    carried = []
    for number in range(count):
        summand = times_trans(pieces[:, :, number, :], pivot[number])
        if number == 0:
            passing = -jnp.swapaxes(lower[0], 1, 2)
        else:
            summand = summand - times_trans(forward[-1], lower[number])
            passing = -times_trans(passing, lower[number])
        forward.append(summand)
        carried.append(passing)
    _, inflow = prefix((carried[-1], forward[-1]), "rows", chain, (unit, blank), False)
    swept = [forward[number] + complex_dot(inflow, carried[number]) for number in range(count)]
    backward = [None] * count
    reaches = [None] * count
    backward[count - 1] = swept[count - 1]
    reaches[count - 1] = -jnp.swapaxes(upper[count - 1], 1, 2)
    number = 0
    backward[number] = swept[number] - times_trans(backward[number + 1], upper[number])
    reaches[number] = -times_trans(reaches[number + 1], upper[number])
    _, outflow = prefix((reaches[0], backward[0]), "rows", chain, (unit, blank), True)
    solved = [backward[number] + complex_dot(outflow, reaches[number]) for number in range(count)]
    solution = jnp.stack(solved, axis=2).reshape(2, vectors, count * width)
    wreal = pole_weights[0, 0]
    wimag = pole_weights[0, 1]
    weighted = jnp.stack(
        [wreal * solution[0] - wimag * solution[1], wreal * solution[1] + wimag * solution[0]]
    )
    total_rows = count * width * lax.axis_size("rows")
    summed = lax.psum(weighted, "pole")
    gram = lax.psum(gram_matrix(summed), "rows")
    inverse_root, frob = newton_schulz(gram)
    columns = vectors // lax.axis_size("pole")
    mixing = lax.dynamic_slice_in_dim(inverse_root, lax.axis_index("pole") * columns, columns, 2)
    result = rotate(mixing, summed) * jnp.sqrt(total_rows / frob)
    return result


def solution(mesh):
    placed = (
        P(None, None, "rows"),
        P("pole", "rows", None, None, None),
        P("pole", "rows", None, None, None),
        P("pole", "rows", None, None, None),
        P("pole", None),
    )
    return jax.shard_map(
        shards, mesh=mesh, in_specs=placed, out_specs=P(None, "pole", "rows"), check_vma=False
    )
```

profile of v0, /device:TPU:0, one launch (start us, length us, event | category | flops | bytes accessed | tf_op | source)
XLA Modules:
  0.0 511.0 jit_solution(7689422893292195343)
XLA Ops:
  6.5 2.0 reshape.577
  24.2 67.8 %all-gather.7.cloned.1.call-done = f32[8,2,256,256]{3,2,1,0:T(8,128)} async-done(((f32[1,2,256,256]{3,2,1,0:T(8,128)}), f32[8,2,256,256]{3,2,1,0:T(8,128)}) %all-gather.7.cloned.1.call-update) | async-done | bytes 4194320 | tf_op jit(solution)/shard_map/all_gather | solution.py:16
  92.0 73.5 %all-gather.5.cloned.1.call-done = f32[8,2,256,256]{3,2,1,0:T(8,128)} async-done(((f32[1,2,256,256]{3,2,1,0:T(8,128)}), f32[8,2,256,256]{3,2,1,0:T(8,128)}) %all-gather.5.cloned.1.call-update) | async-done | bytes 4194320 | tf_op jit(solution)/shard_map/all_gather | solution.py:16
  175.6 63.3 %all-gather.9.cloned.1.call-done = f32[8,2,256,256]{3,2,1,0:T(8,128)} async-done(((f32[1,2,256,256]{3,2,1,0:T(8,128)}), f32[8,2,256,256]{3,2,1,0:T(8,128)}) %all-gather.9.cloned.1.call-update) | async-done | bytes 4194320 | tf_op jit(solution)/shard_map/all_gather | solution.py:16
  238.9 73.3 %all-gather.11.cloned.1.call-done = f32[8,2,256,256]{3,2,1,0:T(8,128)} async-done(((f32[1,2,256,256]{3,2,1,0:T(8,128)}), f32[8,2,256,256]{3,2,1,0:T(8,128)}) %all-gather.11.cloned.1.call-update) | async-done | bytes 4194320 | tf_op jit(solution)/shard_map/all_gather | solution.py:16
  312.3 53.4 %while.27 = (s32[]{:T(128)}, f32[2,256,256]{1,2,0:T(8,128)S(1)}, s32[]{:T(128)}, f32[8,2,256,256]{3,2,1,0:T(8,128)}, f32[8,2,256,256]{3,2,1,0:T(8,128)}, /*index...) while((s32[]{:T(128)}, f32[2,256,256]{1,2,0:T(8,128)S(1)}, s32[]{:T(128)}, f32[8,2,256,256]{3,2,1,0:T(8,128)}, ...), condition=%wide.region_3.4_spmd, body=%wide.region_2.3_spmd.sunk | while | flops 805699584 | bytes 7340219 | solution.py:25
  313.9 1.6 fusion.235
  321.5 1.6 fusion.235
  323.1 1.6 fusion.232
  324.7 1.6 fusion.233
  330.7 1.6 fusion.232
  332.3 1.6 fusion.233
  336.8 1.6 fusion.235
  338.3 1.6 fusion.232
  339.9 1.6 fusion.233
  344.4 1.6 fusion.235
  346.0 1.6 fusion.232
  347.5 1.6 fusion.233
  352.0 1.6 fusion.235
  353.6 1.6 fusion.232
  355.2 1.6 fusion.233
  359.7 1.6 fusion.235
  361.2 1.6 fusion.232
  362.8 1.6 fusion.233
  372.8 9.4 %all-reduce.6.cloned.1.call-start = ((), (), s32[]{:S(2)}) async-start(), calls=%async_computation.5 | async-start | bytes 1048576 | tf_op jit(solution)/shard_map/psum | solution.py:122
  382.2 24.3 %all-reduce.4.cloned.1.call-done = f32[2,256,512]{1,2,0:T(8,128)} async-done(((f32[2,256,512]{1,2,0:T(8,128)}), f32[2,256,512]{1,2,0:T(8,128)}) %all-reduce.4.cloned.1.call-update) | async-done | bytes 1048592 | tf_op jit(solution)/shard_map/psum | solution.py:121
  406.5 2.3 fusion.55
  408.7 2.2 fusion.54
  410.9 2.2 fusion.43
  413.2 2.2 fusion.42
  416.3 73.2 %all-reduce.6.cloned.1.call-done = f32[2,256,256]{2,1,0:T(8,128)} async-done(((f32[2,256,256]{2,1,0:T(8,128)}), f32[2,256,256]{2,1,0:T(8,128)}) %all-reduce.6.cloned.1.call-update) | async-done | bytes 524304 | tf_op jit(solution)/shard_map/psum | solution.py:122
  489.5 1.8 multiply_reduce_fusion
  (201 shorter events, 69.5 us)
Async XLA Ops:
  6.5 2.9 copy-start.6
  6.5 4.1 copy-start.1
  6.5 85.4 %all-gather.7.cloned.1.call-start = ((), (), s32[]{:S(2)}) async-start(), calls=%async_computation.1 | async-start | bytes 4718592 | tf_op jit(solution)/shard_map/all_gather | solution.py:16
  15.2 5.2 %copy-start.2 = (f32[1,2,2,256,256]{4,3,2,1,0:T(8,128)S(1)}, f32[1,2,2,256,256]{4,3,2,1,0:T(8,128)}, u32[]{:S(2)}) copy-start(f32[1,2,2,256,256]{4,3,2,1,0:T(8,128)} %param.12) | copy-start | bytes 3145732
  16.3 149.2 %all-gather.5.cloned.1.call-start = ((), (), s32[]{:S(2)}) async-start(), calls=%async_computation | async-start | bytes 4718592 | tf_op jit(solution)/shard_map/all_gather | solution.py:16
  20.3 3.8 copy-start.31
  20.3 3.8 copy-start.33
  20.3 218.6 %all-gather.9.cloned.1.call-start = ((), (), s32[]{:S(2)}) async-start(), calls=%async_computation.2 | async-start | bytes 4718592 | tf_op jit(solution)/shard_map/all_gather | solution.py:16
  22.2 69.7 %copy-start.21 = (f32[256,256]{1,0:T(8,128)}, f32[256,256]{1,0:T(8,128)S(1)}, u32[]{:S(2)}) copy-start(f32[256,256]{1,0:T(8,128)S(1)} %convolution_subtract_fusion.9) | copy-start | bytes 786436
  22.9 69.1 %copy-start.25 = (f32[256,256]{1,0:T(8,128)}, f32[256,256]{1,0:T(8,128)S(1)}, u32[]{:S(2)}) copy-start(f32[256,256]{1,0:T(8,128)S(1)} %convolution_add_fusion.9) | copy-start | bytes 786436
  23.8 288.5 %all-gather.11.cloned.1.call-start = ((), (), s32[]{:S(2)}) async-start(), calls=%async_computation.3 | async-start | bytes 4718592 | tf_op jit(solution)/shard_map/all_gather | solution.py:16
  165.5 3.8 copy-start.3
  167.9 4.3 copy-start.17
  169.3 3.4 copy-start.5
  170.6 3.4 copy-start.34
  170.6 4.0 copy-start.22
  171.4 3.2 copy-start.19
  172.3 140.1 %copy-start.26 = (f32[256,256]{0,1:T(8,128)}, f32[256,256]{0,1:T(8,128)S(1)}, u32[]{:S(2)}) copy-start(f32[256,256]{0,1:T(8,128)S(1)} %convolution_subtract_fusion.12) | copy-start | bytes 786436
  172.7 139.6 %copy-start.28 = (f32[256,256]{0,1:T(8,128)}, f32[256,256]{0,1:T(8,128)S(1)}, u32[]{:S(2)}) copy-start(f32[256,256]{0,1:T(8,128)S(1)} %convolution_add_fusion.12) | copy-start | bytes 786436
  173.9 232.6 %all-reduce.4.cloned.1.call-start = ((), (), s32[]{:S(2)}) async-start(), calls=%async_computation.4 | async-start | bytes 2097152 | tf_op jit(solution)/shard_map/psum | solution.py:121
  365.7 4.1 copy-start.8
  365.7 4.1 copy-start.10
  365.8 4.1 copy-start.12
  365.8 4.1 copy-start.14
  365.8 4.1 copy-start.16
  365.8 4.1 copy-start.18
  365.8 4.1 copy-start.20
  365.8 4.1 copy-start.24
  365.8 4.1 copy-start.27
  365.8 4.1 copy-start.29
  372.8 116.8 %all-reduce.6.cloned.1.call-start = ((), (), s32[]{:S(2)}) async-start(), calls=%async_computation.5 | async-start | bytes 1048576 | tf_op jit(solution)/shard_map/psum | solution.py:122
  497.0 3.8 copy-start
  (9 other events, 8.3 us)
Sparse Core Ops, SparseCore 0:
  16.4 75.5 all-gather.6
  94.1 71.3 all-gather.4
  167.6 71.3 all-gather.8
  240.9 71.3 all-gather.10
  372.9 33.5 all-reduce.3
  416.4 73.1 all-reduce.5
where the time goes:
time: 521 us; the launch traced here: 511 us
  waiting for transfers between devices  376 us (72%)
  matrix products  81.2 us (16%)
  local copies, waits for them, and re-layouts  16.2 us (3%)
  between operations  15.5 us (3%)
  other arithmetic  12.2 us (2%)
  starting transfers between devices  9.81 us (2%)
    all_gather x4, waiting for transfers between devices, prefix(): gathered = jax.tree.map(lambda a: lax.all_gather(a, axis), part)  278 us
    dot_general x94, matrix products, real_dot(): lax.dot_general(first, second, (dims, ((), ())), precision=HIGH, preferre...  81.2 us
    psum x1, waiting for transfers between devices, shards(): gram = lax.psum(gram_matrix(summed), 'rows')  73.2 us
    psum x1, waiting for transfers between devices, shards(): summed = lax.psum(weighted, 'pole')  24.3 us
  transfers between devices with their start and end apart: 6, of which 6 were waited for; matrix products, arithmetic and copies ran while one was open for 3% of the time, Pallas kernels for 0%

commit v1 on v0

v1 whole, which is shorter than its diff:
```python
import functools

import jax
import jax.numpy as jnp
from jax import lax
from jax.experimental import pallas as pl
from jax.experimental.pallas import tpu as pltpu
from jax.sharding import PartitionSpec as P

NS_ITERS = 2
LANES = 128
HIGH = lax.Precision.HIGH
F32 = jnp.float32


def dot(a, b, dims):
    return lax.dot_general(a, b, (dims, ((), ())), precision=HIGH, preferred_element_type=F32)


def times(left, right, dims):
    real = dot(left[0], right[0], dims) - dot(left[1], right[1], dims)
    imag = dot(left[0], right[1], dims) + dot(left[1], right[0], dims)
    return real, imag


def plain(left, right):
    return times(left, right, ((1,), (0,)))


def trans(left, right):
    return times(left, right, ((1,), (1,)))


def plus(a, b):
    return a[0] + b[0], a[1] + b[1]


def minus(a, b):
    return a[0] - b[0], a[1] - b[1]


def negative(a):
    return -a[0], -a[1]


def pick(choice, a, b):
    return jnp.where(choice, a[0], b[0]), jnp.where(choice, a[1], b[1])


def pair(ref, *index):
    return ref[(*index, 0)], ref[(*index, 1)]


def put(ref, value):
    ref[0] = value[0]
    ref[1] = value[1]


def rows_of(ref, start, size):
    start = pl.multiple_of(start, size)
    return ref[0, pl.ds(start, size), :], ref[1, pl.ds(start, size), :]


def call(body, outs, *args, products=1):
    shapes = [jax.ShapeDtypeStruct(shape, F32) for shape in outs]
    return pl.pallas_call(
        body,
        out_shape=shapes,
        in_specs=[pl.BlockSpec(memory_space=pltpu.VMEM)] * len(args),
        out_specs=[pl.BlockSpec(memory_space=pltpu.VMEM)] * len(outs),
        cost_estimate=pl.CostEstimate(
            flops=products * 3 * 8 * 256**3, bytes_accessed=1 << 20, transcendentals=0
        ),
    )(*args)


def side():
    return lax.rem(lax.axis_index("rows"), 2) == 0


def map_kernel(lower, out):
    count = lower.shape[0]
    value = pair(lower, 0)
    for number in range(1, count):
        value = plain(pair(lower, number), value)
    if count % 2:
        value = negative(value)
    put(out, value)


def back_map_kernel(lower, upper, ahead, out_c, out_r):
    count = upper.shape[0]
    value = pair(upper, count - 1)
    for number in range(count - 2, -1, -1):
        value = plain(pair(upper, number), value)
    if count % 2:
        value = negative(value)
    put(out_c, value)
    levels = [negative(pair(lower, 0))]
    for number in range(1, count - 1):
        levels.append(negative(plain(pair(lower, number), levels[-1])))
    if count > 1:
        levels.append(pair(ahead))
    value = levels[-1]
    for number in range(count - 2, -1, -1):
        value = minus(levels[number], plain(pair(upper, number), value))
    put(out_r, value)


def local_kernel(piece, pivot, lower, upper, states, bkeep, bsend, gkeep, gsend, work):
    count, width = pivot.shape[0], pivot.shape[-1]
    half = bkeep.shape[1]
    mine = jnp.where(side(), 0, half)
    other = half - mine
    last = None
    for number in range(count):
        columns = slice(number * width, (number + 1) * width)
        value = trans((piece[0, :, columns], piece[1, :, columns]), pair(pivot, number))
        if last is not None:
            value = minus(value, trans(last, pair(lower, number)))
        states[number, 0] = value[0]
        states[number, 1] = value[1]
        last = value
    put(bkeep, rows_of(states.at[count - 1], mine, half))
    put(bsend, rows_of(states.at[count - 1], other, half))
    for number in range(count - 2, -1, -1):
        last = minus(pair(states, number), trans(last, pair(upper, number)))
    put(work, last)
    put(gkeep, rows_of(work, mine, half))
    put(gsend, rows_of(work, other, half))


def join_kernel(mine, theirs, bmine, btheirs, out_b, out_a):
    first = side()
    a_first = pick(first, pair(mine), pair(theirs))
    a_second = pick(first, pair(theirs), pair(mine))
    b_first = pick(first, pair(bmine), pair(btheirs))
    b_second = pick(first, pair(btheirs), pair(bmine))
    put(out_b, plus(trans(b_first, a_second), b_second))
    put(out_a, plain(a_second, a_first))


def join_back_kernel(mine, theirs, out):
    first = side()
    c_first = pick(first, pair(mine), pair(theirs))
    c_second = pick(first, pair(theirs), pair(mine))
    put(out, plain(c_first, c_second))


def apply_kernel(state, matrix, base, out):
    put(out, plus(trans(pair(state), pair(matrix)), pair(base)))


def apply_two_kernel(state, matrix, base, more, out):
    value = plus(trans(pair(state), pair(matrix)), pair(base))
    put(out, plus(value, pair(more)))


def turn_kernel(inflow, a_mine, a_theirs, b_mine, b_theirs, r_mine, r_theirs, g_mine, g_theirs,
                c_mine, c_theirs, in_own, in_other, mid, out):
    first = side()
    entering = pair(inflow)
    a_first = pick(first, pair(a_mine), pair(a_theirs))
    b_first = pick(first, pair(b_mine), pair(b_theirs))
    second = plus(trans(entering, a_first), b_first)
    put(in_own, pick(first, entering, second))
    put(in_other, pick(first, second, entering))
    r_second = pick(first, pair(r_theirs), pair(r_mine))
    g_second = pick(first, pair(g_theirs), pair(g_mine))
    middle = plus(g_second, trans(second, r_second))
    put(mid, middle)
    r_first = pick(first, pair(r_mine), pair(r_theirs))
    g_first = pick(first, pair(g_mine), pair(g_theirs))
    c_first = pick(first, pair(c_mine), pair(c_theirs))
    value = plus(g_first, trans(entering, r_first))
    put(out, plus(value, trans(middle, c_first)))


def back_in_kernel(back_inflow, mid, c_mine, c_theirs, own, other):
    first = side()
    c_second = pick(first, pair(c_theirs), pair(c_mine))
    entering = pair(back_inflow)
    first_in = plus(pair(mid), trans(entering, c_second))
    put(own, pick(first, first_in, entering))
    put(other, pick(first, entering, first_in))


def swept_kernel(states, in_own, in_theirs, lower, out, full):
    count = states.shape[0]
    half = in_own.shape[1]
    mine = pl.multiple_of(jnp.where(side(), 0, half), half)
    other = pl.multiple_of(half - mine, half)
    for part in range(2):
        full[part, pl.ds(mine, half), :] = in_own[part]
        full[part, pl.ds(other, half), :] = in_theirs[part]
    carry = pair(full)
    for number in range(count):
        carry = negative(trans(carry, pair(lower, number)))
        out[number, 0] = states[number, 0] + carry[0]
        out[number, 1] = states[number, 1] + carry[1]


def solved_kernel(swept, x_own, x_theirs, upper, weights, keep, send, full):
    count, width = swept.shape[0], swept.shape[-1]
    half = x_own.shape[1]
    mine = pl.multiple_of(jnp.where(side(), 0, half), half)
    other = pl.multiple_of(half - mine, half)
    for part in range(2):
        full[part, pl.ds(mine, half), :] = x_own[part]
        full[part, pl.ds(other, half), :] = x_theirs[part]
    wreal, wimag = weights[0, 0], weights[0, 1]
    carry = pair(full)
    upward = lax.rem(lax.axis_index("pole"), 2) == 1
    for number in range(count - 1, -1, -1):
        carry = minus(pair(swept, number), trans(carry, pair(upper, number)))
        value = (wreal * carry[0] - wimag * carry[1], wreal * carry[1] + wimag * carry[0])
        kept = upward if number >= count // 2 else jnp.logical_not(upward)
        columns = slice((number % (count // 2)) * width, (number % (count // 2) + 1) * width)

        @pl.when(kept)
        def _():
            for part in range(2):
                keep[part, :, columns] = value[part]

        @pl.when(jnp.logical_not(kept))
        def _():
            for part in range(2):
                send[part, :, columns] = value[part]


def halve_kernel(bit, mine, theirs, keep, send):
    width = keep.shape[2]
    up = lax.rem(lax.div(lax.axis_index("pole"), 2**bit), 2) == 1
    for part in range(2):
        low = mine[part, :, :width] + theirs[part, :, :width]
        high = mine[part, :, width:] + theirs[part, :, width:]
        keep[part] = jnp.where(up, high, low)
        send[part] = jnp.where(up, low, high)


def gram_kernel(mine, theirs, total, keep, send, work):
    size = total.shape[1]
    basis = (mine[0] + theirs[0], mine[1] + theirs[1])
    put(total, basis)
    dims = ((1,), (1,))
    real = dot(basis[0], basis[0], dims) + dot(basis[1], basis[1], dims)
    imag = dot(basis[0], basis[1], dims) - dot(basis[1], basis[0], dims)
    row = lax.broadcasted_iota(jnp.int32, (size, size), 0)
    column = lax.broadcasted_iota(jnp.int32, (size, size), 1)
    work[...] = jnp.where(row <= column, real, imag)
    half = size // 2
    start = pl.multiple_of(lax.rem(lax.axis_index("pole"), 2) * half, half)
    keep[...] = work[pl.ds(start, half), :]
    send[...] = work[pl.ds(pl.multiple_of(half - start, half), half), :]


def finish_kernel(states, bits, mine, theirs, *refs):
    pieces, out, held, slab = refs[:-3], refs[-3], refs[-2], refs[-1]
    size = held.shape[0]
    half = size // 2
    pole = lax.axis_index("pole")
    start = pl.multiple_of(lax.rem(pole, 2) * half, half)
    held[pl.ds(start, half), :] = mine[...]
    held[pl.ds(pl.multiple_of(half - start, half), half), :] = theirs[...]
    packed = held[...]
    turned = packed.T
    row = lax.broadcasted_iota(jnp.int32, (size, size), 0)
    column = lax.broadcasted_iota(jnp.int32, (size, size), 1)
    real = jnp.where(row <= column, packed, turned)
    imag = jnp.where(row < column, turned, jnp.where(row > column, -packed, 0.0))
    frob = jnp.sqrt(jnp.sum(real * real + imag * imag, keepdims=True))
    current = (real / frob, imag / frob)
    eye = jnp.where(row == column, 1.0, 0.0)
    columns = out.shape[1]
    inverse = None
    for sweep in range(NS_ITERS):
        both = current if inverse is None else plain(inverse, current)
        factor = (1.5 * eye - 0.5 * both[0], -0.5 * both[1])
        if sweep < NS_ITERS - 1:
            current = plain(current, factor)
            inverse = factor if inverse is None else plain(factor, inverse)
        else:
            put(slab, factor)
            place = pl.multiple_of(pole * columns, columns)
            mixing = (slab[0, pl.ds(place, columns), :], slab[1, pl.ds(place, columns), :])
            if inverse is not None:
                mixing = plain(mixing, inverse)
    factor = jnp.sqrt(states / frob)
    mixing = (mixing[0] * factor, mixing[1] * factor)
    width = pieces[0].shape[2]
    for mask, piece in enumerate(pieces):
        offset = 0
        for bit in range(bits):
            on = lax.rem(lax.div(pole, 2**bit), 2)
            if mask >> bit & 1:
                on = 1 - on
            offset = offset + on * (width << (bits - 1 - bit))
        offset = pl.multiple_of(offset, width)
        value = plain(mixing, pair(piece))
        for part in range(2):
            out[part, :, pl.ds(offset, width)] = value[part]


def shards(subspace, pivots, lower_blocks, upper_blocks, pole_weights):
    devices = lax.axis_size("rows")
    poles = lax.axis_size("pole")
    count, width = pivots.shape[1], pivots.shape[-1]
    vectors = subspace.shape[1]
    half = vectors // 2
    nodes = devices // 2
    pivot, lower, upper = pivots[0], lower_blocks[0], upper_blocks[0]
    square = (2, width, width)
    state = (2, vectors, width)
    strip = (2, half, width)
    vmem = pltpu.VMEM

    def scratch(body, outs, extra, *args, products=1):
        return pl.pallas_call(
            body,
            out_shape=[jax.ShapeDtypeStruct(shape, F32) for shape in outs],
            in_specs=[pl.BlockSpec(memory_space=vmem)] * len(args),
            out_specs=[pl.BlockSpec(memory_space=vmem)] * len(outs),
            scratch_shapes=[vmem(shape, F32) for shape in extra],
            cost_estimate=pl.CostEstimate(
                flops=products * 3 * 8 * 256**3, bytes_accessed=1 << 20, transcendentals=0
            ),
        )(*args)

    swap = [(place, place ^ 1) for place in range(devices)]

    def beside(value):
        return lax.ppermute(value, "rows", swap)

    def between(value, moves):
        return lax.ppermute(
            value, "rows", [(2 * a + s, 2 * b + s) for a, b in moves for s in range(2)]
        )

    def prefix(base, matrix, order):
        if nodes == 4:
            near = between(base, [(order[0], order[1]), (order[2], order[3])])
            ahead = between(matrix, [(order[2], order[3])])
            (passed,) = call(apply_kernel, [strip], near, matrix, base)
            third = between(passed, [(order[1], order[2])])
            fourth = between(passed, [(order[1], order[3])])
            (inflow,) = call(apply_two_kernel, [strip], fourth, ahead, near, third)
            return inflow
        inflow = jnp.zeros(strip, F32)
        for hop in range(nodes - 1):
            (passed,) = call(apply_kernel, [strip], inflow, matrix, base)
            inflow = inflow + between(passed, [(order[hop], order[hop + 1])])
        return inflow

    (a_mine,) = call(map_kernel, [square], lower)
    a_theirs = beside(a_mine)
    states, b_mine, b_send, g_mine, g_send = scratch(
        local_kernel, [(count,) + state, strip, strip, strip, strip], [state],
        subspace, pivot, lower, upper, products=2 * count,
    )
    b_theirs = beside(b_send)
    c_mine, r_mine = call(back_map_kernel, [square, square], lower, upper, a_mine, products=2)
    r_theirs = beside(r_mine)
    g_theirs = beside(g_send)
    c_theirs = beside(c_mine)

    b_node, a_node = call(join_kernel, [strip, square], a_mine, a_theirs, b_mine, b_theirs)
    order = list(range(nodes))
    inflow = prefix(b_node, a_node, order)
    in_own, in_other, mid, g_node = call(
        turn_kernel, [strip] * 4, inflow, a_mine, a_theirs, b_mine, b_theirs,
        r_mine, r_theirs, g_mine, g_theirs, c_mine, c_theirs, products=2,
    )
    (c_node,) = call(join_back_kernel, [square], c_mine, c_theirs)
    back_inflow = prefix(g_node, c_node, order[::-1])
    in_theirs = beside(in_other)
    (swept,) = scratch(
        swept_kernel, [(count,) + state], [state], states, in_own, in_theirs, lower,
        products=count,
    )
    x_own, x_other = call(
        back_in_kernel, [strip] * 2, back_inflow, mid, c_mine, c_theirs
    )
    x_theirs = beside(x_other)

    def over_poles(value, bit):
        return lax.ppermute(value, "pole", [(place, place ^ (1 << bit)) for place in range(poles)])

    columns = count * width
    levels = poles.bit_length() - 1
    bits = levels
    while columns >> bits < LANES:
        bits -= 1
    piece = columns >> 1
    keep, send = pl.pallas_call(
        solved_kernel,
        out_shape=[jax.ShapeDtypeStruct((2, vectors, piece), F32)] * 2,
        in_specs=[pl.BlockSpec(memory_space=vmem)] * 4
        + [pl.BlockSpec(memory_space=pltpu.SMEM)],
        out_specs=[pl.BlockSpec(memory_space=vmem)] * 2,
        scratch_shapes=[vmem(state, F32)],
    )(swept, x_own, x_theirs, upper, pole_weights)
    theirs = over_poles(send, 0)
    for bit in range(1, bits):
        piece >>= 1
        keep, send = call(
            functools.partial(halve_kernel, bit), [(2, vectors, piece)] * 2, keep, theirs
        )
        theirs = over_poles(send, bit)
    for bit in range(bits, levels):
        keep = keep + theirs
        theirs = over_poles(keep, bit)
    total, packed, packed_send = scratch(
        gram_kernel, [(2, vectors, piece), (half, vectors), (half, vectors)],
        [(vectors, vectors)], keep, theirs,
    )
    packed = packed + over_poles(packed_send, 0)
    for bit in range(1, bits):
        packed = packed + over_poles(packed, bit)
    for bit in range(devices.bit_length() - 1):
        packed = packed + lax.ppermute(
            packed, "rows", [(place, place ^ (1 << bit)) for place in range(devices)]
        )
    packed_theirs = over_poles(packed, 0)
    pieces = [total]
    for bit in range(bits):
        pieces = pieces + [over_poles(value, bit) for value in pieces]
    ordered = [None] * len(pieces)
    for index, value in enumerate(pieces):
        ordered[index] = value
    states_in_all = float(columns * devices)
    (result,) = scratch(
        functools.partial(finish_kernel, states_in_all, bits),
        [(2, vectors // poles, columns)], [(vectors, vectors), state],
        packed, packed_theirs, *ordered, products=4,
    )
    return result


def solution(mesh):
    placed = (
        P(None, None, "rows"),
        P("pole", "rows", None, None, None),
        P("pole", "rows", None, None, None),
        P("pole", "rows", None, None, None),
        P("pole", None),
    )
    return jax.shard_map(
        shards, mesh=mesh, in_specs=placed, out_specs=P(None, "pole", "rows"), check_vma=False
    )
```

time: 521 us -> 172 us (0.33); the launches traced: 511 us -> 171 us
  waiting for transfers between devices: 376 us -> 76.7 us
  matrix products: 81.2 us -> 0 us
  Pallas kernels: 0 us -> 52.4 us
  starting transfers between devices: 9.81 us -> 30.1 us
  between operations: 15.5 us -> 0.25 us
  other arithmetic: 12.2 us -> 0.99 us
  local copies, waits for them, and re-layouts: 16.2 us -> 10.7 us
    all_gather x4 -> x0, waiting for transfers between devices: 278 us -> none  [prefix(): gathered = jax.tree.map(lambda a: lax.all_gather(a, axis), part)]
    psum x2 -> x0, waiting for transfers between devices: 97.5 us -> none  [the longest x1 73.2 us: shards(): gram = lax.psum(gram_matrix(summed), 'rows')]
    dot_general x94 -> x0, matrix products: 81.2 us -> none  [real_dot(): lax.dot_general(first, second, (dims, ((), ())), precision=HIGH, preferre...]
    ppermute x0 -> x26, waiting for transfers between devices: none -> 76.7 us  [the longest x7 33.6 us: beside(): return lax.ppermute(value, 'rows', swap)]
    pallas_call x0 -> x16, Pallas kernels: none -> 52.4 us  [the longest x11 32.3 us: call(): pl.pallas_call(body, out_shape=shapes, in_specs=[pl.BlockSpec(memory_spac...]
    ppermute x0 -> x26, starting transfers between devices: none -> 30.1 us  [the longest x8 10.5 us: between(): lax.ppermute(value, 'rows', [(2 * a + s, 2 * b + s) for a, b in moves for...]
    psum x2 -> x0, starting transfers between devices: 9.43 us -> none  [the longest x1 9.39 us: shards(): gram = lax.psum(gram_matrix(summed), 'rows')]
    unnamed x70 -> x52, local copies, waits for them, and re-layouts: 1.6 us -> 10.7 us
  transfers between devices with their start and end apart: 6 -> 26, of which waited for: 6 -> 14; matrix products, arithmetic and copies ran while one was open for 3% -> 0% of each run, Pallas kernels for 0% -> 16%
where the time goes in v1:
time: 172 us; the launch traced here: 171 us
  waiting for transfers between devices  76.7 us (45%)
  Pallas kernels  52.4 us (30%)
  starting transfers between devices  30.1 us (18%)
  local copies, waits for them, and re-layouts  10.7 us (6%)
    ppermute x7, waiting for transfers between devices, beside(): return lax.ppermute(value, 'rows', swap)  33.6 us
    pallas_call x11, Pallas kernels, call(): pl.pallas_call(body, out_shape=shapes, in_specs=[pl.BlockSpec(memory_spac...  32.3 us
    ppermute x8, waiting for transfers between devices, over_poles(): lax.ppermute(value, 'pole', [(place, place ^ 1 << bit) for place in range...  16.8 us
    ppermute x8, waiting for transfers between devices, between(): lax.ppermute(value, 'rows', [(2 * a + s, 2 * b + s) for a, b in moves for...  16.8 us
    pallas_call x4, Pallas kernels, scratch(): pl.pallas_call(body, out_shape=[jax.ShapeDtypeStruct(shape, F32) for shap...  15.9 us
    unnamed x52, local copies, waits for them, and re-layouts  10.7 us
    ppermute x8, starting transfers between devices, between(): lax.ppermute(value, 'rows', [(2 * a + s, 2 * b + s) for a, b in moves for...  10.5 us
    ppermute x7, starting transfers between devices, beside(): return lax.ppermute(value, 'rows', swap)  9.82 us
  transfers between devices with their start and end apart: 26, of which 14 were waited for; matrix products, arithmetic and copies ran while one was open for 0% of the time, Pallas kernels for 16%

profile of v1, /device:TPU:0, one launch (start us, length us, event | category | flops | bytes accessed | tf_op | source)
XLA Modules:
  0.0 171.3 jit_solution(11222797346834347179)
XLA Ops:
  0.0 2.6 %shard_map.56.mine.ahead.a_mine = f32[2,256,256]{2,1,0:T(8,128)} custom-call(f32[2,2,256,256]{3,2,1,0:T(8,128)} %bitcast.3), custom_call_target="tpu_custom_call" | custom-call | flops 402653184 | bytes 1048576 | tf_op jit(solution)/shard_map/pallas_call | solution.py:66
  2.6 3.0 %collective-permute-start = (f32[2,256,256]{2,1,0:T(8,128)}, f32[2,256,256]{2,1,0:T(8,128)S(1)}, u32[]{:S(2)}, u32[]{:S(2)}) collective-permute-start(f32[2,256,256]{2,1,0:T(8,128)} %shard_map.56.mine.ahead.a_mine), channel_id=1, source_target_pairs={{0,1},{1,0},{2,3},{3,2},{4,5},{5,4},{6,7},{7,6},{8,9},{9,8},{10,11... | collective-permute-start | bytes 1572872 | tf_op jit(solution)/shard_map/ppermute | solution.py:332
  5.6 5.1 %shard_map.55 = (f32[2,2,256,256]{3,2,1,0:T(8,128)}, f32[2,128,256]{2,1,0:T(8,128)}, f32[2,128,256]{2,1,0:T(8,128)}, f32[2,128,256]{2,1,0:T(8,128)}, f32[2,128,256]{2,1,0:T(8,128)}) custom-call(f32[2,256,512]{2,1,0:T(8,128)} %piece.1, f32[2,2,256,256]{3,2,1,0:T(8,128)} %bitcast.10, f32[2,2,256,256]{3,2,1,0:T(8,128)} %bitcast.4, f32[2,2,256,256]{3,2,1,0:T(8,128)} %bitcast.7), custom_call_target="tpu_custom_call" | custom-call | flops 1610612736 | bytes 1048576 | tf_op jit(solution)/shard_map/pallas_call | solution.py:318
  10.7 12.7 %collective-permute-done.1.btheirs.b_theirs = f32[2,128,256]{2,1,0:T(8,128)S(1)} collective-permute-done((f32[2,128,256]{2,1,0:T(8,128)}, f32[2,128,256]{2,1,0:T(8,128)S(1)}, u32[]{:S(2)}, u32[]{:S(2)}) %collective-permute-start.1) | collective-permute-done | bytes 262176 | tf_op jit(solution)/shard_map/ppermute | solution.py:332
  24.3 3.2 %shard_map.57 = (f32[2,128,256]{2,1,0:T(8,128)}, f32[2,256,256]{2,1,0:T(8,128)}) custom-call(f32[2,256,256]{2,1,0:T(8,128)} %shard_map.56.mine.ahead.a_mine, f32[2,256,256]{2,1,0:T(8,128)} %copy-done.2, f32[2,128,256]{2,1,0:T(8,128)} %get-tuple-element.28.bmine.b_mine, f32[2,128,256]{2,1,0:T(8,128)} %copy-done.3), custom_call_target="tpu_custom_call" | custom-call | flops 402653184 | bytes 1048576 | tf_op jit(solution)/shard_map/pallas_call | solution.py:66
  27.5 3.7 %collective-permute-start.2 = (f32[2,128,256]{2,1,0:T(8,128)}, f32[2,128,256]{2,1,0:T(8,128)S(1)}, u32[]{:S(2)}, u32[]{:S(2)}) collective-permute-start(f32[2,128,256]{2,1,0:T(8,128)} %get-tuple-element.30.base), channel_id=1, source_target_pairs={{0,2},{1,3},{4,6},{5,7},{8,10},{9,11},{12,14},{13,15},{16,18},{17,... | collective-permute-start | bytes 786440 | tf_op jit(solution)/shard_map/ppermute | solution.py:335
  31.2 3.5 %shard_map.60 = (f32[2,256,256]{2,1,0:T(8,128)}, f32[2,256,256]{2,1,0:T(8,128)}) custom-call(f32[2,2,256,256]{3,2,1,0:T(8,128)} %bitcast.5, f32[2,2,256,256]{3,2,1,0:T(8,128)} %bitcast.8, f32[2,256,256]{2,1,0:T(8,128)} %shard_map.56.mine.ahead.a_mine), custom_call_target="tpu_custom_call" | custom-call | flops 805306368 | bytes 1048576 | tf_op jit(solution)/shard_map/pallas_call | solution.py:66
  36.9 2.5 %shard_map.58 = f32[2,128,256]{2,1,0:T(8,128)} custom-call(f32[2,128,256]{2,1,0:T(8,128)} %copy-done.10, f32[2,256,256]{2,1,0:T(8,128)} %get-tuple-element.31.matrix, f32[2,128,256]{2,1,0:T(8,128)} %get-tuple-element.30.base), custom_call_target="tpu_custom_call" | custom-call | flops 402653184 | bytes 1048576 | tf_op jit(solution)/shard_map/pallas_call | solution.py:66
  46.0 2.6 %shard_map.59.inflow = f32[2,128,256]{2,1,0:T(8,128)} custom-call(f32[2,128,256]{2,1,0:T(8,128)} %copy-done.12, f32[2,256,256]{2,1,0:T(8,128)} %copy-done.6, f32[2,128,256]{2,1,0:T(8,128)} %copy-done.10, f32[2,128,256]{2,1,0:T(8,128)} %copy-done.14), custom_call_target="tpu_custom_call" | custom-call | flops 402653184 | bytes 1048576 | tf_op jit(solution)/shard_map/pallas_call | solution.py:66
  48.6 20.4 %collective-permute-done.7.g_theirs = f32[2,128,256]{2,1,0:T(8,128)S(1)} collective-permute-done((f32[2,128,256]{2,1,0:T(8,128)}, f32[2,128,256]{2,1,0:T(8,128)S(1)}, u32[]{:S(2)}, u32[]{:S(2)}) %collective-permute-start.7) | collective-permute-done | bytes 262176 | tf_op jit(solution)/shard_map/ppermute | solution.py:332
  70.1 5.2 %shard_map.61 = (f32[2,128,256]{2,1,0:T(8,128)}, f32[2,128,256]{2,1,0:T(8,128)}, f32[2,128,256]{2,1,0:T(8,128)}, f32[2,128,256]{2,1,0:T(8,128)}) custom-call(f32[2,128,256]{2,1,0:T(8,128)} %shard_map.59.inflow, f32[2,256,256]{2,1,0:T(8,128)} %shard_map.56.mine.ahead.a_mine, f32[2,256,256]{2,1,0:T(8,128)} %copy-done.2, ...), custom_call_target="tpu_custom_call" | custom-call | flops 805306368 | bytes 1048576 | tf_op jit(solution)/shard_map/pallas_call | solution.py:66
  76.6 2.6 %shard_map.63.matrix = f32[2,256,256]{2,1,0:T(8,128)} custom-call(f32[2,256,256]{2,1,0:T(8,128)} %get-tuple-element.35.c_mine.mine, f32[2,256,256]{2,1,0:T(8,128)} %copy-done.1), custom_call_target="tpu_custom_call" | custom-call | flops 402653184 | bytes 1048576 | tf_op jit(solution)/shard_map/pallas_call | solution.py:66
  80.6 9.2 %collective-permute-done.10.state.base = f32[2,128,256]{2,1,0:T(8,128)S(1)} collective-permute-done((f32[2,128,256]{2,1,0:T(8,128)}, f32[2,128,256]{2,1,0:T(8,128)S(1)}, u32[]{:S(2)}, u32[]{:S(2)}) %collective-permute-start.10) | collective-permute-done | bytes 262176 | tf_op jit(solution)/shard_map/ppermute | solution.py:335
  90.5 2.5 %shard_map.64 = f32[2,128,256]{2,1,0:T(8,128)} custom-call(f32[2,128,256]{2,1,0:T(8,128)} %copy-done.11, f32[2,256,256]{2,1,0:T(8,128)} %shard_map.63.matrix, f32[2,128,256]{2,1,0:T(8,128)} %get-tuple-element.38.base), custom_call_target="tpu_custom_call" | custom-call | flops 402653184 | bytes 1048576 | tf_op jit(solution)/shard_map/pallas_call | solution.py:66
  95.1 1.6 collective-permute-start.9
  96.7 6.8 %collective-permute-done.12.matrix = f32[2,256,256]{2,1,0:T(8,128)S(1)} collective-permute-done((f32[2,256,256]{2,1,0:T(8,128)}, f32[2,256,256]{2,1,0:T(8,128)S(1)}, u32[]{:S(2)}, u32[]{:S(2)}) %collective-permute-start.12) | collective-permute-done | bytes 524320 | tf_op jit(solution)/shard_map/ppermute | solution.py:335
  105.1 2.6 %shard_map.65.back_inflow = f32[2,128,256]{2,1,0:T(8,128)} custom-call(f32[2,128,256]{2,1,0:T(8,128)} %copy-done.13, f32[2,256,256]{2,1,0:T(8,128)} %copy-done.7, f32[2,128,256]{2,1,0:T(8,128)} %copy-done.11, f32[2,128,256]{2,1,0:T(8,128)} %copy-done.15), custom_call_target="tpu_custom_call" | custom-call | flops 402653184 | bytes 1048576 | tf_op jit(solution)/shard_map/pallas_call | solution.py:66
  107.7 2.8 %shard_map.66 = (f32[2,128,256]{2,1,0:T(8,128)}, f32[2,128,256]{2,1,0:T(8,128)}) custom-call(f32[2,128,256]{2,1,0:T(8,128)} %shard_map.65.back_inflow, f32[2,128,256]{2,1,0:T(8,128)} %get-tuple-element.39.mid, f32[2,256,256]{2,1,0:T(8,128)} %get-tuple-element.35.c_mine.mine, f32[2,256,256]{2,1,0:T(8,128)} %copy-done.1), custom_call_target="tpu_custom_call" | custom-call | flops 402653184 | bytes 1048576 | tf_op jit(solution)/shard_map/pallas_call | solution.py:66
  112.8 3.8 %shard_map.62.swept = f32[2,2,256,256]{3,2,1,0:T(8,128)} custom-call(f32[2,2,256,256]{3,2,1,0:T(8,128)} %get-tuple-element.27.states, f32[2,128,256]{2,1,0:T(8,128)} %get-tuple-element.36.in_own, f32[2,128,256]{2,1,0:T(8,128)} %copy-done.8, f32[2,2,256,256]{3,2,1,0:T(8,128)} %bitcast.6), custom_call_target="tpu_custom_call" | custom-call | flops 805306368 | bytes 1048576 | tf_op jit(solution)/shard_map/pallas_call | solution.py:318
  117.8 4.3 %shard_map.67 = (f32[2,256,256]{2,1,0:T(8,128)}, f32[2,256,256]{2,1,0:T(8,128)}) custom-call(f32[2,2,256,256]{3,2,1,0:T(8,128)} %shard_map.62.swept, f32[2,128,256]{2,1,0:T(8,128)} %get-tuple-element.40.x_own, f32[2,128,256]{2,1,0:T(8,128)} %copy-done.16, f32[2,2,256,256]{3,2,1,0:T(8,128)} %bitcast.9, f32[1,2]{1,0:T(1,128)} %weights.1), custom_call_target="tpu_custom_call" | custom-call | tf_op jit(solution)/shard_map/pallas_call | solution.py:394
  122.1 2.1 %collective-permute-done.15.theirs = f32[2,256,256]{2,1,0:T(8,128)S(1)} collective-permute-done((f32[2,256,256]{2,1,0:T(8,128)}, f32[2,256,256]{2,1,0:T(8,128)S(1)}, u32[]{:S(2)}, u32[]{:S(2)}) %collective-permute-start.15) | collective-permute-done | bytes 524320 | tf_op jit(solution)/shard_map/ppermute | solution.py:386
  125.0 2.1 %shard_map.68 = (f32[2,256,128]{2,1,0:T(8,128)}, f32[2,256,128]{2,1,0:T(8,128)}) custom-call(f32[2,256,256]{2,1,0:T(8,128)} %get-tuple-element.42.mine, f32[2,256,256]{2,1,0:T(8,128)} %copy-done.18), custom_call_target="tpu_custom_call" | custom-call | flops 402653184 | bytes 1048576 | tf_op jit(solution)/shard_map/pallas_call | solution.py:66
  128.6 7.0 %collective-permute-done.16.theirs = f32[2,256,128]{2,1,0:T(8,128)S(1)} collective-permute-done((f32[2,256,128]{2,1,0:T(8,128)}, f32[2,256,128]{2,1,0:T(8,128)S(1)}, u32[]{:S(2)}, u32[]{:S(2)}) %collective-permute-start.16) | collective-permute-done | bytes 262176 | tf_op jit(solution)/shard_map/ppermute | solution.py:386
  136.4 2.4 %shard_map.69 = (f32[2,256,128]{2,1,0:T(8,128)}, f32[128,256]{1,0:T(8,128)}, f32[128,256]{1,0:T(8,128)}) custom-call(f32[2,256,128]{2,1,0:T(8,128)} %get-tuple-element.44.mine, f32[2,256,128]{2,1,0:T(8,128)} %copy-done.24), custom_call_target="tpu_custom_call" | custom-call | flops 402653184 | bytes 1048576 | tf_op jit(solution)/shard_map/pallas_call | solution.py:318
  141.2 1.6 collective-permute-start.18
  142.8 4.0 %collective-permute-done.18 = f32[128,256]{1,0:T(8,128)S(1)} collective-permute-done((f32[128,256]{1,0:T(8,128)S(1)}, f32[128,256]{1,0:T(8,128)S(1)}, u32[]{:S(2)}, u32[]{:S(2)}) %collective-permute-start.18) | collective-permute-done | bytes 131104 | tf_op jit(solution)/shard_map/ppermute | solution.py:386
  146.8 1.6 collective-permute-start.19
  148.5 3.4 %collective-permute-done.19 = f32[128,256]{1,0:T(8,128)S(1)} collective-permute-done((f32[128,256]{1,0:T(8,128)S(1)}, f32[128,256]{1,0:T(8,128)S(1)}, u32[]{:S(2)}, u32[]{:S(2)}) %collective-permute-start.19) | collective-permute-done | bytes 131104 | tf_op jit(solution)/shard_map/ppermute | solution.py:420
  155.0 2.2 %collective-permute-done.20 = f32[128,256]{1,0:T(8,128)S(1)} collective-permute-done((f32[128,256]{1,0:T(8,128)S(1)}, f32[128,256]{1,0:T(8,128)S(1)}, u32[]{:S(2)}, u32[]{:S(2)}) %collective-permute-start.20) | collective-permute-done | bytes 131104 | tf_op jit(solution)/shard_map/ppermute | solution.py:420
  159.1 4.0 %collective-permute-done.21 = f32[128,256]{1,0:T(8,128)S(1)} collective-permute-done((f32[128,256]{1,0:T(8,128)S(1)}, f32[128,256]{1,0:T(8,128)S(1)}, u32[]{:S(2)}, u32[]{:S(2)}) %collective-permute-start.21) | collective-permute-done | bytes 131104 | tf_op jit(solution)/shard_map/ppermute | solution.py:420
  163.3 2.1 %collective-permute-done.25.refs_3_ = f32[2,256,128]{2,1,0:T(8,128)S(1)} collective-permute-done((f32[2,256,128]{2,1,0:T(8,128)S(1)}, f32[2,256,128]{2,1,0:T(8,128)S(1)}, u32[]{:S(2)}, u32[]{:S(2)}) %collective-permute-start.25) | collective-permute-done | bytes 262176 | tf_op jit(solution)/shard_map/ppermute | solution.py:386
  166.7 4.6 %shard_map.70 = f32[2,64,512]{2,1,0:T(8,128)} custom-call(f32[128,256]{1,0:T(8,128)} %copy-done.17, f32[128,256]{1,0:T(8,128)} %copy-done.25, f32[2,256,128]{2,1,0:T(8,128)} %get-tuple-element.48.refs_0_, f32[2,256,128]{2,1,0:T(8,128)} %copy-done.21, f32[2,256,128]{2,1,0:T(8,128)} %copy-done.22, f32[2,256,128]{2,1,0:T(8,128)} %copy-done.23), custom_call_target="tpu_custom_call" | custom-call | flops 1610612736 | bytes 1048576 | tf_op jit(solution)/shard_map/pallas_call | solution.py:318
  (93 shorter events, 33.1 us)
Async XLA Ops:
  2.6 20.7 %collective-permute-start = (f32[2,256,256]{2,1,0:T(8,128)}, f32[2,256,256]{2,1,0:T(8,128)S(1)}, u32[]{:S(2)}, u32[]{:S(2)}) collective-permute-start(f32[2,256,256]{2,1,0:T(8,128)} %shard_map.56.mine.ahead.a_mine), channel_id=1, source_target_pairs={{0,1},{1,0},{2,3},{3,2},{4,5},{5,4},{6,7},{7,6},{8,9},{9,8},{10,11... | collective-permute-start | bytes 1572872 | tf_op jit(solution)/shard_map/ppermute | solution.py:332
  10.7 12.7 %collective-permute-start.1 = (f32[2,128,256]{2,1,0:T(8,128)}, f32[2,128,256]{2,1,0:T(8,128)S(1)}, u32[]{:S(2)}, u32[]{:S(2)}) collective-permute-start(f32[2,128,256]{2,1,0:T(8,128)} %get-tuple-element.29), channel_id=1, source_target_pairs={{0,1},{1,0},{2,3},{3,2},{4,5},{5,4},{6,7},{7,6},{8,9},{9,8},{10,11... | collective-permute-start | bytes 786440 | tf_op jit(solution)/shard_map/ppermute | solution.py:332
  27.5 8.7 %collective-permute-start.2 = (f32[2,128,256]{2,1,0:T(8,128)}, f32[2,128,256]{2,1,0:T(8,128)S(1)}, u32[]{:S(2)}, u32[]{:S(2)}) collective-permute-start(f32[2,128,256]{2,1,0:T(8,128)} %get-tuple-element.30.base), channel_id=1, source_target_pairs={{0,2},{1,3},{4,6},{5,7},{8,10},{9,11},{12,14},{13,15},{16,18},{17,... | collective-permute-start | bytes 786440 | tf_op jit(solution)/shard_map/ppermute | solution.py:335
  34.7 5.4 %copy-start.4 = (f32[2,256,256]{2,1,0:T(8,128)S(1)}, f32[2,256,256]{2,1,0:T(8,128)}, u32[]{:S(2)}) copy-start(f32[2,256,256]{2,1,0:T(8,128)} %get-tuple-element.32.r_mine) | copy-start | bytes 1572868
  34.7 7.0 %copy-start = (f32[2,256,256]{2,1,0:T(8,128)S(1)}, f32[2,256,256]{2,1,0:T(8,128)}, u32[]{:S(2)}) copy-start(f32[2,256,256]{2,1,0:T(8,128)} %get-tuple-element.35.c_mine.mine) | copy-start | bytes 1572868
  34.7 9.8 %collective-permute-start.4 = (f32[2,256,256]{2,1,0:T(8,128)}, f32[2,256,256]{2,1,0:T(8,128)S(1)}, u32[]{:S(2)}, u32[]{:S(2)}) collective-permute-start(f32[2,256,256]{2,1,0:T(8,128)} %get-tuple-element.31.matrix), channel_id=1, source_target_pairs={{4,6},{5,7},{12,14},{13,15},{20,22},{21,23},{28,30},{29,31}} | collective-permute-start | bytes 1572872 | tf_op jit(solution)/shard_map/ppermute | solution.py:335
  39.5 3.5 %collective-permute-start.3 = (f32[2,128,256]{2,1,0:T(8,128)}, f32[2,128,256]{2,1,0:T(8,128)S(1)}, u32[]{:S(2)}, u32[]{:S(2)}) collective-permute-start(f32[2,128,256]{2,1,0:T(8,128)} %shard_map.58), channel_id=1, source_target_pairs={{2,6},{3,7},{10,14},{11,15},{18,22},{19,23},{26,30},{27,31}} | collective-permute-start | bytes 786440 | tf_op jit(solution)/shard_map/ppermute | solution.py:335
  40.2 28.9 %collective-permute-start.6 = (f32[2,256,256]{2,1,0:T(8,128)S(1)}, f32[2,256,256]{2,1,0:T(8,128)S(1)}, u32[]{:S(2)}, u32[]{:S(2)}) collective-permute-start(f32[2,256,256]{2,1,0:T(8,128)S(1)} %copy-done.4), channel_id=1, source_target_pairs={{0,1},{1,0},{2,3},{3,2},{4,5},{5,4},{6,7},{7,6},{8,9},{9,8},{10,11... | collective-permute-start | bytes 1572872 | tf_op jit(solution)/shard_map/ppermute | solution.py:332
  41.7 27.3 %collective-permute-start.8 = (f32[2,256,256]{2,1,0:T(8,128)S(1)}, f32[2,256,256]{2,1,0:T(8,128)S(1)}, u32[]{:S(2)}, u32[]{:S(2)}) collective-permute-start(f32[2,256,256]{2,1,0:T(8,128)S(1)} %copy-done), channel_id=1, source_target_pairs={{0,1},{1,0},{2,3},{3,2},{4,5},{5,4},{6,7},{7,6},{8,9},{9,8},{10,11... | collective-permute-start | bytes 1572872 | tf_op jit(solution)/shard_map/ppermute | solution.py:332
  42.2 2.3 %collective-permute-start.5 = (f32[2,128,256]{2,1,0:T(8,128)}, f32[2,128,256]{2,1,0:T(8,128)S(1)}, u32[]{:S(2)}, u32[]{:S(2)}) collective-permute-start(f32[2,128,256]{2,1,0:T(8,128)} %shard_map.58), channel_id=1, source_target_pairs={{2,4},{3,5},{10,12},{11,13},{18,20},{19,21},{26,28},{27,29}} | collective-permute-start | bytes 786440 | tf_op jit(solution)/shard_map/ppermute | solution.py:335
  42.9 26.1 %collective-permute-start.7 = (f32[2,128,256]{2,1,0:T(8,128)}, f32[2,128,256]{2,1,0:T(8,128)S(1)}, u32[]{:S(2)}, u32[]{:S(2)}) collective-permute-start(f32[2,128,256]{2,1,0:T(8,128)} %get-tuple-element.34), channel_id=1, source_target_pairs={{0,1},{1,0},{2,3},{3,2},{4,5},{5,4},{6,7},{7,6},{8,9},{9,8},{10,11... | collective-permute-start | bytes 786440 | tf_op jit(solution)/shard_map/ppermute | solution.py:332
  75.3 14.5 %collective-permute-start.10 = (f32[2,128,256]{2,1,0:T(8,128)}, f32[2,128,256]{2,1,0:T(8,128)S(1)}, u32[]{:S(2)}, u32[]{:S(2)}) collective-permute-start(f32[2,128,256]{2,1,0:T(8,128)} %get-tuple-element.38.base), channel_id=1, source_target_pairs={{6,4},{7,5},{2,0},{3,1},{14,12},{15,13},{10,8},{11,9},{22,20},{23,... | collective-permute-start | bytes 786440 | tf_op jit(solution)/shard_map/ppermute | solution.py:335
  79.2 15.9 %copy-start.20 = (f32[2,128,256]{2,1,0:T(8,128)S(1)}, f32[2,128,256]{2,1,0:T(8,128)}, u32[]{:S(2)}) copy-start(f32[2,128,256]{2,1,0:T(8,128)} %get-tuple-element.37) | copy-start | bytes 786436
  79.2 24.3 %collective-permute-start.12 = (f32[2,256,256]{2,1,0:T(8,128)}, f32[2,256,256]{2,1,0:T(8,128)S(1)}, u32[]{:S(2)}, u32[]{:S(2)}) collective-permute-start(f32[2,256,256]{2,1,0:T(8,128)} %shard_map.63.matrix), channel_id=1, source_target_pairs={{2,0},{3,1},{10,8},{11,9},{18,16},{19,17},{26,24},{27,25}} | collective-permute-start | bytes 1572872 | tf_op jit(solution)/shard_map/ppermute | solution.py:335
  93.1 10.4 %collective-permute-start.11 = (f32[2,128,256]{2,1,0:T(8,128)}, f32[2,128,256]{2,1,0:T(8,128)S(1)}, u32[]{:S(2)}, u32[]{:S(2)}) collective-permute-start(f32[2,128,256]{2,1,0:T(8,128)} %shard_map.64), channel_id=1, source_target_pairs={{4,0},{5,1},{12,8},{13,9},{20,16},{21,17},{28,24},{29,25}} | collective-permute-start | bytes 786440 | tf_op jit(solution)/shard_map/ppermute | solution.py:335
  94.4 9.1 %collective-permute-start.13 = (f32[2,128,256]{2,1,0:T(8,128)}, f32[2,128,256]{2,1,0:T(8,128)S(1)}, u32[]{:S(2)}, u32[]{:S(2)}) collective-permute-start(f32[2,128,256]{2,1,0:T(8,128)} %shard_map.64), channel_id=1, source_target_pairs={{4,2},{5,3},{12,10},{13,11},{20,18},{21,19},{28,26},{29,27}} | collective-permute-start | bytes 786440 | tf_op jit(solution)/shard_map/ppermute | solution.py:335
  95.1 17.1 %collective-permute-start.9 = (f32[2,128,256]{2,1,0:T(8,128)S(1)}, f32[2,128,256]{2,1,0:T(8,128)S(1)}, u32[]{:S(2)}, u32[]{:S(2)}) collective-permute-start(f32[2,128,256]{2,1,0:T(8,128)S(1)} %copy-done.20), channel_id=1, source_target_pairs={{0,1},{1,0},{2,3},{3,2},{4,5},{5,4},{6,7},{7,6},{8,9},{9,8},{10,11... | collective-permute-start | bytes 786440 | tf_op jit(solution)/shard_map/ppermute | solution.py:332
  110.6 6.6 %collective-permute-start.14 = (f32[2,128,256]{2,1,0:T(8,128)}, f32[2,128,256]{2,1,0:T(8,128)S(1)}, u32[]{:S(2)}, u32[]{:S(2)}) collective-permute-start(f32[2,128,256]{2,1,0:T(8,128)} %get-tuple-element.41), channel_id=1, source_target_pairs={{0,1},{1,0},{2,3},{3,2},{4,5},{5,4},{6,7},{7,6},{8,9},{9,8},{10,11... | collective-permute-start | bytes 786440 | tf_op jit(solution)/shard_map/ppermute | solution.py:332
  122.1 2.1 %collective-permute-start.15 = (f32[2,256,256]{2,1,0:T(8,128)}, f32[2,256,256]{2,1,0:T(8,128)S(1)}, u32[]{:S(2)}, u32[]{:S(2)}) collective-permute-start(f32[2,256,256]{2,1,0:T(8,128)} %get-tuple-element.43), channel_id=1, source_target_pairs={{0,8},{8,0},{16,24},{24,16},{1,9},{9,1},{17,25},{25,17},{2,10},{10... | collective-permute-start | bytes 1572872 | tf_op jit(solution)/shard_map/ppermute | solution.py:386
  127.1 8.6 %collective-permute-start.16 = (f32[2,256,128]{2,1,0:T(8,128)}, f32[2,256,128]{2,1,0:T(8,128)S(1)}, u32[]{:S(2)}, u32[]{:S(2)}) collective-permute-start(f32[2,256,128]{2,1,0:T(8,128)} %get-tuple-element.45), channel_id=1, source_target_pairs={{0,16},{8,24},{16,0},{24,8},{1,17},{9,25},{17,1},{25,9},{2,18},{10... | collective-permute-start | bytes 786440 | tf_op jit(solution)/shard_map/ppermute | solution.py:386
  138.7 1.6 collective-permute-start.17
  141.2 7.3 %copy-start.19 = (f32[2,256,128]{2,1,0:T(8,128)S(1)}, f32[2,256,128]{2,1,0:T(8,128)}, u32[]{:S(2)}) copy-start(f32[2,256,128]{2,1,0:T(8,128)} %get-tuple-element.48.refs_0_) | copy-start | bytes 786436
  141.2 5.6 %collective-permute-start.18 = (f32[128,256]{1,0:T(8,128)S(1)}, f32[128,256]{1,0:T(8,128)S(1)}, u32[]{:S(2)}, u32[]{:S(2)}) collective-permute-start(f32[128,256]{1,0:T(8,128)S(1)} %add.15), channel_id=1, source_target_pairs={{0,16},{8,24},{16,0},{24,8},{1,17},{9,25},{17,1},{25,9},{2,18},{10... | collective-permute-start | bytes 393224 | tf_op jit(solution)/shard_map/ppermute | solution.py:386
  146.8 5.0 %collective-permute-start.19 = (f32[128,256]{1,0:T(8,128)S(1)}, f32[128,256]{1,0:T(8,128)S(1)}, u32[]{:S(2)}, u32[]{:S(2)}) collective-permute-start(f32[128,256]{1,0:T(8,128)S(1)} %add.16), channel_id=1, source_target_pairs={{0,1},{1,0},{2,3},{3,2},{4,5},{5,4},{6,7},{7,6},{8,9},{9,8},{10,11... | collective-permute-start | bytes 393224 | tf_op jit(solution)/shard_map/ppermute | solution.py:420
  148.5 9.1 %collective-permute-start.23 = (f32[2,256,128]{2,1,0:T(8,128)S(1)}, f32[2,256,128]{2,1,0:T(8,128)S(1)}, u32[]{:S(2)}, u32[]{:S(2)}) collective-permute-start(f32[2,256,128]{2,1,0:T(8,128)S(1)} %copy-done.19), channel_id=1, source_target_pairs={{0,8},{8,0},{16,24},{24,16},{1,9},{9,1},{17,25},{25,17},{2,10},{10... | collective-permute-start | bytes 786440 | tf_op jit(solution)/shard_map/ppermute | solution.py:386
  151.9 5.3 %collective-permute-start.20 = (f32[128,256]{1,0:T(8,128)S(1)}, f32[128,256]{1,0:T(8,128)S(1)}, u32[]{:S(2)}, u32[]{:S(2)}) collective-permute-start(f32[128,256]{1,0:T(8,128)S(1)} %add.17), channel_id=1, source_target_pairs={{0,2},{1,3},{2,0},{3,1},{4,6},{5,7},{6,4},{7,5},{8,10},{9,11},{10,... | collective-permute-start | bytes 393224 | tf_op jit(solution)/shard_map/ppermute | solution.py:420
  153.4 9.8 %collective-permute-start.24 = (f32[2,256,128]{2,1,0:T(8,128)S(1)}, f32[2,256,128]{2,1,0:T(8,128)S(1)}, u32[]{:S(2)}, u32[]{:S(2)}) collective-permute-start(f32[2,256,128]{2,1,0:T(8,128)S(1)} %copy-done.19), channel_id=1, source_target_pairs={{0,16},{8,24},{16,0},{24,8},{1,17},{9,25},{17,1},{25,9},{2,18},{10... | collective-permute-start | bytes 786440 | tf_op jit(solution)/shard_map/ppermute | solution.py:386
  157.2 5.9 %collective-permute-start.21 = (f32[128,256]{1,0:T(8,128)S(1)}, f32[128,256]{1,0:T(8,128)S(1)}, u32[]{:S(2)}, u32[]{:S(2)}) collective-permute-start(f32[128,256]{1,0:T(8,128)S(1)} %add.18), channel_id=1, source_target_pairs={{0,4},{1,5},{2,6},{3,7},{4,0},{5,1},{6,2},{7,3},{8,12},{9,13},{10,... | collective-permute-start | bytes 393224 | tf_op jit(solution)/shard_map/ppermute | solution.py:420
  157.6 7.7 %copy-start.21 = (f32[2,256,128]{2,1,0:T(8,128)}, f32[2,256,128]{2,1,0:T(8,128)S(1)}, u32[]{:S(2)}) copy-start(f32[2,256,128]{2,1,0:T(8,128)S(1)} %collective-permute-done.23.refs_1_) | copy-start | bytes 786436
  157.6 7.7 %collective-permute-start.25 = (f32[2,256,128]{2,1,0:T(8,128)S(1)}, f32[2,256,128]{2,1,0:T(8,128)S(1)}, u32[]{:S(2)}, u32[]{:S(2)}) collective-permute-start(f32[2,256,128]{2,1,0:T(8,128)S(1)} %collective-permute-done.23.refs_1_), channel_id=1, source_target_pairs={{0,16},{8,24},{16,0},{24,8},{1,17},{9,25},{17,1},{25,9},{2,18},{10... | collective-permute-start | bytes 786440 | tf_op jit(solution)/shard_map/ppermute | solution.py:386
  163.1 2.2 %copy-start.17 = (f32[128,256]{1,0:T(8,128)}, f32[128,256]{1,0:T(8,128)S(1)}, u32[]{:S(2)}) copy-start(f32[128,256]{1,0:T(8,128)S(1)} %add.19.mine) | copy-start | bytes 393220
  163.2 2.2 %collective-permute-start.22 = (f32[128,256]{1,0:T(8,128)S(1)}, f32[128,256]{1,0:T(8,128)S(1)}, u32[]{:S(2)}, u32[]{:S(2)}) collective-permute-start(f32[128,256]{1,0:T(8,128)S(1)} %add.19.mine), channel_id=1, source_target_pairs={{0,8},{8,0},{16,24},{24,16},{1,9},{9,1},{17,25},{25,17},{2,10},{10... | collective-permute-start | bytes 393224 | tf_op jit(solution)/shard_map/ppermute | solution.py:386
  (20 other events, 17.6 us)

commit v2 on v1

v2 whole, which is shorter than its diff:
```python
import functools

import jax
import jax.numpy as jnp
from jax import lax
from jax.experimental import pallas as pl
from jax.experimental.pallas import tpu as pltpu
from jax.sharding import PartitionSpec as P


NS_ITERS = 2
GRANT = 16 << 20
HIGH = lax.Precision.HIGH
F32 = jnp.float32


def dot(a, b, dims):
    return lax.dot_general(a, b, (dims, ((), ())), precision=HIGH, preferred_element_type=F32)


def times(left, right, dims):
    real = dot(left[0], right[0], dims) - dot(left[1], right[1], dims)
    imag = dot(left[0], right[1], dims) + dot(left[1], right[0], dims)
    return real, imag


def plain(left, right):
    return times(left, right, ((1,), (0,)))


def trans(left, right):
    return times(left, right, ((1,), (1,)))


def plus(a, b):
    return a[0] + b[0], a[1] + b[1]


def minus(a, b):
    return a[0] - b[0], a[1] - b[1]


def negative(a):
    return -a[0], -a[1]


def pick(choice, a, b):
    return jnp.where(choice, a[0], b[0]), jnp.where(choice, a[1], b[1])


def pair(ref, *index):
    return ref[(*index, 0)], ref[(*index, 1)]


def put(ref, value):
    ref[0] = value[0]
    ref[1] = value[1]


def rows_of(ref, start, size):
    start = pl.multiple_of(start, size)
    return ref[0, pl.ds(start, size), :], ref[1, pl.ds(start, size), :]


def call(body, outs, *args, products=1):
    shapes = [jax.ShapeDtypeStruct(shape, F32) for shape in outs]
    return pl.pallas_call(
        body,
        out_shape=shapes,
        in_specs=[pl.BlockSpec(memory_space=pltpu.VMEM)] * len(args),
        out_specs=[pl.BlockSpec(memory_space=pltpu.VMEM)] * len(outs),
        cost_estimate=pl.CostEstimate(
            flops=products * 3 * 8 * 256**3, bytes_accessed=1 << 20, transcendentals=0
        ),
        compiler_params=pltpu.CompilerParams(vmem_limit_bytes=GRANT),
    )(*args)


def side():
    return lax.rem(lax.axis_index("rows"), 2) == 0


def map_kernel(lower, out):
    count = lower.shape[0]
    value = pair(lower, 0)
    for number in range(1, count):
        value = plain(pair(lower, number), value)
    if count % 2:
        value = negative(value)
    put(out, value)


def local_kernel(piece, pivot, lower, upper, ahead, states, bkeep, bsend, gkeep, late, work):
    count, width = pivot.shape[0], pivot.shape[-1]
    half = bkeep.shape[1]
    mine = jnp.where(side(), 0, half)
    other = half - mine
    last = None
    for number in range(count):
        columns = slice(number * width, (number + 1) * width)
        value = trans((piece[0, :, columns], piece[1, :, columns]), pair(pivot, number))
        if last is not None:
            value = minus(value, trans(last, pair(lower, number)))
        states[number, 0] = value[0]
        states[number, 1] = value[1]
        last = value
    put(bkeep, rows_of(states.at[count - 1], mine, half))
    put(bsend, rows_of(states.at[count - 1], other, half))
    for number in range(count - 2, -1, -1):
        last = minus(pair(states, number), trans(last, pair(upper, number)))
    put(work, last)
    put(gkeep, rows_of(work, mine, half))
    value = rows_of(work, other, half)
    for part in range(2):
        late[part, 2 * width :, :] = value[part]
    levels = [negative(pair(lower, 0))]
    for number in range(1, count - 1):
        levels.append(negative(plain(pair(lower, number), levels[-1])))
    if count > 1:
        levels.append(pair(ahead))
    value = levels[-1]
    for number in range(count - 2, -1, -1):
        value = minus(levels[number], plain(pair(upper, number), value))
    for part in range(2):
        late[part, :width, :] = value[part]
    value = pair(upper, count - 1)
    for number in range(count - 2, -1, -1):
        value = plain(pair(upper, number), value)
    if count % 2:
        value = negative(value)
    for part in range(2):
        late[part, width : 2 * width, :] = value[part]


def part_of(ref, start, size):
    return ref[0, start : start + size, :], ref[1, start : start + size, :]


def join_kernel(mine, theirs, bmine, btheirs, out_b, out_a):
    first = side()
    a_first = pick(first, pair(mine), pair(theirs))
    a_second = pick(first, pair(theirs), pair(mine))
    b_first = pick(first, pair(bmine), pair(btheirs))
    b_second = pick(first, pair(btheirs), pair(bmine))
    put(out_b, plus(trans(b_first, a_second), b_second))
    put(out_a, plain(a_second, a_first))


def join_back_kernel(mine, theirs, out):
    first = side()
    size = out.shape[1]
    c_first = pick(first, part_of(mine, size, size), part_of(theirs, size, size))
    c_second = pick(first, part_of(theirs, size, size), part_of(mine, size, size))
    put(out, plain(c_first, c_second))


def apply_kernel(state, matrix, base, out):
    put(out, plus(trans(pair(state), pair(matrix)), pair(base)))


def turn_kernel(inflow, a_mine, a_theirs, b_mine, b_theirs, g_mine, late_mine, late_theirs,
                in_own, in_other, mid, out):
    first = side()
    size = a_mine.shape[1]
    half = inflow.shape[1]
    entering = pair(inflow)
    a_first = pick(first, pair(a_mine), pair(a_theirs))
    b_first = pick(first, pair(b_mine), pair(b_theirs))
    second = plus(trans(entering, a_first), b_first)
    put(in_own, pick(first, entering, second))
    put(in_other, pick(first, second, entering))
    r_mine, r_theirs = part_of(late_mine, 0, size), part_of(late_theirs, 0, size)
    c_mine, c_theirs = part_of(late_mine, size, size), part_of(late_theirs, size, size)
    g_own, g_theirs = pair(g_mine), part_of(late_theirs, 2 * size, half)
    middle = plus(pick(first, g_theirs, g_own), trans(second, pick(first, r_theirs, r_mine)))
    put(mid, middle)
    value = plus(pick(first, g_own, g_theirs), trans(entering, pick(first, r_mine, r_theirs)))
    put(out, plus(value, trans(middle, pick(first, c_mine, c_theirs))))


def back_in_kernel(back_inflow, mid, late_mine, late_theirs, own, other):
    first = side()
    size = back_inflow.shape[2]
    c_mine, c_theirs = part_of(late_mine, size, size), part_of(late_theirs, size, size)
    entering = pair(back_inflow)
    first_in = plus(pair(mid), trans(entering, pick(first, c_theirs, c_mine)))
    put(own, pick(first, first_in, entering))
    put(other, pick(first, entering, first_in))


def swept_kernel(states, in_own, in_theirs, lower, out_own, out_theirs):
    count = states.shape[0]
    half = in_own.shape[1]
    mine = jnp.where(side(), 0, half)
    for carry, start, out in ((in_own, mine, out_own), (in_theirs, half - mine, out_theirs)):
        carry = pair(carry)
        for number in range(count):
            carry = negative(trans(carry, pair(lower, number)))
            put(out.at[number], plus(rows_of(states.at[number], start, half), carry))


def solved_kernel(swept, entering, upper, weights, keep, send):
    count, width = swept.shape[0], swept.shape[-1]
    wreal, wimag = weights[0, 0], weights[0, 1]
    carry = pair(entering)
    upward = lax.rem(lax.axis_index("pole"), 2) == 1
    for number in range(count - 1, -1, -1):
        carry = minus(pair(swept, number), trans(carry, pair(upper, number)))
        value = (wreal * carry[0] - wimag * carry[1], wreal * carry[1] + wimag * carry[0])
        kept = upward if number >= count // 2 else jnp.logical_not(upward)
        columns = slice((number % (count // 2)) * width, (number % (count // 2) + 1) * width)

        @pl.when(kept)
        def _():
            for part in range(2):
                keep[part, :, columns] = value[part]

        @pl.when(jnp.logical_not(kept))
        def _():
            for part in range(2):
                send[part, :, columns] = value[part]


def gram_kernel(own, own_more, theirs, theirs_more, total, keep, send, work):
    size = total.shape[1]
    half = size // 2
    mine = jnp.where(side(), 0, half)
    for first, second, start in ((own, own_more, mine), (theirs, theirs_more, half - mine)):
        start = pl.multiple_of(start, half)
        for part in range(2):
            total[part, pl.ds(start, half), :] = first[part] + second[part]
    basis = pair(total)
    dims = ((1,), (1,))
    real = dot(basis[0], basis[0], dims) + dot(basis[1], basis[1], dims)
    imag = dot(basis[0], basis[1], dims) - dot(basis[1], basis[0], dims)
    row = lax.broadcasted_iota(jnp.int32, (size, size), 0)
    column = lax.broadcasted_iota(jnp.int32, (size, size), 1)
    work[...] = jnp.where(row <= column, real, imag)
    start = pl.multiple_of(lax.rem(lax.axis_index("pole"), 2) * half, half)
    keep[...] = work[pl.ds(start, half), :]
    send[...] = work[pl.ds(pl.multiple_of(half - start, half), half), :]


def finish_kernel(states, mine, theirs, q_mine, q_theirs, out, held, slab):
    size = held.shape[0]
    half = size // 2
    pole = lax.axis_index("pole")
    start = pl.multiple_of(lax.rem(pole, 2) * half, half)
    held[pl.ds(start, half), :] = mine[...]
    held[pl.ds(pl.multiple_of(half - start, half), half), :] = theirs[...]
    packed = held[...]
    turned = packed.T
    row = lax.broadcasted_iota(jnp.int32, (size, size), 0)
    column = lax.broadcasted_iota(jnp.int32, (size, size), 1)
    real = jnp.where(row <= column, packed, turned)
    imag = jnp.where(row < column, turned, jnp.where(row > column, -packed, 0.0))
    frob = jnp.sqrt(jnp.sum(real * real + imag * imag, keepdims=True))
    current = (real / frob, imag / frob)
    eye = jnp.where(row == column, 1.0, 0.0)
    columns = out.shape[1]
    inverse = None
    for sweep in range(NS_ITERS):
        both = current if inverse is None else plain(inverse, current)
        factor = (1.5 * eye - 0.5 * both[0], -0.5 * both[1])
        if sweep < NS_ITERS - 1:
            current = plain(current, factor)
            inverse = factor if inverse is None else plain(factor, inverse)
        else:
            put(slab, factor)
            place = pl.multiple_of(pole * columns, columns)
            mixing = (slab[0, pl.ds(place, columns), :], slab[1, pl.ds(place, columns), :])
            if inverse is not None:
                mixing = plain(mixing, inverse)
    factor = jnp.sqrt(states / frob)
    mixing = (mixing[0] * factor, mixing[1] * factor)
    width = q_mine.shape[2]
    place = lax.rem(pole, 2) * width
    for piece, offset in ((q_mine, place), (q_theirs, width - place)):
        value = plain(mixing, pair(piece))
        for part in range(2):
            out[part, :, pl.ds(pl.multiple_of(offset, width), width)] = value[part]


def shards(subspace, pivots, lower_blocks, upper_blocks, pole_weights):
    devices = lax.axis_size("rows")
    poles = lax.axis_size("pole")
    count, width = pivots.shape[1], pivots.shape[-1]
    vectors = subspace.shape[1]
    half = vectors // 2
    nodes = devices // 2
    pivot, lower, upper = pivots[0], lower_blocks[0], upper_blocks[0]
    square = (2, width, width)
    state = (2, vectors, width)
    strip = (2, half, width)
    vmem = pltpu.VMEM

    def scratch(body, outs, extra, *args, products=1):
        return pl.pallas_call(
            body,
            out_shape=[jax.ShapeDtypeStruct(shape, F32) for shape in outs],
            in_specs=[pl.BlockSpec(memory_space=vmem)] * len(args),
            out_specs=[pl.BlockSpec(memory_space=vmem)] * len(outs),
            scratch_shapes=[vmem(shape, F32) for shape in extra],
            cost_estimate=pl.CostEstimate(
                flops=products * 3 * 8 * 256**3, bytes_accessed=1 << 20, transcendentals=0
            ),
            compiler_params=pltpu.CompilerParams(vmem_limit_bytes=GRANT),
        )(*args)

    swap = [(place, place ^ 1) for place in range(devices)]

    def beside(value):
        return lax.ppermute(value, "rows", swap)

    def between(value, moves):
        return lax.ppermute(
            value, "rows", [(2 * a + s, 2 * b + s) for a, b in moves for s in range(2)]
        )

    def prefix(base, matrix, order):
        inflow = None
        for hop in range(nodes - 1):
            passed = base
            if hop:
                (passed,) = call(apply_kernel, [strip], inflow, matrix, base)
            came = between(passed, [(order[hop], order[hop + 1])])
            inflow = came if inflow is None else inflow + came
        return jnp.zeros(strip, F32) if inflow is None else inflow

    (a_mine,) = call(map_kernel, [square], lower)
    a_theirs = beside(a_mine)
    states, b_mine, b_send, g_mine, late_mine = scratch(
        local_kernel, [(count,) + state, strip, strip, strip, (2, 2 * width + half, width)],
        [state], subspace, pivot, lower, upper, a_mine, products=2 * count + 3,
    )
    b_theirs = beside(b_send)
    late_theirs = beside(late_mine)

    b_node, a_node = call(join_kernel, [strip, square], a_mine, a_theirs, b_mine, b_theirs)
    order = list(range(nodes))
    inflow = prefix(b_node, a_node, order)
    in_own, in_other, mid, g_node = call(
        turn_kernel, [strip] * 4, inflow, a_mine, a_theirs, b_mine, b_theirs,
        g_mine, late_mine, late_theirs, products=2,
    )
    (c_node,) = call(join_back_kernel, [square], late_mine, late_theirs)
    back_inflow = prefix(g_node, c_node, order[::-1])
    in_theirs = beside(in_other)
    swept_own, swept_theirs = call(
        swept_kernel, [(count,) + strip] * 2, states, in_own, in_theirs, lower, products=count
    )
    x_own, x_other = call(
        back_in_kernel, [strip] * 2, back_inflow, mid, late_mine, late_theirs
    )
    x_theirs = beside(x_other)

    def over_poles(value, bit):
        return lax.ppermute(value, "pole", [(place, place ^ (1 << bit)) for place in range(poles)])

    levels = poles.bit_length() - 1
    columns = count * width
    block = (2, half, columns // 2)

    def poled(swept, entering):
        keep, send = pl.pallas_call(
            solved_kernel,
            out_shape=[jax.ShapeDtypeStruct(block, F32)] * 2,
            in_specs=[pl.BlockSpec(memory_space=vmem)] * 3
            + [pl.BlockSpec(memory_space=pltpu.SMEM)],
            out_specs=[pl.BlockSpec(memory_space=vmem)] * 2,
            compiler_params=pltpu.CompilerParams(vmem_limit_bytes=GRANT),
        )(swept, entering, upper, pole_weights)
        value, more = keep, over_poles(send, 0)
        for bit in range(1, levels):
            value = value + more
            more = over_poles(value, bit)
        return value, more

    own, own_more = poled(swept_own, x_own)
    theirs, theirs_more = poled(swept_theirs, x_theirs)
    total, packed, packed_send = scratch(
        gram_kernel, [(2, vectors, columns // 2), (half, vectors), (half, vectors)],
        [(vectors, vectors)], own, own_more, theirs, theirs_more,
    )
    packed = packed + over_poles(packed_send, 0)
    for bit in range(devices.bit_length() - 1):
        packed = packed + lax.ppermute(
            packed, "rows", [(place, place ^ (1 << bit)) for place in range(devices)]
        )
    packed_theirs = over_poles(packed, 0)
    total_theirs = over_poles(total, 0)
    (result,) = scratch(
        functools.partial(finish_kernel, float(columns * devices)),
        [(2, vectors // poles, columns)], [(vectors, vectors), state],
        packed, packed_theirs, total, total_theirs, products=4,
    )
    return result


def solution(mesh):
    placed = (
        P(None, None, "rows"),
        P("pole", "rows", None, None, None),
        P("pole", "rows", None, None, None),
        P("pole", "rows", None, None, None),
        P("pole", None),
    )
    return jax.shard_map(
        shards, mesh=mesh, in_specs=placed, out_specs=P(None, "pole", "rows"), check_vma=False
    )
```

time: 172 us -> 149 us (0.87)
  Pallas kernels: 52.4 us -> 20.8 us
  waiting for transfers between devices: 76.7 us -> 102 us
  starting transfers between devices: 30.1 us -> 21.2 us
  local copies, waits for them, and re-layouts: 10.7 us -> 3.78 us
    pallas_call x11 -> x10, Pallas kernels: 32.3 us -> 10 us  [call(): pl.pallas_call(body, out_shape=shapes, in_specs=[pl.BlockSpec(memory_spac...]
    ppermute x8 -> x6, waiting for transfers between devices: 16.8 us -> 33.5 us  [between(): lax.ppermute(value, 'rows', [(2 * a + s, 2 * b + s) for a, b in moves for...]
    pallas_call x4 -> x3, Pallas kernels: 15.9 us -> 6.92 us  [scratch(): pl.pallas_call(body, out_shape=[jax.ShapeDtypeStruct(shape, F32) for shap...]
    unnamed x52 -> x12, local copies, waits for them, and re-layouts: 10.7 us -> 3.78 us
    ppermute x3, waiting for transfers between devices: 9.63 us -> 15.8 us  [shards(): lax.ppermute(packed, 'rows', [(place, place ^ 1 << bit) for place in rang...]
    ppermute x7 -> x5, waiting for transfers between devices: 33.6 us -> 38.5 us  [beside(): return lax.ppermute(value, 'rows', swap)]
    ppermute x8 -> x7, starting transfers between devices: 6.24 us -> 3.29 us  [over_poles(): lax.ppermute(value, 'pole', [(place, place ^ 1 << bit) for place in range...]
    ppermute x8 -> x6, starting transfers between devices: 10.5 us -> 7.74 us  [between(): lax.ppermute(value, 'rows', [(2 * a + s, 2 * b + s) for a, b in moves for...]
  transfers between devices with their start and end apart: 26 -> 21, of which waited for: 14 -> 11; matrix products, arithmetic and copies ran while one was open for 0% -> 0% of each run, Pallas kernels for 16% -> 9%
where the time goes in v2:
time: 149 us; the launch traced here: 148 us
  waiting for transfers between devices  102 us (68%)
  starting transfers between devices  21.2 us (14%)
  Pallas kernels  20.8 us (14%)
  local copies, waits for them, and re-layouts  3.78 us (3%)
    ppermute x5, waiting for transfers between devices, beside(): return lax.ppermute(value, 'rows', swap)  38.5 us
    ppermute x6, waiting for transfers between devices, between(): lax.ppermute(value, 'rows', [(2 * a + s, 2 * b + s) for a, b in moves for...  33.5 us
    ppermute x3, waiting for transfers between devices, shards(): lax.ppermute(packed, 'rows', [(place, place ^ 1 << bit) for place in rang...  15.8 us
    ppermute x7, waiting for transfers between devices, over_poles(): lax.ppermute(value, 'pole', [(place, place ^ 1 << bit) for place in range...  14 us
    pallas_call x10, Pallas kernels, call(): pl.pallas_call(body, out_shape=shapes, in_specs=[pl.BlockSpec(memory_spac...  10 us
    ppermute x5, starting transfers between devices, beside(): return lax.ppermute(value, 'rows', swap)  8.25 us
    ppermute x6, starting transfers between devices, between(): lax.ppermute(value, 'rows', [(2 * a + s, 2 * b + s) for a, b in moves for...  7.74 us
    pallas_call x3, Pallas kernels, scratch(): pl.pallas_call(body, out_shape=[jax.ShapeDtypeStruct(shape, F32) for shap...  6.92 us
  transfers between devices with their start and end apart: 21, of which 11 were waited for; matrix products, arithmetic and copies ran while one was open for 0% of the time, Pallas kernels for 9%

profile of v2, /device:TPU:0, one launch (start us, length us, event | category | flops | bytes accessed | tf_op | source)
XLA Modules:
  0.0 148.2 jit_solution(13803950970132565908)
XLA Ops:
  0.0 1.3 copy-done.1
  1.9 3.0 %collective-permute-start = (f32[2,256,256]{2,1,0:T(8,128)S(1)}, f32[2,256,256]{2,1,0:T(8,128)S(1)}, u32[]{:S(2)}, u32[]{:S(2)}) collective-permute-start(f32[2,256,256]{2,1,0:T(8,128)S(1)} %shard_map.55.ahead.mine.a_mine), channel_id=1, source_target_pairs={{0,1},{1,0},{2,3},{3,2},{4,5},{5,4},{6,7},{7,6},{8,9},{9,8},{10,11... | collective-permute-start | bytes 1572872 | tf_op jit(solution)/shard_map/ppermute | solution.py:313
  5.0 1.2 copy-done.4
  6.2 1.2 copy-done.5
  7.4 3.0 %shard_map.56 = (f32[2,2,256,256]{3,2,1,0:T(8,128)S(1)}, f32[2,128,256]{2,1,0:T(8,128)S(1)}, f32[2,128,256]{2,1,0:T(8,128)S(1)}, f32[2,128,256]{2,1,0:T(8,128)S(1)}, f32[2,640,256]{2,1,0:T(8,128)S(1)}) custom-call(f32[2,256,512]{2,1,0:T(8,128)S(1)} %copy-done.4, f32[2,2,256,256]{3,2,1,0:T(8,128)S(1)} %bitcast.9, f32[2,2,256,256]{3,2,1,0:T(8,128)S(1)} %bitcast.7, ...), custom_call_target="tpu_custom_call" | custom-call | flops 2818572288 | bytes 1048576 | tf_op jit(solution)/shard_map/pallas_call | solution.py:298
  10.5 2.0 %collective-permute-start.1 = (f32[2,128,256]{2,1,0:T(8,128)S(1)}, f32[2,128,256]{2,1,0:T(8,128)S(1)}, u32[]{:S(2)}, u32[]{:S(2)}) collective-permute-start(f32[2,128,256]{2,1,0:T(8,128)S(1)} %get-tuple-element.29), channel_id=1, source_target_pairs={{0,1},{1,0},{2,3},{3,2},{4,5},{5,4},{6,7},{7,6},{8,9},{9,8},{10,11... | collective-permute-start | bytes 786440 | tf_op jit(solution)/shard_map/ppermute | solution.py:313
  12.5 38.1 %collective-permute-done.1.btheirs.b_theirs = f32[2,128,256]{2,1,0:T(8,128)S(1)} collective-permute-done((f32[2,128,256]{2,1,0:T(8,128)S(1)}, f32[2,128,256]{2,1,0:T(8,128)S(1)}, u32[]{:S(2)}, u32[]{:S(2)}) %collective-permute-start.1) | collective-permute-done | bytes 262176 | tf_op jit(solution)/shard_map/ppermute | solution.py:313
  50.6 1.1 shard_map.57
  51.7 3.7 %collective-permute-start.2 = (f32[2,128,256]{2,1,0:T(8,128)S(1)}, f32[2,128,256]{2,1,0:T(8,128)S(1)}, u32[]{:S(2)}, u32[]{:S(2)}) collective-permute-start(f32[2,128,256]{2,1,0:T(8,128)S(1)} %get-tuple-element.30.base), channel_id=1, source_target_pairs={{0,2},{1,3},{8,10},{9,11},{16,18},{17,19},{24,26},{25,27}} | collective-permute-start | bytes 786440 | tf_op jit(solution)/shard_map/ppermute | solution.py:316
  55.4 4.7 %collective-permute-done.2.state = f32[2,128,256]{2,1,0:T(8,128)S(1)} collective-permute-done((f32[2,128,256]{2,1,0:T(8,128)S(1)}, f32[2,128,256]{2,1,0:T(8,128)S(1)}, u32[]{:S(2)}, u32[]{:S(2)}) %collective-permute-start.2) | collective-permute-done | bytes 262176 | tf_op jit(solution)/shard_map/ppermute | solution.py:316
  60.8 0.7 collective-permute-start.3
  62.2 0.7 collective-permute-start.4
  62.9 2.2 %shard_map.60 = (f32[2,128,256]{2,1,0:T(8,128)S(1)}, f32[2,128,256]{2,1,0:T(8,128)S(1)}, f32[2,128,256]{2,1,0:T(8,128)S(1)}, f32[2,128,256]{2,1,0:T(8,128)S(1)}) custom-call(f32[2,128,256]{2,1,0:T(8,128)S(1)} %add.31.inflow, f32[2,256,256]{2,1,0:T(8,128)S(1)} %shard_map.55.ahead.mine.a_mine, f32[2,256,256]{2,1,0:T(8,128)S(1)} %collective-permute-done.theirs.a_theirs, ...), custom_call_target="tpu_custom_call" | custom-call | flops 805306368 | bytes 1048576 | tf_op jit(solution)/shard_map/pallas_call | solution.py:67
  68.5 1.3 collective-permute-start.9
  69.8 1.6 %collective-permute-start.6 = (f32[2,128,256]{2,1,0:T(8,128)S(1)}, f32[2,128,256]{2,1,0:T(8,128)S(1)}, u32[]{:S(2)}, u32[]{:S(2)}) collective-permute-start(f32[2,128,256]{2,1,0:T(8,128)S(1)} %get-tuple-element.35), channel_id=1, source_target_pairs={{0,1},{1,0},{2,3},{3,2},{4,5},{5,4},{6,7},{7,6},{8,9},{9,8},{10,11... | collective-permute-start | bytes 786440 | tf_op jit(solution)/shard_map/ppermute | solution.py:313
  71.4 28.8 %collective-permute-done.9 = f32[2,128,256]{2,1,0:T(8,128)S(1)} collective-permute-done((f32[2,128,256]{2,1,0:T(8,128)S(1)}, f32[2,128,256]{2,1,0:T(8,128)S(1)}, u32[]{:S(2)}, u32[]{:S(2)}) %collective-permute-start.9) | collective-permute-done | bytes 262176 | tf_op jit(solution)/shard_map/ppermute | solution.py:316
  100.9 1.6 %collective-permute-start.12 = (f32[2,128,256]{2,1,0:T(8,128)S(1)}, f32[2,128,256]{2,1,0:T(8,128)S(1)}, u32[]{:S(2)}, u32[]{:S(2)}) collective-permute-start(f32[2,128,256]{2,1,0:T(8,128)S(1)} %get-tuple-element.43), channel_id=1, source_target_pairs={{0,1},{1,0},{2,3},{3,2},{4,5},{5,4},{6,7},{7,6},{8,9},{9,8},{10,11... | collective-permute-start | bytes 786440 | tf_op jit(solution)/shard_map/ppermute | solution.py:313
  102.4 2.3 %shard_map.61 = (f32[2,2,128,256]{3,2,1,0:T(8,128)S(1)}, f32[2,2,128,256]{3,2,1,0:T(8,128)S(1)}) custom-call(f32[2,2,256,256]{3,2,1,0:T(8,128)S(1)} %get-tuple-element.27.states, f32[2,128,256]{2,1,0:T(8,128)S(1)} %get-tuple-element.34.in_own, f32[2,128,256]{2,1,0:T(8,128)S(1)} %collective-permute-done.6.in_theirs, f32[2,2,256,256]{3,2,1,0:T(8,128)S(1)} %bitcast.8), custom_call_target="tpu_custom_call" | custom-call | flops 805306368 | bytes 1048576 | tf_op jit(solution)/shard_map/pallas_call | solution.py:67
  104.7 2.0 %shard_map.66 = (f32[2,128,256]{2,1,0:T(8,128)S(1)}, f32[2,128,256]{2,1,0:T(8,128)S(1)}) custom-call(f32[2,2,128,256]{3,2,1,0:T(8,128)S(1)} %get-tuple-element.36.swept, f32[2,128,256]{2,1,0:T(8,128)S(1)} %get-tuple-element.39.entering, f32[2,2,256,256]{3,2,1,0:T(8,128)S(1)} %bitcast.4, f32[1,2]{1,0:T(1,128)S(1)} %copy-done.3), custom_call_target="tpu_custom_call" | custom-call | tf_op jit(solution)/shard_map/pallas_call | solution.py:365
  107.3 1.9 %shard_map.67 = (f32[2,128,256]{2,1,0:T(8,128)S(1)}, f32[2,128,256]{2,1,0:T(8,128)S(1)}) custom-call(f32[2,2,128,256]{3,2,1,0:T(8,128)S(1)} %get-tuple-element.42.swept, f32[2,128,256]{2,1,0:T(8,128)S(1)} %collective-permute-done.12.entering, f32[2,2,256,256]{3,2,1,0:T(8,128)S(1)} %bitcast.5, f32[1,2]{1,0:T(1,128)S(1)} %copy-done.3), custom_call_target="tpu_custom_call" | custom-call | tf_op jit(solution)/shard_map/pallas_call | solution.py:365
  109.3 1.5 %collective-permute-start.11 = (f32[2,128,256]{2,1,0:T(8,128)S(1)}, f32[2,128,256]{2,1,0:T(8,128)S(1)}, u32[]{:S(2)}, u32[]{:S(2)}) collective-permute-start(f32[2,128,256]{2,1,0:T(8,128)S(1)} %add.34.own), channel_id=1, source_target_pairs={{0,16},{8,24},{16,0},{24,8},{1,17},{9,25},{17,1},{25,9},{2,18},{10... | collective-permute-start | bytes 786440 | tf_op jit(solution)/shard_map/ppermute | solution.py:358
  110.9 1.4 collective-permute-start.14
  112.4 6.2 %collective-permute-done.11.own_more = f32[2,128,256]{2,1,0:T(8,128)S(1)} collective-permute-done((f32[2,128,256]{2,1,0:T(8,128)S(1)}, f32[2,128,256]{2,1,0:T(8,128)S(1)}, u32[]{:S(2)}, u32[]{:S(2)}) %collective-permute-start.11) | collective-permute-done | bytes 262176 | tf_op jit(solution)/shard_map/ppermute | solution.py:358
  118.6 5.1 %collective-permute-done.14.theirs_more = f32[2,128,256]{2,1,0:T(8,128)S(1)} collective-permute-done((f32[2,128,256]{2,1,0:T(8,128)S(1)}, f32[2,128,256]{2,1,0:T(8,128)S(1)}, u32[]{:S(2)}, u32[]{:S(2)}) %collective-permute-start.14) | collective-permute-done | bytes 262176 | tf_op jit(solution)/shard_map/ppermute | solution.py:358
  123.7 0.7 shard_map.68
  124.5 1.3 collective-permute-done.15
  125.9 1.6 %collective-permute-start.16 = (f32[128,256]{1,0:T(8,128)S(1)}, f32[128,256]{1,0:T(8,128)S(1)}, u32[]{:S(2)}, u32[]{:S(2)}) collective-permute-start(f32[128,256]{1,0:T(8,128)S(1)} %add.36), channel_id=1, source_target_pairs={{0,1},{1,0},{2,3},{3,2},{4,5},{5,4},{6,7},{7,6},{8,9},{9,8},{10,11... | collective-permute-start | bytes 393224 | tf_op jit(solution)/shard_map/ppermute | solution.py:387
  127.4 4.1 %collective-permute-done.16 = f32[128,256]{1,0:T(8,128)S(1)} collective-permute-done((f32[128,256]{1,0:T(8,128)S(1)}, f32[128,256]{1,0:T(8,128)S(1)}, u32[]{:S(2)}, u32[]{:S(2)}) %collective-permute-start.16) | collective-permute-done | bytes 131104 | tf_op jit(solution)/shard_map/ppermute | solution.py:387
  131.8 4.8 %collective-permute-done.17 = f32[128,256]{1,0:T(8,128)S(1)} collective-permute-done((f32[128,256]{1,0:T(8,128)S(1)}, f32[128,256]{1,0:T(8,128)S(1)}, u32[]{:S(2)}, u32[]{:S(2)}) %collective-permute-start.17) | collective-permute-done | bytes 131104 | tf_op jit(solution)/shard_map/ppermute | solution.py:387
  136.6 7.0 %collective-permute-done.18 = f32[128,256]{1,0:T(8,128)S(1)} collective-permute-done((f32[128,256]{1,0:T(8,128)S(1)}, f32[128,256]{1,0:T(8,128)S(1)}, u32[]{:S(2)}, u32[]{:S(2)}) %collective-permute-start.18) | collective-permute-done | bytes 131104 | tf_op jit(solution)/shard_map/ppermute | solution.py:387
  143.7 1.3 collective-permute-done.19.theirs
  145.0 3.2 %shard_map.69 = f32[2,64,512]{2,1,0:T(8,128)} custom-call(f32[128,256]{1,0:T(8,128)S(1)} %add.39.mine, f32[128,256]{1,0:T(8,128)S(1)} %collective-permute-done.19.theirs, f32[2,256,256]{2,1,0:T(8,128)S(1)} %get-tuple-element.48.q_mine, f32[2,256,256]{2,1,0:T(8,128)S(1)} %collective-permute-done.20.q_theirs), custom_call_target="tpu_custom_call" | custom-call | flops 1610612736 | bytes 1048576 | tf_op jit(solution)/shard_map/pallas_call | solution.py:298
  (47 shorter events, 7.3 us)
Async XLA Ops:
  0.0 5.0 %copy-start = (f32[1,2,2,256,256]{4,3,2,1,0:T(8,128)S(1)}, f32[1,2,2,256,256]{4,3,2,1,0:T(8,128)}, u32[]{:S(2)}) copy-start(f32[1,2,2,256,256]{4,3,2,1,0:T(8,128)} %param.8) | copy-start | bytes 3145732
  0.0 1.3 copy-start.1
  1.9 48.7 %collective-permute-start = (f32[2,256,256]{2,1,0:T(8,128)S(1)}, f32[2,256,256]{2,1,0:T(8,128)S(1)}, u32[]{:S(2)}, u32[]{:S(2)}) collective-permute-start(f32[2,256,256]{2,1,0:T(8,128)S(1)} %shard_map.55.ahead.mine.a_mine), channel_id=1, source_target_pairs={{0,1},{1,0},{2,3},{3,2},{4,5},{5,4},{6,7},{7,6},{8,9},{9,8},{10,11... | collective-permute-start | bytes 1572872 | tf_op jit(solution)/shard_map/ppermute | solution.py:313
  5.0 1.2 copy-start.4
  6.2 1.2 copy-start.5
  10.4 52.5 %collective-permute-start.5 = (f32[2,640,256]{2,1,0:T(8,128)S(1)}, f32[2,640,256]{2,1,0:T(8,128)S(1)}, u32[]{:S(2)}, u32[]{:S(2)}) collective-permute-start(f32[2,640,256]{2,1,0:T(8,128)S(1)} %get-tuple-element.33.late_mine.mine), channel_id=1, source_target_pairs={{0,1},{1,0},{2,3},{3,2},{4,5},{5,4},{6,7},{7,6},{8,9},{9,8},{10,11... | collective-permute-start | bytes 3932168 | tf_op jit(solution)/shard_map/ppermute | solution.py:313
  10.5 40.1 %collective-permute-start.1 = (f32[2,128,256]{2,1,0:T(8,128)S(1)}, f32[2,128,256]{2,1,0:T(8,128)S(1)}, u32[]{:S(2)}, u32[]{:S(2)}) collective-permute-start(f32[2,128,256]{2,1,0:T(8,128)S(1)} %get-tuple-element.29), channel_id=1, source_target_pairs={{0,1},{1,0},{2,3},{3,2},{4,5},{5,4},{6,7},{7,6},{8,9},{9,8},{10,11... | collective-permute-start | bytes 786440 | tf_op jit(solution)/shard_map/ppermute | solution.py:313
  51.7 8.4 %collective-permute-start.2 = (f32[2,128,256]{2,1,0:T(8,128)S(1)}, f32[2,128,256]{2,1,0:T(8,128)S(1)}, u32[]{:S(2)}, u32[]{:S(2)}) collective-permute-start(f32[2,128,256]{2,1,0:T(8,128)S(1)} %get-tuple-element.30.base), channel_id=1, source_target_pairs={{0,2},{1,3},{8,10},{9,11},{16,18},{17,19},{24,26},{25,27}} | collective-permute-start | bytes 786440 | tf_op jit(solution)/shard_map/ppermute | solution.py:316
  60.8 0.7 collective-permute-start.3
  62.2 0.7 collective-permute-start.4
  65.2 1.3 collective-permute-start.7
  67.1 0.7 collective-permute-start.8
  68.5 31.7 %collective-permute-start.9 = (f32[2,128,256]{2,1,0:T(8,128)S(1)}, f32[2,128,256]{2,1,0:T(8,128)S(1)}, u32[]{:S(2)}, u32[]{:S(2)}) collective-permute-start(f32[2,128,256]{2,1,0:T(8,128)S(1)} %shard_map.64), channel_id=1, source_target_pairs={{2,0},{3,1},{10,8},{11,9},{18,16},{19,17},{26,24},{27,25}} | collective-permute-start | bytes 786440 | tf_op jit(solution)/shard_map/ppermute | solution.py:316
  69.8 32.6 %collective-permute-start.6 = (f32[2,128,256]{2,1,0:T(8,128)S(1)}, f32[2,128,256]{2,1,0:T(8,128)S(1)}, u32[]{:S(2)}, u32[]{:S(2)}) collective-permute-start(f32[2,128,256]{2,1,0:T(8,128)S(1)} %get-tuple-element.35), channel_id=1, source_target_pairs={{0,1},{1,0},{2,3},{3,2},{4,5},{5,4},{6,7},{7,6},{8,9},{9,8},{10,11... | collective-permute-start | bytes 786440 | tf_op jit(solution)/shard_map/ppermute | solution.py:313
  100.2 2.2 %copy-start.2 = (f32[1,2,2,256,256]{4,3,2,1,0:T(8,128)S(1)}, f32[1,2,2,256,256]{4,3,2,1,0:T(8,128)}, u32[]{:S(2)}) copy-start(f32[1,2,2,256,256]{4,3,2,1,0:T(8,128)} %param.7) | copy-start | bytes 3145732
  100.9 6.4 %collective-permute-start.12 = (f32[2,128,256]{2,1,0:T(8,128)S(1)}, f32[2,128,256]{2,1,0:T(8,128)S(1)}, u32[]{:S(2)}, u32[]{:S(2)}) collective-permute-start(f32[2,128,256]{2,1,0:T(8,128)S(1)} %get-tuple-element.43), channel_id=1, source_target_pairs={{0,1},{1,0},{2,3},{3,2},{4,5},{5,4},{6,7},{7,6},{8,9},{9,8},{10,11... | collective-permute-start | bytes 786440 | tf_op jit(solution)/shard_map/ppermute | solution.py:313
  102.4 2.3 %copy-start.3 = (f32[1,2]{1,0:T(1,128)S(1)}, f32[1,2]{1,0:T(1,128)}, u32[]{:S(2)}) copy-start(f32[1,2]{1,0:T(1,128)} %weights.3) | copy-start | bytes 28
  106.8 2.5 %collective-permute-start.10 = (f32[2,128,256]{2,1,0:T(8,128)S(1)}, f32[2,128,256]{2,1,0:T(8,128)S(1)}, u32[]{:S(2)}, u32[]{:S(2)}) collective-permute-start(f32[2,128,256]{2,1,0:T(8,128)S(1)} %get-tuple-element.41), channel_id=1, source_target_pairs={{0,8},{8,0},{16,24},{24,16},{1,9},{9,1},{17,25},{25,17},{2,10},{10... | collective-permute-start | bytes 786440 | tf_op jit(solution)/shard_map/ppermute | solution.py:358
  109.2 1.7 %collective-permute-start.13 = (f32[2,128,256]{2,1,0:T(8,128)S(1)}, f32[2,128,256]{2,1,0:T(8,128)S(1)}, u32[]{:S(2)}, u32[]{:S(2)}) collective-permute-start(f32[2,128,256]{2,1,0:T(8,128)S(1)} %get-tuple-element.45), channel_id=1, source_target_pairs={{0,8},{8,0},{16,24},{24,16},{1,9},{9,1},{17,25},{25,17},{2,10},{10... | collective-permute-start | bytes 786440 | tf_op jit(solution)/shard_map/ppermute | solution.py:358
  109.3 9.2 %collective-permute-start.11 = (f32[2,128,256]{2,1,0:T(8,128)S(1)}, f32[2,128,256]{2,1,0:T(8,128)S(1)}, u32[]{:S(2)}, u32[]{:S(2)}) collective-permute-start(f32[2,128,256]{2,1,0:T(8,128)S(1)} %add.34.own), channel_id=1, source_target_pairs={{0,16},{8,24},{16,0},{24,8},{1,17},{9,25},{17,1},{25,9},{2,18},{10... | collective-permute-start | bytes 786440 | tf_op jit(solution)/shard_map/ppermute | solution.py:358
  110.9 12.8 %collective-permute-start.14 = (f32[2,128,256]{2,1,0:T(8,128)S(1)}, f32[2,128,256]{2,1,0:T(8,128)S(1)}, u32[]{:S(2)}, u32[]{:S(2)}) collective-permute-start(f32[2,128,256]{2,1,0:T(8,128)S(1)} %add.35.theirs), channel_id=1, source_target_pairs={{0,16},{8,24},{16,0},{24,8},{1,17},{9,25},{17,1},{25,9},{2,18},{10... | collective-permute-start | bytes 786440 | tf_op jit(solution)/shard_map/ppermute | solution.py:358
  124.4 1.4 collective-permute-start.15
  125.9 5.6 %collective-permute-start.16 = (f32[128,256]{1,0:T(8,128)S(1)}, f32[128,256]{1,0:T(8,128)S(1)}, u32[]{:S(2)}, u32[]{:S(2)}) collective-permute-start(f32[128,256]{1,0:T(8,128)S(1)} %add.36), channel_id=1, source_target_pairs={{0,1},{1,0},{2,3},{3,2},{4,5},{5,4},{6,7},{7,6},{8,9},{9,8},{10,11... | collective-permute-start | bytes 393224 | tf_op jit(solution)/shard_map/ppermute | solution.py:387
  127.4 16.3 %collective-permute-start.20 = (f32[2,256,256]{2,1,0:T(8,128)S(1)}, f32[2,256,256]{2,1,0:T(8,128)S(1)}, u32[]{:S(2)}, u32[]{:S(2)}) collective-permute-start(f32[2,256,256]{2,1,0:T(8,128)S(1)} %get-tuple-element.48.q_mine), channel_id=1, source_target_pairs={{0,8},{8,0},{16,24},{24,16},{1,9},{9,1},{17,25},{25,17},{2,10},{10... | collective-permute-start | bytes 1572872 | tf_op jit(solution)/shard_map/ppermute | solution.py:358
  131.5 5.0 %collective-permute-start.17 = (f32[128,256]{1,0:T(8,128)S(1)}, f32[128,256]{1,0:T(8,128)S(1)}, u32[]{:S(2)}, u32[]{:S(2)}) collective-permute-start(f32[128,256]{1,0:T(8,128)S(1)} %add.37), channel_id=1, source_target_pairs={{0,2},{1,3},{2,0},{3,1},{4,6},{5,7},{6,4},{7,5},{8,10},{9,11},{10,... | collective-permute-start | bytes 393224 | tf_op jit(solution)/shard_map/ppermute | solution.py:387
  136.6 7.0 %collective-permute-start.18 = (f32[128,256]{1,0:T(8,128)S(1)}, f32[128,256]{1,0:T(8,128)S(1)}, u32[]{:S(2)}, u32[]{:S(2)}) collective-permute-start(f32[128,256]{1,0:T(8,128)S(1)} %add.38), channel_id=1, source_target_pairs={{0,4},{1,5},{2,6},{3,7},{4,0},{5,1},{6,2},{7,3},{8,12},{9,13},{10,... | collective-permute-start | bytes 393224 | tf_op jit(solution)/shard_map/ppermute | solution.py:387
  143.6 1.4 collective-permute-start.19

commit v3 on v2

--- a/solution.py
+++ b/solution.py
@@ -9,7 +9,7 @@
 
 
 NS_ITERS = 2
-GRANT = 16 << 20
+GRANT = 8 << 20
 HIGH = lax.Precision.HIGH
 F32 = jnp.float32
 
@@ -90,7 +90,7 @@
     put(out, value)
 
 
-def local_kernel(piece, pivot, lower, upper, ahead, states, bkeep, bsend, gkeep, late, work):
+def local_kernel(piece, pivot, lower, upper, ahead, states, bkeep, bsend, gkeep, cmap, late, work):
     count, width = pivot.shape[0], pivot.shape[-1]
     half = bkeep.shape[1]
     mine = jnp.where(side(), 0, half)
@@ -112,7 +112,7 @@
     put(gkeep, rows_of(work, mine, half))
     value = rows_of(work, other, half)
     for part in range(2):
-        late[part, 2 * width :, :] = value[part]
+        late[part, width:, :] = value[part]
     levels = [negative(pair(lower, 0))]
     for number in range(1, count - 1):
         levels.append(negative(plain(pair(lower, number), levels[-1])))
@@ -128,8 +128,7 @@
         value = plain(pair(upper, number), value)
     if count % 2:
         value = negative(value)
-    for part in range(2):
-        late[part, width : 2 * width, :] = value[part]
+    put(cmap, value)
 
 
 def part_of(ref, start, size):
@@ -148,9 +147,8 @@
 
 def join_back_kernel(mine, theirs, out):
     first = side()
-    size = out.shape[1]
-    c_first = pick(first, part_of(mine, size, size), part_of(theirs, size, size))
-    c_second = pick(first, part_of(theirs, size, size), part_of(mine, size, size))
+    c_first = pick(first, pair(mine), pair(theirs))
+    c_second = pick(first, pair(theirs), pair(mine))
     put(out, plain(c_first, c_second))
 
 
@@ -159,7 +157,7 @@
 
 
 def turn_kernel(inflow, a_mine, a_theirs, b_mine, b_theirs, g_mine, late_mine, late_theirs,
-                in_own, in_other, mid, out):
+                c_mine, c_theirs, in_own, in_other, mid, *outs):
     first = side()
     size = a_mine.shape[1]
     half = inflow.shape[1]
@@ -170,22 +168,59 @@
     put(in_own, pick(first, entering, second))
     put(in_other, pick(first, second, entering))
     r_mine, r_theirs = part_of(late_mine, 0, size), part_of(late_theirs, 0, size)
-    c_mine, c_theirs = part_of(late_mine, size, size), part_of(late_theirs, size, size)
-    g_own, g_theirs = pair(g_mine), part_of(late_theirs, 2 * size, half)
+    g_own, g_theirs = pair(g_mine), part_of(late_theirs, size, half)
     middle = plus(pick(first, g_theirs, g_own), trans(second, pick(first, r_theirs, r_mine)))
     put(mid, middle)
     value = plus(pick(first, g_own, g_theirs), trans(entering, pick(first, r_mine, r_theirs)))
-    put(out, plus(value, trans(middle, pick(first, c_mine, c_theirs))))
-
-
-def back_in_kernel(back_inflow, mid, late_mine, late_theirs, own, other):
+    value = plus(value, trans(middle, pick(first, pair(c_mine), pair(c_theirs))))
+    if len(outs) == 1:
+        put(outs[0], value)
+        return
+    quarter = half // 2
+    low = (value[0][:quarter], value[1][:quarter])
+    high = (value[0][quarter:], value[1][quarter:])
+    source = back_place(4) == 0
+    put(outs[0], pick(source, low, high))
+    put(outs[1], pick(source, high, low))
+
+
+def back_place(nodes):
+    return nodes - 1 - lax.div(lax.axis_index("rows"), 2)
+
+
+def middle_kernel(mine_a, mine_b, came_a, came_b, c_mine, c_other, keep, send, last):
+    place = back_place(4)
+    one = place == 1
+    c_one = pick(one, pair(c_mine), pair(c_other))
+    c_two = pick(one, pair(c_other), pair(c_mine))
+    start = pick(one, pair(came_a), pair(came_b))
+    second = plus(trans(start, c_one), pick(one, pair(mine_b), pair(came_a)))
+    third = plus(trans(second, c_two), pick(one, pair(came_b), pair(mine_a)))
+    put(keep, pick(one, start, second))
+    put(send, pick(place == 0, pair(mine_b), pick(one, second, third)))
+    put(last, third)
+
+
+def back_in(entering, mid, c_mine, c_theirs, own, other):
     first = side()
-    size = back_inflow.shape[2]
-    c_mine, c_theirs = part_of(late_mine, size, size), part_of(late_theirs, size, size)
-    entering = pair(back_inflow)
-    first_in = plus(pair(mid), trans(entering, pick(first, c_theirs, c_mine)))
+    first_in = plus(pair(mid), trans(entering, pick(first, pair(c_theirs), pair(c_mine))))
     put(own, pick(first, first_in, entering))
     put(other, pick(first, entering, first_in))
+
+
+def back_in_kernel(back_inflow, *refs):
+    back_in(pair(back_inflow), *refs)
+
+
+def back_in_parts_kernel(keep, came, last, mid, c_mine, c_theirs, own, other, work):
+    place = back_place(4)
+    low = pick(place == 1, pair(keep), pick(place == 2, pair(came), pair(last)))
+    high = pick(place == 2, pair(keep), pair(came))
+    quarter = keep.shape[1]
+    for part in range(2):
+        work[part, :quarter] = low[part]
+        work[part, quarter:] = high[part]
+    back_in(pair(work), mid, c_mine, c_theirs, own, other)
 
 
 def swept_kernel(states, in_own, in_theirs, lower, out_own, out_theirs):
@@ -329,29 +364,49 @@
 
     (a_mine,) = call(map_kernel, [square], lower)
     a_theirs = beside(a_mine)
-    states, b_mine, b_send, g_mine, late_mine = scratch(
-        local_kernel, [(count,) + state, strip, strip, strip, (2, 2 * width + half, width)],
+    states, b_mine, b_send, g_mine, c_mine, late_mine = scratch(
+        local_kernel,
+        [(count,) + state, strip, strip, strip, square, (2, width + half, width)],
         [state], subspace, pivot, lower, upper, a_mine, products=2 * count + 3,
     )
     b_theirs = beside(b_send)
+    c_theirs = beside(c_mine)
     late_theirs = beside(late_mine)
 
     b_node, a_node = call(join_kernel, [strip, square], a_mine, a_theirs, b_mine, b_theirs)
     order = list(range(nodes))
     inflow = prefix(b_node, a_node, order)
-    in_own, in_other, mid, g_node = call(
-        turn_kernel, [strip] * 4, inflow, a_mine, a_theirs, b_mine, b_theirs,
-        g_mine, late_mine, late_theirs, products=2,
-    )
-    (c_node,) = call(join_back_kernel, [square], late_mine, late_theirs)
-    back_inflow = prefix(g_node, c_node, order[::-1])
+    (c_node,) = call(join_back_kernel, [square], c_mine, c_theirs)
+    quarter = (2, half // 2, width)
+    short = nodes == 4
+    in_own, in_other, mid, *ends = call(
+        turn_kernel, [strip] * 3 + ([quarter] * 2 if short else [strip]), inflow, a_mine, a_theirs,
+        b_mine, b_theirs, g_mine, late_mine, late_theirs, c_mine, c_theirs, products=2,
+    )
+    if short:
+        c_other = between(c_node, [(1, 2), (2, 1)])
+        came_a = between(ends[0], [(3, 2), (2, 1)])
+        came_b = between(ends[1], [(3, 1), (1, 2)])
+        keep, send, last = call(
+            middle_kernel, [quarter] * 3, *ends, came_a, came_b, c_node, c_other
+        )
+        came = between(send, [(3, 2), (2, 1), (1, 0)])
+        last = between(last, [(2, 0)])
+    else:
+        back_inflow = prefix(ends[0], c_node, order[::-1])
     in_theirs = beside(in_other)
     swept_own, swept_theirs = call(
-        swept_kernel, [(count,) + strip] * 2, states, in_own, in_theirs, lower, products=count
-    )
-    x_own, x_other = call(
-        back_in_kernel, [strip] * 2, back_inflow, mid, late_mine, late_theirs
-    )
+        swept_kernel, [(count,) + strip] * 2, states, in_own, in_theirs, lower,
+        products=count,
+    )
+    if short:
+        x_own, x_other = scratch(
+            back_in_parts_kernel, [strip] * 2, [strip], keep, came, last, mid, c_mine, c_theirs
+        )
+    else:
+        x_own, x_other = call(
+            back_in_kernel, [strip] * 2, back_inflow, mid, c_mine, c_theirs
+        )
     x_theirs = beside(x_other)
 
     def over_poles(value, bit):

time: 149 us -> 123 us (0.83)
  waiting for transfers between devices: 102 us -> 67.2 us
  starting transfers between devices: 21.2 us -> 30.1 us
    ppermute x6 -> x8, waiting for transfers between devices: 33.5 us -> 16.1 us  [between(): lax.ppermute(value, 'rows', [(2 * a + s, 2 * b + s) for a, b in moves for...]
    ppermute x5 -> x6, waiting for transfers between devices: 38.5 us -> 25 us  [beside(): return lax.ppermute(value, 'rows', swap)]
    ppermute x3, starting transfers between devices: 1.89 us -> 6.43 us  [shards(): lax.ppermute(packed, 'rows', [(place, place ^ 1 << bit) for place in rang...]
    ppermute x3, waiting for transfers between devices: 15.8 us -> 12.2 us  [shards(): lax.ppermute(packed, 'rows', [(place, place ^ 1 << bit) for place in rang...]
    ppermute x6 -> x8, starting transfers between devices: 7.74 us -> 10.1 us  [between(): lax.ppermute(value, 'rows', [(2 * a + s, 2 * b + s) for a, b in moves for...]
    ppermute x5 -> x6, starting transfers between devices: 8.25 us -> 10.1 us  [beside(): return lax.ppermute(value, 'rows', swap)]
    pallas_call x10 -> x8, Pallas kernels: 10 us -> 9.21 us  [call(): pl.pallas_call(body, out_shape=shapes, in_specs=[pl.BlockSpec(memory_spac...]
    pallas_call x3 -> x4, Pallas kernels: 6.92 us -> 7.6 us  [scratch(): pl.pallas_call(body, out_shape=[jax.ShapeDtypeStruct(shape, F32) for shap...]
  transfers between devices with their start and end apart: 21 -> 24, of which waited for: 11 -> 13; matrix products, arithmetic and copies ran while one was open for 0% -> 0% of each run, Pallas kernels for 9% -> 12%
where the time goes in v3:
time: 123 us
  waiting for transfers between devices  67.2 us (55%)
  starting transfers between devices  30.1 us (24%)
  Pallas kernels  20.7 us (17%)
  local copies, waits for them, and re-layouts  4.42 us (4%)
    ppermute x6, waiting for transfers between devices, beside(): return lax.ppermute(value, 'rows', swap)  25 us
    ppermute x8, waiting for transfers between devices, between(): lax.ppermute(value, 'rows', [(2 * a + s, 2 * b + s) for a, b in moves for...  16.1 us
    ppermute x7, waiting for transfers between devices, over_poles(): lax.ppermute(value, 'pole', [(place, place ^ 1 << bit) for place in range...  13.9 us
    ppermute x3, waiting for transfers between devices, shards(): lax.ppermute(packed, 'rows', [(place, place ^ 1 << bit) for place in rang...  12.2 us
    ppermute x6, starting transfers between devices, beside(): return lax.ppermute(value, 'rows', swap)  10.1 us
    ppermute x8, starting transfers between devices, between(): lax.ppermute(value, 'rows', [(2 * a + s, 2 * b + s) for a, b in moves for...  10.1 us
    pallas_call x8, Pallas kernels, call(): pl.pallas_call(body, out_shape=shapes, in_specs=[pl.BlockSpec(memory_spac...  9.21 us
    pallas_call x4, Pallas kernels, scratch(): pl.pallas_call(body, out_shape=[jax.ShapeDtypeStruct(shape, F32) for shap...  7.6 us
  transfers between devices with their start and end apart: 24, of which 13 were waited for; matrix products, arithmetic and copies ran while one was open for 0% of the time, Pallas kernels for 12%

profile of v3, /device:TPU:0, one launch (start us, length us, event | category | flops | bytes accessed | tf_op | source)
XLA Modules:
  0.0 123.0 jit_solution(17261432203353301340)
XLA Ops:
  0.0 1.3 %copy-done.1 = f32[1,2,2,256,256]{4,3,2,1,0:T(8,128)S(1)} copy-done((f32[1,2,2,256,256]{4,3,2,1,0:T(8,128)S(1)}, f32[1,2,2,256,256]{4,3,2,1,0:T(8,128)}, u32[]{:S(2)}) %copy-start.1) | copy-done | bytes 1048600
  1.9 3.0 %collective-permute-start = (f32[2,256,256]{2,1,0:T(8,128)S(1)}, f32[2,256,256]{2,1,0:T(8,128)S(1)}, u32[]{:S(2)}, u32[]{:S(2)}) collective-permute-start(f32[2,256,256]{2,1,0:T(8,128)S(1)} %shard_map.55.ahead.mine.a_mine), channel_id=1, source_target_pairs={{0,1},{1,0},{2,3},{3,2},{4,5},{5,4},{6,7},{7,6},{8,9},{9,8},{10,11... | collective-permute-start | bytes 1572872 | tf_op jit(solution)/shard_map/ppermute | solution.py:348
  5.0 1.2 copy-done.4
  7.4 3.0 %shard_map.56 = (f32[2,2,256,256]{3,2,1,0:T(8,128)S(1)}, f32[2,128,256]{2,1,0:T(8,128)S(1)}, f32[2,128,256]{2,1,0:T(8,128)S(1)}, f32[2,128,256]{2,1,0:T(8,128)S(...) custom-call(f32[2,256,512]{2,1,0:T(8,128)S(1)} %copy-done.4, f32[2,2,256,256]{3,2,1,0:T(8,128)S(1)} %bitcast.9, ...), custom_call_target="tpu_custom_call" | custom-call | flops 2818572288 | bytes 1048576 | tf_op jit(solution)/shard_map/pallas_call | solution.py:333
  10.5 2.0 %collective-permute-start.6 = (f32[2,256,256]{2,1,0:T(8,128)S(1)}, f32[2,256,256]{2,1,0:T(8,128)S(1)}, u32[]{:S(2)}, u32[]{:S(2)}) collective-permute-start(f32[2,256,256]{2,1,0:T(8,128)S(1)} %get-tuple-element.39.c_mine.mine), channel_id=1, source_target_pairs={{0,1},{1,0},{2,3},{3,2},{4,5},{5,4},{6,7},{7,6},{8,9},{9,8},{10,11... | collective-permute-start | bytes 1572872 | tf_op jit(solution)/shard_map/ppermute | solution.py:348
  12.5 10.8 %collective-permute-done.1.btheirs.b_theirs = f32[2,128,256]{2,1,0:T(8,128)S(1)} collective-permute-done((f32[2,128,256]{2,1,0:T(8,128)S(1)}, f32[2,128,256]{2,1,0:T(8,128)S(1)}, u32[]{:S(2)}, u32[]{:S(2)}) %collective-permute-start.1) | collective-permute-done | bytes 262176 | tf_op jit(solution)/shard_map/ppermute | solution.py:348
  24.5 4.0 %collective-permute-start.2 = (f32[2,128,256]{2,1,0:T(8,128)S(1)}, f32[2,128,256]{2,1,0:T(8,128)S(1)}, u32[]{:S(2)}, u32[]{:S(2)}) collective-permute-start(f32[2,128,256]{2,1,0:T(8,128)S(1)} %get-tuple-element.35.base), channel_id=1, source_target_pairs={{0,2},{1,3},{8,10},{9,11},{16,18},{17,19},{24,26},{25,27}} | collective-permute-start | bytes 786440 | tf_op jit(solution)/shard_map/ppermute | solution.py:351
  28.5 1.6 %collective-permute-start.5 = (f32[2,384,256]{2,1,0:T(8,128)S(1)}, f32[2,384,256]{2,1,0:T(8,128)S(1)}, u32[]{:S(2)}, u32[]{:S(2)}) collective-permute-start(f32[2,384,256]{2,1,0:T(8,128)S(1)} %get-tuple-element.38.late_mine), channel_id=1, source_target_pairs={{0,1},{1,0},{2,3},{3,2},{4,5},{5,4},{6,7},{7,6},{8,9},{9,8},{10,11... | collective-permute-start | bytes 2359304 | tf_op jit(solution)/shard_map/ppermute | solution.py:348
  30.1 2.3 %collective-permute-done.2.state = f32[2,128,256]{2,1,0:T(8,128)S(1)} collective-permute-done((f32[2,128,256]{2,1,0:T(8,128)S(1)}, f32[2,128,256]{2,1,0:T(8,128)S(1)}, u32[]{:S(2)}, u32[]{:S(2)}) %collective-permute-start.2) | collective-permute-done | bytes 262176 | tf_op jit(solution)/shard_map/ppermute | solution.py:351
  37.3 13.3 %collective-permute-done.5.late_theirs = f32[2,384,256]{2,1,0:T(8,128)S(1)} collective-permute-done((f32[2,384,256]{2,1,0:T(8,128)S(1)}, f32[2,384,256]{2,1,0:T(8,128)S(1)}, u32[]{:S(2)}, u32[]{:S(2)}) %collective-permute-start.5) | collective-permute-done | bytes 786464 | tf_op jit(solution)/shard_map/ppermute | solution.py:348
  50.6 2.2 %shard_map.60 = (f32[2,128,256]{2,1,0:T(8,128)S(1)}, f32[2,128,256]{2,1,0:T(8,128)S(1)}, f32[2,128,256]{2,1,0:T(8,128)S(1)}, f32[2,64,256]{2,1,0:T(8,128)S(1)}, f32[2,64,256]{2,1,0:T(8,128)S(1)}) custom-call(f32[2,128,256]{2,1,0:T(8,128)S(1)} %add.25.inflow, f32[2,256,256]{2,1,0:T(8,128)S(1)} %shard_map.55.ahead.mine.a_mine, ...), custom_call_target="tpu_custom_call" | custom-call | flops 805306368 | bytes 1048576 | tf_op jit(solution)/shard_map/pallas_call | solution.py:67
  55.4 1.4 %collective-permute-start.11 = (f32[2,64,256]{2,1,0:T(8,128)S(1)}, f32[2,64,256]{2,1,0:T(8,128)S(1)}, u32[]{:S(2)}, u32[]{:S(2)}) collective-permute-start(f32[2,64,256]{2,1,0:T(8,128)S(1)} %get-tuple-element.46), channel_id=1, source_target_pairs={{6,4},{7,5},{4,2},{5,3},{2,0},{3,1},{14,12},{15,13},{12,10},{13,11... | collective-permute-start | bytes 393224 | tf_op jit(solution)/shard_map/ppermute | solution.py:351
  56.8 1.3 %collective-permute-start.12 = (f32[2,64,256]{2,1,0:T(8,128)S(1)}, f32[2,64,256]{2,1,0:T(8,128)S(1)}, u32[]{:S(2)}, u32[]{:S(2)}) collective-permute-start(f32[2,64,256]{2,1,0:T(8,128)S(1)} %get-tuple-element.47), channel_id=1, source_target_pairs={{4,0},{5,1},{12,8},{13,9},{20,16},{21,17},{28,24},{29,25}} | collective-permute-start | bytes 393224 | tf_op jit(solution)/shard_map/ppermute | solution.py:351
  58.1 1.8 %collective-permute-start.7 = (f32[2,128,256]{2,1,0:T(8,128)S(1)}, f32[2,128,256]{2,1,0:T(8,128)S(1)}, u32[]{:S(2)}, u32[]{:S(2)}) collective-permute-start(f32[2,128,256]{2,1,0:T(8,128)S(1)} %get-tuple-element.41), channel_id=1, source_target_pairs={{0,1},{1,0},{2,3},{3,2},{4,5},{5,4},{6,7},{7,6},{8,9},{9,8},{10,11... | collective-permute-start | bytes 786440 | tf_op jit(solution)/shard_map/ppermute | solution.py:348
  59.9 12.1 %collective-permute-done.11.came = f32[2,64,256]{2,1,0:T(8,128)S(1)} collective-permute-done((f32[2,64,256]{2,1,0:T(8,128)S(1)}, f32[2,64,256]{2,1,0:T(8,128)S(1)}, u32[]{:S(2)}, u32[]{:S(2)}) %collective-permute-start.11) | collective-permute-done | bytes 131104 | tf_op jit(solution)/shard_map/ppermute | solution.py:351
  72.0 1.7 %collective-permute-done.12.last = f32[2,64,256]{2,1,0:T(8,128)S(1)} collective-permute-done((f32[2,64,256]{2,1,0:T(8,128)S(1)}, f32[2,64,256]{2,1,0:T(8,128)S(1)}, u32[]{:S(2)}, u32[]{:S(2)}) %collective-permute-start.12) | collective-permute-done | bytes 131104 | tf_op jit(solution)/shard_map/ppermute | solution.py:351
  74.4 1.6 %collective-permute-start.15 = (f32[2,128,256]{2,1,0:T(8,128)S(1)}, f32[2,128,256]{2,1,0:T(8,128)S(1)}, u32[]{:S(2)}, u32[]{:S(2)}) collective-permute-start(f32[2,128,256]{2,1,0:T(8,128)S(1)} %get-tuple-element.53), channel_id=1, source_target_pairs={{0,1},{1,0},{2,3},{3,2},{4,5},{5,4},{6,7},{7,6},{8,9},{9,8},{10,11... | collective-permute-start | bytes 786440 | tf_op jit(solution)/shard_map/ppermute | solution.py:348
  76.0 2.3 %shard_map.61 = (f32[2,2,128,256]{3,2,1,0:T(8,128)S(1)}, f32[2,2,128,256]{3,2,1,0:T(8,128)S(1)}) custom-call(f32[2,2,256,256]{3,2,1,0:T(8,128)S(1)} %get-tuple-element.32.states, f32[2,128,256]{2,1,0:T(8,128)S(1)} %get-tuple-element.40.in_own, f32[2,128,256]{2,1,0:T(8,128)S(1)} %collective-permute-done.7.in_theirs, f32[2,2,256,256]{3,2,1,0:T(8,128)S(1)} %bitcast.8), custom_call_target="tpu_custom_call" | custom-call | flops 805306368 | bytes 1048576 | tf_op jit(solution)/shard_map/pallas_call | solution.py:67
  78.9 2.0 %shard_map.65 = (f32[2,128,256]{2,1,0:T(8,128)S(1)}, f32[2,128,256]{2,1,0:T(8,128)S(1)}) custom-call(f32[2,2,128,256]{3,2,1,0:T(8,128)S(1)} %get-tuple-element.42.swept, f32[2,128,256]{2,1,0:T(8,128)S(1)} %get-tuple-element.49.entering, f32[2,2,256,256]{3,2,1,0:T(8,128)S(1)} %bitcast.4, f32[1,2]{1,0:T(1,128)S(1)} %copy-done.3), custom_call_target="tpu_custom_call" | custom-call | tf_op jit(solution)/shard_map/pallas_call | solution.py:420
  81.1 1.9 %shard_map.66 = (f32[2,128,256]{2,1,0:T(8,128)S(1)}, f32[2,128,256]{2,1,0:T(8,128)S(1)}) custom-call(f32[2,2,128,256]{3,2,1,0:T(8,128)S(1)} %get-tuple-element.52.swept, f32[2,128,256]{2,1,0:T(8,128)S(1)} %collective-permute-done.15.entering, f32[2,2,256,256]{3,2,1,0:T(8,128)S(1)} %bitcast.5, f32[1,2]{1,0:T(1,128)S(1)} %copy-done.3), custom_call_target="tpu_custom_call" | custom-call | tf_op jit(solution)/shard_map/pallas_call | solution.py:420
  83.5 1.5 %collective-permute-start.14 = (f32[2,128,256]{2,1,0:T(8,128)S(1)}, f32[2,128,256]{2,1,0:T(8,128)S(1)}, u32[]{:S(2)}, u32[]{:S(2)}) collective-permute-start(f32[2,128,256]{2,1,0:T(8,128)S(1)} %add.26.own), channel_id=1, source_target_pairs={{0,16},{8,24},{16,0},{24,8},{1,17},{9,25},{17,1},{25,9},{2,18},{10... | collective-permute-start | bytes 786440 | tf_op jit(solution)/shard_map/ppermute | solution.py:413
  86.2 6.6 %collective-permute-done.14.own_more = f32[2,128,256]{2,1,0:T(8,128)S(1)} collective-permute-done((f32[2,128,256]{2,1,0:T(8,128)S(1)}, f32[2,128,256]{2,1,0:T(8,128)S(1)}, u32[]{:S(2)}, u32[]{:S(2)}) %collective-permute-start.14) | collective-permute-done | bytes 262176 | tf_op jit(solution)/shard_map/ppermute | solution.py:413
  92.8 4.7 %collective-permute-done.17.theirs_more = f32[2,128,256]{2,1,0:T(8,128)S(1)} collective-permute-done((f32[2,128,256]{2,1,0:T(8,128)S(1)}, f32[2,128,256]{2,1,0:T(8,128)S(1)}, u32[]{:S(2)}, u32[]{:S(2)}) %collective-permute-start.17) | collective-permute-done | bytes 262176 | tf_op jit(solution)/shard_map/ppermute | solution.py:413
  98.3 1.3 %collective-permute-done.18 = f32[128,256]{1,0:T(8,128)S(1)} collective-permute-done((f32[128,256]{1,0:T(8,128)S(1)}, f32[128,256]{1,0:T(8,128)S(1)}, u32[]{:S(2)}, u32[]{:S(2)}) %collective-permute-start.18) | collective-permute-done | bytes 131104 | tf_op jit(solution)/shard_map/ppermute | solution.py:413
  99.6 1.4 %collective-permute-start.19 = (f32[128,256]{1,0:T(8,128)S(1)}, f32[128,256]{1,0:T(8,128)S(1)}, u32[]{:S(2)}, u32[]{:S(2)}) collective-permute-start(f32[128,256]{1,0:T(8,128)S(1)} %add.28), channel_id=1, source_target_pairs={{0,1},{1,0},{2,3},{3,2},{4,5},{5,4},{6,7},{7,6},{8,9},{9,8},{10,11... | collective-permute-start | bytes 393224 | tf_op jit(solution)/shard_map/ppermute | solution.py:442
  101.0 4.3 %collective-permute-done.19 = f32[128,256]{1,0:T(8,128)S(1)} collective-permute-done((f32[128,256]{1,0:T(8,128)S(1)}, f32[128,256]{1,0:T(8,128)S(1)}, u32[]{:S(2)}, u32[]{:S(2)}) %collective-permute-start.19) | collective-permute-done | bytes 131104 | tf_op jit(solution)/shard_map/ppermute | solution.py:442
  105.3 1.3 %collective-permute-start.20 = (f32[128,256]{1,0:T(8,128)S(1)}, f32[128,256]{1,0:T(8,128)S(1)}, u32[]{:S(2)}, u32[]{:S(2)}) collective-permute-start(f32[128,256]{1,0:T(8,128)S(1)} %add.29), channel_id=1, source_target_pairs={{0,2},{1,3},{2,0},{3,1},{4,6},{5,7},{6,4},{7,5},{8,10},{9,11},{10,... | collective-permute-start | bytes 393224 | tf_op jit(solution)/shard_map/ppermute | solution.py:442
  106.6 3.7 %collective-permute-done.20 = f32[128,256]{1,0:T(8,128)S(1)} collective-permute-done((f32[128,256]{1,0:T(8,128)S(1)}, f32[128,256]{1,0:T(8,128)S(1)}, u32[]{:S(2)}, u32[]{:S(2)}) %collective-permute-start.20) | collective-permute-done | bytes 131104 | tf_op jit(solution)/shard_map/ppermute | solution.py:442
  110.3 3.8 %collective-permute-start.21 = (f32[128,256]{1,0:T(8,128)S(1)}, f32[128,256]{1,0:T(8,128)S(1)}, u32[]{:S(2)}, u32[]{:S(2)}) collective-permute-start(f32[128,256]{1,0:T(8,128)S(1)} %add.30), channel_id=1, source_target_pairs={{0,4},{1,5},{2,6},{3,7},{4,0},{5,1},{6,2},{7,3},{8,12},{9,13},{10,... | collective-permute-start | bytes 393224 | tf_op jit(solution)/shard_map/ppermute | solution.py:442
  114.1 4.2 %collective-permute-done.21 = f32[128,256]{1,0:T(8,128)S(1)} collective-permute-done((f32[128,256]{1,0:T(8,128)S(1)}, f32[128,256]{1,0:T(8,128)S(1)}, u32[]{:S(2)}, u32[]{:S(2)}) %collective-permute-start.21) | collective-permute-done | bytes 131104 | tf_op jit(solution)/shard_map/ppermute | solution.py:442
  118.4 1.3 %collective-permute-done.22.theirs = f32[128,256]{1,0:T(8,128)S(1)} collective-permute-done((f32[128,256]{1,0:T(8,128)S(1)}, f32[128,256]{1,0:T(8,128)S(1)}, u32[]{:S(2)}, u32[]{:S(2)}) %collective-permute-start.22) | collective-permute-done | bytes 131104 | tf_op jit(solution)/shard_map/ppermute | solution.py:413
  119.8 3.2 %shard_map.68 = f32[2,64,512]{2,1,0:T(8,128)} custom-call(f32[128,256]{1,0:T(8,128)S(1)} %add.31.mine, f32[128,256]{1,0:T(8,128)S(1)} %collective-permute-done.22.theirs, f32[2,256,256]{2,1,0:T(8,128)S(1)} %get-tuple-element.58.q_mine, f32[2,256,256]{2,1,0:T(8,128)S(1)} %collective-permute-done.23.q_theirs), custom_call_target="tpu_custom_call" | custom-call | flops 1610612736 | bytes 1048576 | tf_op jit(solution)/shard_map/pallas_call | solution.py:333
  (50 shorter events, 14.5 us)
Async XLA Ops:
  0.0 5.0 %copy-start = (f32[1,2,2,256,256]{4,3,2,1,0:T(8,128)S(1)}, f32[1,2,2,256,256]{4,3,2,1,0:T(8,128)}, u32[]{:S(2)}) copy-start(f32[1,2,2,256,256]{4,3,2,1,0:T(8,128)} %param.8) | copy-start | bytes 3145732
  0.0 1.3 %copy-start.1 = (f32[1,2,2,256,256]{4,3,2,1,0:T(8,128)S(1)}, f32[1,2,2,256,256]{4,3,2,1,0:T(8,128)}, u32[]{:S(2)}) copy-start(f32[1,2,2,256,256]{4,3,2,1,0:T(8,128)} %param.7) | copy-start | bytes 3145732
  1.9 21.4 %collective-permute-start = (f32[2,256,256]{2,1,0:T(8,128)S(1)}, f32[2,256,256]{2,1,0:T(8,128)S(1)}, u32[]{:S(2)}, u32[]{:S(2)}) collective-permute-start(f32[2,256,256]{2,1,0:T(8,128)S(1)} %shard_map.55.ahead.mine.a_mine), channel_id=1, source_target_pairs={{0,1},{1,0},{2,3},{3,2},{4,5},{5,4},{6,7},{7,6},{8,9},{9,8},{10,11... | collective-permute-start | bytes 1572872 | tf_op jit(solution)/shard_map/ppermute | solution.py:348
  5.0 1.2 copy-start.4
  6.2 1.2 copy-start.5
  10.4 12.9 %collective-permute-start.1 = (f32[2,128,256]{2,1,0:T(8,128)S(1)}, f32[2,128,256]{2,1,0:T(8,128)S(1)}, u32[]{:S(2)}, u32[]{:S(2)}) collective-permute-start(f32[2,128,256]{2,1,0:T(8,128)S(1)} %get-tuple-element.34), channel_id=1, source_target_pairs={{0,1},{1,0},{2,3},{3,2},{4,5},{5,4},{6,7},{7,6},{8,9},{9,8},{10,11... | collective-permute-start | bytes 786440 | tf_op jit(solution)/shard_map/ppermute | solution.py:348
  10.5 24.1 %collective-permute-start.6 = (f32[2,256,256]{2,1,0:T(8,128)S(1)}, f32[2,256,256]{2,1,0:T(8,128)S(1)}, u32[]{:S(2)}, u32[]{:S(2)}) collective-permute-start(f32[2,256,256]{2,1,0:T(8,128)S(1)} %get-tuple-element.39.c_mine.mine), channel_id=1, source_target_pairs={{0,1},{1,0},{2,3},{3,2},{4,5},{5,4},{6,7},{7,6},{8,9},{9,8},{10,11... | collective-permute-start | bytes 1572872 | tf_op jit(solution)/shard_map/ppermute | solution.py:348
  24.5 7.9 %collective-permute-start.2 = (f32[2,128,256]{2,1,0:T(8,128)S(1)}, f32[2,128,256]{2,1,0:T(8,128)S(1)}, u32[]{:S(2)}, u32[]{:S(2)}) collective-permute-start(f32[2,128,256]{2,1,0:T(8,128)S(1)} %get-tuple-element.35.base), channel_id=1, source_target_pairs={{0,2},{1,3},{8,10},{9,11},{16,18},{17,19},{24,26},{25,27}} | collective-permute-start | bytes 786440 | tf_op jit(solution)/shard_map/ppermute | solution.py:351
  28.5 22.1 %collective-permute-start.5 = (f32[2,384,256]{2,1,0:T(8,128)S(1)}, f32[2,384,256]{2,1,0:T(8,128)S(1)}, u32[]{:S(2)}, u32[]{:S(2)}) collective-permute-start(f32[2,384,256]{2,1,0:T(8,128)S(1)} %get-tuple-element.38.late_mine), channel_id=1, source_target_pairs={{0,1},{1,0},{2,3},{3,2},{4,5},{5,4},{6,7},{7,6},{8,9},{9,8},{10,11... | collective-permute-start | bytes 2359304 | tf_op jit(solution)/shard_map/ppermute | solution.py:348
  33.0 2.9 %collective-permute-start.3 = (f32[2,128,256]{2,1,0:T(8,128)S(1)}, f32[2,128,256]{2,1,0:T(8,128)S(1)}, u32[]{:S(2)}, u32[]{:S(2)}) collective-permute-start(f32[2,128,256]{2,1,0:T(8,128)S(1)} %shard_map.58), channel_id=1, source_target_pairs={{2,4},{3,5},{10,12},{11,13},{18,20},{19,21},{26,28},{27,29}} | collective-permute-start | bytes 786440 | tf_op jit(solution)/shard_map/ppermute | solution.py:351
  35.2 19.0 %collective-permute-start.10 = (f32[2,256,256]{2,1,0:T(8,128)S(1)}, f32[2,256,256]{2,1,0:T(8,128)S(1)}, u32[]{:S(2)}, u32[]{:S(2)}) collective-permute-start(f32[2,256,256]{2,1,0:T(8,128)S(1)} %shard_map.62.c_mine), channel_id=1, source_target_pairs={{2,4},{3,5},{4,2},{5,3},{10,12},{11,13},{12,10},{13,11},{18,20},{1... | collective-permute-start | bytes 1572872 | tf_op jit(solution)/shard_map/ppermute | solution.py:351
  36.6 0.7 collective-permute-start.4
  52.8 1.4 %collective-permute-start.8 = (f32[2,64,256]{2,1,0:T(8,128)S(1)}, f32[2,64,256]{2,1,0:T(8,128)S(1)}, u32[]{:S(2)}, u32[]{:S(2)}) collective-permute-start(f32[2,64,256]{2,1,0:T(8,128)S(1)} %get-tuple-element.43.mine_a), channel_id=1, source_target_pairs={{6,4},{7,5},{4,2},{5,3},{14,12},{15,13},{12,10},{13,11},{22,20},{2... | collective-permute-start | bytes 393224 | tf_op jit(solution)/shard_map/ppermute | solution.py:351
  53.5 0.7 collective-permute-start.9
  55.4 20.6 %copy-start.2 = (f32[1,2,2,256,256]{4,3,2,1,0:T(8,128)S(1)}, f32[1,2,2,256,256]{4,3,2,1,0:T(8,128)}, u32[]{:S(2)}) copy-start(f32[1,2,2,256,256]{4,3,2,1,0:T(8,128)} %param.7) | copy-start | bytes 3145732
  55.4 16.6 %collective-permute-start.11 = (f32[2,64,256]{2,1,0:T(8,128)S(1)}, f32[2,64,256]{2,1,0:T(8,128)S(1)}, u32[]{:S(2)}, u32[]{:S(2)}) collective-permute-start(f32[2,64,256]{2,1,0:T(8,128)S(1)} %get-tuple-element.46), channel_id=1, source_target_pairs={{6,4},{7,5},{4,2},{5,3},{2,0},{3,1},{14,12},{15,13},{12,10},{13,11... | collective-permute-start | bytes 393224 | tf_op jit(solution)/shard_map/ppermute | solution.py:351
  56.8 16.9 %collective-permute-start.12 = (f32[2,64,256]{2,1,0:T(8,128)S(1)}, f32[2,64,256]{2,1,0:T(8,128)S(1)}, u32[]{:S(2)}, u32[]{:S(2)}) collective-permute-start(f32[2,64,256]{2,1,0:T(8,128)S(1)} %get-tuple-element.47), channel_id=1, source_target_pairs={{4,0},{5,1},{12,8},{13,9},{20,16},{21,17},{28,24},{29,25}} | collective-permute-start | bytes 393224 | tf_op jit(solution)/shard_map/ppermute | solution.py:351
  58.1 17.9 %collective-permute-start.7 = (f32[2,128,256]{2,1,0:T(8,128)S(1)}, f32[2,128,256]{2,1,0:T(8,128)S(1)}, u32[]{:S(2)}, u32[]{:S(2)}) collective-permute-start(f32[2,128,256]{2,1,0:T(8,128)S(1)} %get-tuple-element.41), channel_id=1, source_target_pairs={{0,1},{1,0},{2,3},{3,2},{4,5},{5,4},{6,7},{7,6},{8,9},{9,8},{10,11... | collective-permute-start | bytes 786440 | tf_op jit(solution)/shard_map/ppermute | solution.py:348
  74.4 6.7 %collective-permute-start.15 = (f32[2,128,256]{2,1,0:T(8,128)S(1)}, f32[2,128,256]{2,1,0:T(8,128)S(1)}, u32[]{:S(2)}, u32[]{:S(2)}) collective-permute-start(f32[2,128,256]{2,1,0:T(8,128)S(1)} %get-tuple-element.53), channel_id=1, source_target_pairs={{0,1},{1,0},{2,3},{3,2},{4,5},{5,4},{6,7},{7,6},{8,9},{9,8},{10,11... | collective-permute-start | bytes 786440 | tf_op jit(solution)/shard_map/ppermute | solution.py:348
  78.3 0.7 copy-start.3
  81.0 2.5 %collective-permute-start.13 = (f32[2,128,256]{2,1,0:T(8,128)S(1)}, f32[2,128,256]{2,1,0:T(8,128)S(1)}, u32[]{:S(2)}, u32[]{:S(2)}) collective-permute-start(f32[2,128,256]{2,1,0:T(8,128)S(1)} %get-tuple-element.51), channel_id=1, source_target_pairs={{0,8},{8,0},{16,24},{24,16},{1,9},{9,1},{17,25},{25,17},{2,10},{10... | collective-permute-start | bytes 786440 | tf_op jit(solution)/shard_map/ppermute | solution.py:413
  82.9 2.1 %collective-permute-start.16 = (f32[2,128,256]{2,1,0:T(8,128)S(1)}, f32[2,128,256]{2,1,0:T(8,128)S(1)}, u32[]{:S(2)}, u32[]{:S(2)}) collective-permute-start(f32[2,128,256]{2,1,0:T(8,128)S(1)} %get-tuple-element.55), channel_id=1, source_target_pairs={{0,8},{8,0},{16,24},{24,16},{1,9},{9,1},{17,25},{25,17},{2,10},{10... | collective-permute-start | bytes 786440 | tf_op jit(solution)/shard_map/ppermute | solution.py:413
  83.5 9.2 %collective-permute-start.14 = (f32[2,128,256]{2,1,0:T(8,128)S(1)}, f32[2,128,256]{2,1,0:T(8,128)S(1)}, u32[]{:S(2)}, u32[]{:S(2)}) collective-permute-start(f32[2,128,256]{2,1,0:T(8,128)S(1)} %add.26.own), channel_id=1, source_target_pairs={{0,16},{8,24},{16,0},{24,8},{1,17},{9,25},{17,1},{25,9},{2,18},{10... | collective-permute-start | bytes 786440 | tf_op jit(solution)/shard_map/ppermute | solution.py:413
  85.1 12.3 %collective-permute-start.17 = (f32[2,128,256]{2,1,0:T(8,128)S(1)}, f32[2,128,256]{2,1,0:T(8,128)S(1)}, u32[]{:S(2)}, u32[]{:S(2)}) collective-permute-start(f32[2,128,256]{2,1,0:T(8,128)S(1)} %add.27.theirs), channel_id=1, source_target_pairs={{0,16},{8,24},{16,0},{24,8},{1,17},{9,25},{17,1},{25,9},{2,18},{10... | collective-permute-start | bytes 786440 | tf_op jit(solution)/shard_map/ppermute | solution.py:413
  98.2 1.4 %collective-permute-start.18 = (f32[128,256]{1,0:T(8,128)S(1)}, f32[128,256]{1,0:T(8,128)S(1)}, u32[]{:S(2)}, u32[]{:S(2)}) collective-permute-start(f32[128,256]{1,0:T(8,128)S(1)} %get-tuple-element.57), channel_id=1, source_target_pairs={{0,8},{8,0},{16,24},{24,16},{1,9},{9,1},{17,25},{25,17},{2,10},{10... | collective-permute-start | bytes 393224 | tf_op jit(solution)/shard_map/ppermute | solution.py:413
  99.6 5.6 %collective-permute-start.19 = (f32[128,256]{1,0:T(8,128)S(1)}, f32[128,256]{1,0:T(8,128)S(1)}, u32[]{:S(2)}, u32[]{:S(2)}) collective-permute-start(f32[128,256]{1,0:T(8,128)S(1)} %add.28), channel_id=1, source_target_pairs={{0,1},{1,0},{2,3},{3,2},{4,5},{5,4},{6,7},{7,6},{8,9},{9,8},{10,11... | collective-permute-start | bytes 393224 | tf_op jit(solution)/shard_map/ppermute | solution.py:442
  101.0 17.4 %collective-permute-start.23 = (f32[2,256,256]{2,1,0:T(8,128)S(1)}, f32[2,256,256]{2,1,0:T(8,128)S(1)}, u32[]{:S(2)}, u32[]{:S(2)}) collective-permute-start(f32[2,256,256]{2,1,0:T(8,128)S(1)} %get-tuple-element.58.q_mine), channel_id=1, source_target_pairs={{0,8},{8,0},{16,24},{24,16},{1,9},{9,1},{17,25},{25,17},{2,10},{10... | collective-permute-start | bytes 1572872 | tf_op jit(solution)/shard_map/ppermute | solution.py:413
  105.3 5.0 %collective-permute-start.20 = (f32[128,256]{1,0:T(8,128)S(1)}, f32[128,256]{1,0:T(8,128)S(1)}, u32[]{:S(2)}, u32[]{:S(2)}) collective-permute-start(f32[128,256]{1,0:T(8,128)S(1)} %add.29), channel_id=1, source_target_pairs={{0,2},{1,3},{2,0},{3,1},{4,6},{5,7},{6,4},{7,5},{8,10},{9,11},{10,... | collective-permute-start | bytes 393224 | tf_op jit(solution)/shard_map/ppermute | solution.py:442
  110.3 8.0 %collective-permute-start.21 = (f32[128,256]{1,0:T(8,128)S(1)}, f32[128,256]{1,0:T(8,128)S(1)}, u32[]{:S(2)}, u32[]{:S(2)}) collective-permute-start(f32[128,256]{1,0:T(8,128)S(1)} %add.30), channel_id=1, source_target_pairs={{0,4},{1,5},{2,6},{3,7},{4,0},{5,1},{6,2},{7,3},{8,12},{9,13},{10,... | collective-permute-start | bytes 393224 | tf_op jit(solution)/shard_map/ppermute | solution.py:442
  118.3 1.4 %collective-permute-start.22 = (f32[128,256]{1,0:T(8,128)S(1)}, f32[128,256]{1,0:T(8,128)S(1)}, u32[]{:S(2)}, u32[]{:S(2)}) collective-permute-start(f32[128,256]{1,0:T(8,128)S(1)} %add.31.mine), channel_id=1, source_target_pairs={{0,8},{8,0},{16,24},{24,16},{1,9},{9,1},{17,25},{25,17},{2,10},{10... | collective-permute-start | bytes 393224 | tf_op jit(solution)/shard_map/ppermute | solution.py:413

commit v4 on v3

--- a/solution.py
+++ b/solution.py
@@ -8,19 +8,49 @@
 from jax.sharding import PartitionSpec as P
 
 
-NS_ITERS = 2
 GRANT = 8 << 20
+LANES = 128
 HIGH = lax.Precision.HIGH
 F32 = jnp.float32
 
 
-def dot(a, b, dims):
-    return lax.dot_general(a, b, (dims, ((), ())), precision=HIGH, preferred_element_type=F32)
+def dot(a, b, dims, precision=None):
+    return lax.dot_general(
+        a, b, (dims, ((), ())), precision=precision, preferred_element_type=F32
+    )
+
+
+def halves(a):
+    high = a.astype(jnp.bfloat16)
+    return high, (a - high.astype(F32)).astype(jnp.bfloat16)
+
+
+def stacked(value):
+    real, imag = halves(value[0]), halves(value[1])
+    high = jnp.concatenate([real[0], imag[0]], axis=0)
+    return high, jnp.concatenate([high, real[1], imag[1]], axis=0)
+
+
+def against(left, part, dims):
+    high, both = left
+    size = high.shape[0]
+    wide = dot(both, part[0], dims)
+    value = wide[:size] + (wide[size:] + dot(high, part[1], dims))
+    return value[: size // 2], value[size // 2 :]
+
+
+def few(left, parts, dims):
+    left = stacked(left)
+    with_real, with_imag = against(left, parts[0], dims), against(left, parts[1], dims)
+    return with_real[0] - with_imag[1], with_imag[0] + with_real[1]
 
 
 def times(left, right, dims):
-    real = dot(left[0], right[0], dims) - dot(left[1], right[1], dims)
-    imag = dot(left[0], right[1], dims) + dot(left[1], right[0], dims)
+    rows = left[0].shape[0]
+    if rows <= LANES // 2 or (rows <= LANES and dims[1] == (1,)):
+        return few(left, (halves(right[0]), halves(right[1])), dims)
+    real = dot(left[0], right[0], dims, HIGH) - dot(left[1], right[1], dims, HIGH)
+    imag = dot(left[0], right[1], dims, HIGH) + dot(left[1], right[0], dims, HIGH)
     return real, imag
 
 
@@ -156,17 +186,21 @@
     put(out, plus(trans(pair(state), pair(matrix)), pair(base)))
 
 
-def turn_kernel(inflow, a_mine, a_theirs, b_mine, b_theirs, g_mine, late_mine, late_theirs,
-                c_mine, c_theirs, in_own, in_other, mid, *outs):
+def enter_kernel(inflow, a_mine, a_theirs, b_mine, b_theirs, in_own, in_other):
     first = side()
-    size = a_mine.shape[1]
-    half = inflow.shape[1]
     entering = pair(inflow)
     a_first = pick(first, pair(a_mine), pair(a_theirs))
-    b_first = pick(first, pair(b_mine), pair(b_theirs))
-    second = plus(trans(entering, a_first), b_first)
+    second = plus(trans(entering, a_first), pick(first, pair(b_mine), pair(b_theirs)))
     put(in_own, pick(first, entering, second))
     put(in_other, pick(first, second, entering))
+
+
+def turn_kernel(in_own, in_other, g_mine, late_mine, late_theirs, c_mine, c_theirs, mid, *outs):
+    first = side()
+    size = c_mine.shape[1]
+    half = in_own.shape[1]
+    entering = pick(first, pair(in_own), pair(in_other))
+    second = pick(first, pair(in_other), pair(in_own))
     r_mine, r_theirs = part_of(late_mine, 0, size), part_of(late_theirs, 0, size)
     g_own, g_theirs = pair(g_mine), part_of(late_theirs, size, half)
     middle = plus(pick(first, g_theirs, g_own), trans(second, pick(first, r_theirs, r_mine)))
@@ -223,7 +257,7 @@
     back_in(pair(work), mid, c_mine, c_theirs, own, other)
 
 
-def swept_kernel(states, in_own, in_theirs, lower, out_own, out_theirs):
+def swept_kernel(states, in_own, in_theirs, lower, upper, out_own, out_theirs):
     count = states.shape[0]
     half = in_own.shape[1]
     mine = jnp.where(side(), 0, half)
@@ -239,21 +273,19 @@
     wreal, wimag = weights[0, 0], weights[0, 1]
     carry = pair(entering)
     upward = lax.rem(lax.axis_index("pole"), 2) == 1
+    values = [None] * count
     for number in range(count - 1, -1, -1):
         carry = minus(pair(swept, number), trans(carry, pair(upper, number)))
-        value = (wreal * carry[0] - wimag * carry[1], wreal * carry[1] + wimag * carry[0])
-        kept = upward if number >= count // 2 else jnp.logical_not(upward)
-        columns = slice((number % (count // 2)) * width, (number % (count // 2) + 1) * width)
-
-        @pl.when(kept)
-        def _():
-            for part in range(2):
-                keep[part, :, columns] = value[part]
-
-        @pl.when(jnp.logical_not(kept))
-        def _():
-            for part in range(2):
-                send[part, :, columns] = value[part]
+        values[number] = (
+            wreal * carry[0] - wimag * carry[1], wreal * carry[1] + wimag * carry[0]
+        )
+    blocks = count // 2
+    for number in range(blocks):
+        columns = slice(number * width, (number + 1) * width)
+        for part in range(2):
+            low, high = values[number][part], values[number + blocks][part]
+            keep[part, :, columns] = jnp.where(upward, high, low)
+            send[part, :, columns] = jnp.where(upward, low, high)
 
 
 def gram_kernel(own, own_more, theirs, theirs_more, total, keep, send, work):
@@ -266,8 +298,8 @@
             total[part, pl.ds(start, half), :] = first[part] + second[part]
     basis = pair(total)
     dims = ((1,), (1,))
-    real = dot(basis[0], basis[0], dims) + dot(basis[1], basis[1], dims)
-    imag = dot(basis[0], basis[1], dims) - dot(basis[1], basis[0], dims)
+    real = dot(basis[0], basis[0], dims, HIGH) + dot(basis[1], basis[1], dims, HIGH)
+    imag = dot(basis[0], basis[1], dims, HIGH) - dot(basis[1], basis[0], dims, HIGH)
     row = lax.broadcasted_iota(jnp.int32, (size, size), 0)
     column = lax.broadcasted_iota(jnp.int32, (size, size), 1)
     work[...] = jnp.where(row <= column, real, imag)
@@ -276,9 +308,16 @@
     send[...] = work[pl.ds(pl.multiple_of(half - start, half), half), :]
 
 
-def finish_kernel(states, mine, theirs, q_mine, q_theirs, out, held, slab):
+def parts_kernel(mine, theirs, high, low):
+    for number, piece in enumerate((mine, theirs)):
+        for part in range(2):
+            high[number, part], low[number, part] = halves(piece[part])
+
+
+def finish_kernel(states, mine, theirs, q_high, q_low, out, held, slab):
     size = held.shape[0]
     half = size // 2
+    columns = out.shape[1]
     pole = lax.axis_index("pole")
     start = pl.multiple_of(lax.rem(pole, 2) * half, half)
     held[pl.ds(start, half), :] = mine[...]
@@ -290,28 +329,26 @@
     real = jnp.where(row <= column, packed, turned)
     imag = jnp.where(row < column, turned, jnp.where(row > column, -packed, 0.0))
     frob = jnp.sqrt(jnp.sum(real * real + imag * imag, keepdims=True))
-    current = (real / frob, imag / frob)
-    eye = jnp.where(row == column, 1.0, 0.0)
-    columns = out.shape[1]
-    inverse = None
-    for sweep in range(NS_ITERS):
-        both = current if inverse is None else plain(inverse, current)
-        factor = (1.5 * eye - 0.5 * both[0], -0.5 * both[1])
-        if sweep < NS_ITERS - 1:
-            current = plain(current, factor)
-            inverse = factor if inverse is None else plain(factor, inverse)
-        else:
-            put(slab, factor)
-            place = pl.multiple_of(pole * columns, columns)
-            mixing = (slab[0, pl.ds(place, columns), :], slab[1, pl.ds(place, columns), :])
-            if inverse is not None:
-                mixing = plain(mixing, inverse)
+    scale = 1.0 / frob
+    current = (real * scale, imag * scale)
+    put(slab, current)
+    factor = (jnp.where(row == column, 1.5, 0.0) - 0.5 * current[0], -0.5 * current[1])
+    factor = (halves(factor[0]), halves(factor[1]))
+    dims = ((1,), (0,))
+    place = pl.multiple_of(pole * columns, columns)
+    strip = (slab[0, pl.ds(place, columns), :], slab[1, pl.ds(place, columns), :])
+    strip = few(few(strip, factor, dims), factor, dims)
+    on = lax.broadcasted_iota(jnp.int32, strip[0].shape, 0) + place
+    on = on == lax.broadcasted_iota(jnp.int32, strip[0].shape, 1)
+    strip = (jnp.where(on, 1.5, 0.0) - 0.5 * strip[0], -0.5 * strip[1])
+    mixing = few(strip, factor, dims)
     factor = jnp.sqrt(states / frob)
     mixing = (mixing[0] * factor, mixing[1] * factor)
-    width = q_mine.shape[2]
+    width = q_high.shape[3]
     place = lax.rem(pole, 2) * width
-    for piece, offset in ((q_mine, place), (q_theirs, width - place)):
-        value = plain(mixing, pair(piece))
+    for number, offset in enumerate((place, width - place)):
+        parts = tuple((q_high[number, part], q_low[number, part]) for part in range(2))
+        value = few(mixing, parts, dims)
         for part in range(2):
             out[part, :, pl.ds(pl.multiple_of(offset, width), width)] = value[part]
 
@@ -379,9 +416,11 @@
     (c_node,) = call(join_back_kernel, [square], c_mine, c_theirs)
     quarter = (2, half // 2, width)
     short = nodes == 4
-    in_own, in_other, mid, *ends = call(
-        turn_kernel, [strip] * 3 + ([quarter] * 2 if short else [strip]), inflow, a_mine, a_theirs,
-        b_mine, b_theirs, g_mine, late_mine, late_theirs, c_mine, c_theirs, products=2,
+    in_own, in_other = call(enter_kernel, [strip] * 2, inflow, a_mine, a_theirs, b_mine, b_theirs)
+    in_theirs = beside(in_other)
+    mid, *ends = call(
+        turn_kernel, [strip] + ([quarter] * 2 if short else [strip]), in_own, in_other,
+        g_mine, late_mine, late_theirs, c_mine, c_theirs, products=2,
     )
     if short:
         c_other = between(c_node, [(1, 2), (2, 1)])
@@ -394,9 +433,8 @@
         last = between(last, [(2, 0)])
     else:
         back_inflow = prefix(ends[0], c_node, order[::-1])
-    in_theirs = beside(in_other)
     swept_own, swept_theirs = call(
-        swept_kernel, [(count,) + strip] * 2, states, in_own, in_theirs, lower,
+        swept_kernel, [(count,) + strip] * 2, states, in_own, in_theirs, lower, upper,
         products=count,
     )
     if short:
@@ -439,15 +477,23 @@
     )
     packed = packed + over_poles(packed_send, 0)
     for bit in range(devices.bit_length() - 1):
+        mask = (2 << bit) - 2 if bit else 1
         packed = packed + lax.ppermute(
-            packed, "rows", [(place, place ^ (1 << bit)) for place in range(devices)]
+            packed, "rows", [(place, place ^ mask) for place in range(devices)]
         )
     packed_theirs = over_poles(packed, 0)
     total_theirs = over_poles(total, 0)
+    q_high, q_low = pl.pallas_call(
+        parts_kernel,
+        out_shape=[jax.ShapeDtypeStruct((2,) + total.shape, jnp.bfloat16)] * 2,
+        in_specs=[pl.BlockSpec(memory_space=vmem)] * 2,
+        out_specs=[pl.BlockSpec(memory_space=vmem)] * 2,
+        compiler_params=pltpu.CompilerParams(vmem_limit_bytes=GRANT),
+    )(total, total_theirs)
     (result,) = scratch(
         functools.partial(finish_kernel, float(columns * devices)),
         [(2, vectors // poles, columns)], [(vectors, vectors), state],
-        packed, packed_theirs, total, total_theirs, products=4,
+        packed, packed_theirs, q_high, q_low, products=4,
     )
     return result
 

time: 123 us -> 119 us (0.967)
  Pallas kernels: 20.7 us -> 16.6 us
    pallas_call x8 -> x9, Pallas kernels: 9.21 us -> 6.65 us  [call(): pl.pallas_call(body, out_shape=shapes, in_specs=[pl.BlockSpec(memory_spac...]
  transfers between devices with their start and end apart: 24 -> 24, of which waited for: 13 -> 14; matrix products, arithmetic and copies ran while one was open for 0% -> 0% of each run, Pallas kernels for 12% -> 10%
where the time goes in v4:
time: 119 us
  waiting for transfers between devices  68.3 us (57%)
  starting transfers between devices  28.9 us (24%)
  Pallas kernels  16.6 us (14%)
  local copies, waits for them, and re-layouts  4.42 us (4%)
    ppermute x6, waiting for transfers between devices, beside(): return lax.ppermute(value, 'rows', swap)  26.2 us
    ppermute x8, waiting for transfers between devices, between(): lax.ppermute(value, 'rows', [(2 * a + s, 2 * b + s) for a, b in moves for...  15.9 us
    ppermute x7, waiting for transfers between devices, over_poles(): lax.ppermute(value, 'pole', [(place, place ^ 1 << bit) for place in range...  13.8 us
    ppermute x3, waiting for transfers between devices, shards(): lax.ppermute(packed, 'rows', [(place, place ^ mask) for place in range(de...  12.4 us
    ppermute x8, starting transfers between devices, between(): lax.ppermute(value, 'rows', [(2 * a + s, 2 * b + s) for a, b in moves for...  10.3 us
    ppermute x6, starting transfers between devices, beside(): return lax.ppermute(value, 'rows', swap)  10.1 us
    pallas_call x9, Pallas kernels, call(): pl.pallas_call(body, out_shape=shapes, in_specs=[pl.BlockSpec(memory_spac...  6.65 us
    pallas_call x4, Pallas kernels, scratch(): pl.pallas_call(body, out_shape=[jax.ShapeDtypeStruct(shape, F32) for shap...  6.54 us
  transfers between devices with their start and end apart: 24, of which 14 were waited for; matrix products, arithmetic and copies ran while one was open for 0% of the time, Pallas kernels for 10%

profile of v4, /device:TPU:0, one launch (start us, length us, event | category | flops | bytes accessed | tf_op | source)
XLA Modules:
  0.0 118.9 jit_solution(12076170006439417658)
XLA Ops:
  0.0 1.3 %copy-done.1 = f32[1,2,2,256,256]{4,3,2,1,0:T(8,128)S(1)} copy-done((f32[1,2,2,256,256]{4,3,2,1,0:T(8,128)S(1)}, f32[1,2,2,256,256]{4,3,2,1,0:T(8,128)}, u32[]{:S(2)}) %copy-start.1) | copy-done | bytes 1048600
  1.9 3.0 %collective-permute-start = (f32[2,256,256]{2,1,0:T(8,128)S(1)}, f32[2,256,256]{2,1,0:T(8,128)S(1)}, u32[]{:S(2)}, u32[]{:S(2)}) collective-permute-start(f32[2,256,256]{2,1,0:T(8,128)S(1)} %shard_map.55.ahead.mine.a_mine), channel_id=1, source_target_pairs={{0,1},{1,0},{2,3},{3,2},{4,5},{5,4},{6,7},{7,6},{8,9},{9,8},{10,11... | collective-permute-start | bytes 1572872 | tf_op jit(solution)/shard_map/ppermute | solution.py:385
  5.0 1.2 %copy-done.4 = f32[2,256,512]{2,1,0:T(8,128)S(1)} copy-done((f32[2,256,512]{2,1,0:T(8,128)S(1)}, f32[2,256,512]{2,1,0:T(8,128)}, u32[]{:S(2)}) %copy-start.4) | copy-done | bytes 1048600
  6.2 1.2 %copy-done.5 = f32[1,2,2,256,256]{4,3,2,1,0:T(8,128)S(1)} copy-done((f32[1,2,2,256,256]{4,3,2,1,0:T(8,128)S(1)}, f32[1,2,2,256,256]{4,3,2,1,0:T(8,128)}, u32[]{:S(2)}) %copy-start.5) | copy-done | bytes 1048600
  7.4 3.0 %shard_map.56 = (f32[2,2,256,256]{3,2,1,0:T(8,128)S(1)}, f32[2,128,256]{2,1,0:T(8,128)S(1)}, f32[2,128,256]{2,1,0:T(8,128)S(1)}, f32[2,128,256]{2,1,0:T(8,128)S(...) custom-call(f32[2,256,512]{2,1,0:T(8,128)S(1)} %copy-done.4, f32[2,2,256,256]{3,2,1,0:T(8,128)S(1)} %bitcast.10, ...), custom_call_target="tpu_custom_call" | custom-call | flops 2818572288 | bytes 1048576 | tf_op jit(solution)/shard_map/pallas_call | solution.py:370
  10.5 2.0 %collective-permute-start.7 = (f32[2,256,256]{2,1,0:T(8,128)S(1)}, f32[2,256,256]{2,1,0:T(8,128)S(1)}, u32[]{:S(2)}, u32[]{:S(2)}) collective-permute-start(f32[2,256,256]{2,1,0:T(8,128)S(1)} %get-tuple-element.44.c_mine.mine), channel_id=1, source_target_pairs={{0,1},{1,0},{2,3},{3,2},{4,5},{5,4},{6,7},{7,6},{8,9},{9,8},{10,11... | collective-permute-start | bytes 1572872 | tf_op jit(solution)/shard_map/ppermute | solution.py:385
  12.5 10.8 %collective-permute-done.1.btheirs.b_theirs = f32[2,128,256]{2,1,0:T(8,128)S(1)} collective-permute-done((f32[2,128,256]{2,1,0:T(8,128)S(1)}, f32[2,128,256]{2,1,0:T(8,128)S(1)}, u32[]{:S(2)}, u32[]{:S(2)}) %collective-permute-start.1) | collective-permute-done | bytes 262176 | tf_op jit(solution)/shard_map/ppermute | solution.py:385
  24.2 4.0 %collective-permute-start.2 = (f32[2,128,256]{2,1,0:T(8,128)S(1)}, f32[2,128,256]{2,1,0:T(8,128)S(1)}, u32[]{:S(2)}, u32[]{:S(2)}) collective-permute-start(f32[2,128,256]{2,1,0:T(8,128)S(1)} %get-tuple-element.37.base), channel_id=1, source_target_pairs={{0,2},{1,3},{8,10},{9,11},{16,18},{17,19},{24,26},{25,27}} | collective-permute-start | bytes 786440 | tf_op jit(solution)/shard_map/ppermute | solution.py:388
  28.2 1.6 %collective-permute-start.6 = (f32[2,384,256]{2,1,0:T(8,128)S(1)}, f32[2,384,256]{2,1,0:T(8,128)S(1)}, u32[]{:S(2)}, u32[]{:S(2)}) collective-permute-start(f32[2,384,256]{2,1,0:T(8,128)S(1)} %get-tuple-element.43.late_mine), channel_id=1, source_target_pairs={{0,1},{1,0},{2,3},{3,2},{4,5},{5,4},{6,7},{7,6},{8,9},{9,8},{10,11... | collective-permute-start | bytes 2359304 | tf_op jit(solution)/shard_map/ppermute | solution.py:385
  29.8 2.3 %collective-permute-done.2.state = f32[2,128,256]{2,1,0:T(8,128)S(1)} collective-permute-done((f32[2,128,256]{2,1,0:T(8,128)S(1)}, f32[2,128,256]{2,1,0:T(8,128)S(1)}, u32[]{:S(2)}, u32[]{:S(2)}) %collective-permute-start.2) | collective-permute-done | bytes 262176 | tf_op jit(solution)/shard_map/ppermute | solution.py:388
  33.1 1.4 %collective-permute-done.7.c_theirs.theirs = f32[2,256,256]{2,1,0:T(8,128)S(1)} collective-permute-done((f32[2,256,256]{2,1,0:T(8,128)S(1)}, f32[2,256,256]{2,1,0:T(8,128)S(1)}, u32[]{:S(2)}, u32[]{:S(2)}) %collective-permute-start.7) | collective-permute-done | bytes 524320 | tf_op jit(solution)/shard_map/ppermute | solution.py:385
  37.5 13.0 %collective-permute-done.6.late_theirs = f32[2,384,256]{2,1,0:T(8,128)S(1)} collective-permute-done((f32[2,384,256]{2,1,0:T(8,128)S(1)}, f32[2,384,256]{2,1,0:T(8,128)S(1)}, u32[]{:S(2)}, u32[]{:S(2)}) %collective-permute-start.6) | collective-permute-done | bytes 786464 | tf_op jit(solution)/shard_map/ppermute | solution.py:385
  53.9 1.4 %collective-permute-start.11 = (f32[2,64,256]{2,1,0:T(8,128)S(1)}, f32[2,64,256]{2,1,0:T(8,128)S(1)}, u32[]{:S(2)}, u32[]{:S(2)}) collective-permute-start(f32[2,64,256]{2,1,0:T(8,128)S(1)} %get-tuple-element.48), channel_id=1, source_target_pairs={{6,4},{7,5},{4,2},{5,3},{2,0},{3,1},{14,12},{15,13},{12,10},{13,11... | collective-permute-start | bytes 393224 | tf_op jit(solution)/shard_map/ppermute | solution.py:388
  55.3 1.5 %collective-permute-start.12 = (f32[2,64,256]{2,1,0:T(8,128)S(1)}, f32[2,64,256]{2,1,0:T(8,128)S(1)}, u32[]{:S(2)}, u32[]{:S(2)}) collective-permute-start(f32[2,64,256]{2,1,0:T(8,128)S(1)} %get-tuple-element.49), channel_id=1, source_target_pairs={{4,0},{5,1},{12,8},{13,9},{20,16},{21,17},{28,24},{29,25}} | collective-permute-start | bytes 393224 | tf_op jit(solution)/shard_map/ppermute | solution.py:388
  56.8 1.8 %collective-permute-start.5 = (f32[2,128,256]{2,1,0:T(8,128)S(1)}, f32[2,128,256]{2,1,0:T(8,128)S(1)}, u32[]{:S(2)}, u32[]{:S(2)}) collective-permute-start(f32[2,128,256]{2,1,0:T(8,128)S(1)} %get-tuple-element.40.in_other), channel_id=1, source_target_pairs={{0,1},{1,0},{2,3},{3,2},{4,5},{5,4},{6,7},{7,6},{8,9},{9,8},{10,11... | collective-permute-start | bytes 786440 | tf_op jit(solution)/shard_map/ppermute | solution.py:385
  58.6 11.9 %collective-permute-done.11.came = f32[2,64,256]{2,1,0:T(8,128)S(1)} collective-permute-done((f32[2,64,256]{2,1,0:T(8,128)S(1)}, f32[2,64,256]{2,1,0:T(8,128)S(1)}, u32[]{:S(2)}, u32[]{:S(2)}) %collective-permute-start.11) | collective-permute-done | bytes 131104 | tf_op jit(solution)/shard_map/ppermute | solution.py:388
  70.5 1.7 %collective-permute-done.12.last = f32[2,64,256]{2,1,0:T(8,128)S(1)} collective-permute-done((f32[2,64,256]{2,1,0:T(8,128)S(1)}, f32[2,64,256]{2,1,0:T(8,128)S(1)}, u32[]{:S(2)}, u32[]{:S(2)}) %collective-permute-start.12) | collective-permute-done | bytes 131104 | tf_op jit(solution)/shard_map/ppermute | solution.py:388
  72.7 1.6 %collective-permute-start.15 = (f32[2,128,256]{2,1,0:T(8,128)S(1)}, f32[2,128,256]{2,1,0:T(8,128)S(1)}, u32[]{:S(2)}, u32[]{:S(2)}) collective-permute-start(f32[2,128,256]{2,1,0:T(8,128)S(1)} %get-tuple-element.55), channel_id=1, source_target_pairs={{0,1},{1,0},{2,3},{3,2},{4,5},{5,4},{6,7},{7,6},{8,9},{9,8},{10,11... | collective-permute-start | bytes 786440 | tf_op jit(solution)/shard_map/ppermute | solution.py:385
  74.3 1.5 %shard_map.61 = (f32[2,2,128,256]{3,2,1,0:T(8,128)S(1)}, f32[2,2,128,256]{3,2,1,0:T(8,128)S(1)}) custom-call(f32[2,2,256,256]{3,2,1,0:T(8,128)S(1)} %get-tuple-element.34.states, f32[2,128,256]{2,1,0:T(8,128)S(1)} %get-tuple-element.39.in_own, f32[2,128,256]{2,1,0:T(8,128)S(1)} %collective-permute-done.5.in_theirs, f32[2,2,256,256]{3,2,1,0:T(8,128)S(1)} %bitcast.9, ...), custom_call_target="tpu_custom_call" | custom-call | flops 805306368 | bytes 1048576 | tf_op jit(solution)/shard_map/pallas_call | solution.py:97
  76.5 1.6 %shard_map.66 = (f32[2,128,256]{2,1,0:T(8,128)S(1)}, f32[2,128,256]{2,1,0:T(8,128)S(1)}) custom-call(f32[2,2,128,256]{3,2,1,0:T(8,128)S(1)} %get-tuple-element.41.swept, f32[2,128,256]{2,1,0:T(8,128)S(1)} %get-tuple-element.51.entering, f32[2,2,256,256]{3,2,1,0:T(8,128)S(1)} %bitcast.5, f32[1,2]{1,0:T(1,128)S(1)} %copy-done.3), custom_call_target="tpu_custom_call" | custom-call | tf_op jit(solution)/shard_map/pallas_call | solution.py:458
  79.1 1.6 %shard_map.67 = (f32[2,128,256]{2,1,0:T(8,128)S(1)}, f32[2,128,256]{2,1,0:T(8,128)S(1)}) custom-call(f32[2,2,128,256]{3,2,1,0:T(8,128)S(1)} %get-tuple-element.54.swept, f32[2,128,256]{2,1,0:T(8,128)S(1)} %collective-permute-done.15.entering, f32[2,2,256,256]{3,2,1,0:T(8,128)S(1)} %bitcast.6, f32[1,2]{1,0:T(1,128)S(1)} %copy-done.3), custom_call_target="tpu_custom_call" | custom-call | tf_op jit(solution)/shard_map/pallas_call | solution.py:458
  80.9 1.5 %collective-permute-start.14 = (f32[2,128,256]{2,1,0:T(8,128)S(1)}, f32[2,128,256]{2,1,0:T(8,128)S(1)}, u32[]{:S(2)}, u32[]{:S(2)}) collective-permute-start(f32[2,128,256]{2,1,0:T(8,128)S(1)} %add.26.own), channel_id=1, source_target_pairs={{0,16},{8,24},{16,0},{24,8},{1,17},{9,25},{17,1},{25,9},{2,18},{10... | collective-permute-start | bytes 786440 | tf_op jit(solution)/shard_map/ppermute | solution.py:451
  82.5 1.5 %collective-permute-start.17 = (f32[2,128,256]{2,1,0:T(8,128)S(1)}, f32[2,128,256]{2,1,0:T(8,128)S(1)}, u32[]{:S(2)}, u32[]{:S(2)}) collective-permute-start(f32[2,128,256]{2,1,0:T(8,128)S(1)} %add.27.theirs), channel_id=1, source_target_pairs={{0,16},{8,24},{16,0},{24,8},{1,17},{9,25},{17,1},{25,9},{2,18},{10... | collective-permute-start | bytes 786440 | tf_op jit(solution)/shard_map/ppermute | solution.py:451
  84.0 6.2 %collective-permute-done.14.own_more = f32[2,128,256]{2,1,0:T(8,128)S(1)} collective-permute-done((f32[2,128,256]{2,1,0:T(8,128)S(1)}, f32[2,128,256]{2,1,0:T(8,128)S(1)}, u32[]{:S(2)}, u32[]{:S(2)}) %collective-permute-start.14) | collective-permute-done | bytes 262176 | tf_op jit(solution)/shard_map/ppermute | solution.py:451
  90.1 5.1 %collective-permute-done.17.theirs_more = f32[2,128,256]{2,1,0:T(8,128)S(1)} collective-permute-done((f32[2,128,256]{2,1,0:T(8,128)S(1)}, f32[2,128,256]{2,1,0:T(8,128)S(1)}, u32[]{:S(2)}, u32[]{:S(2)}) %collective-permute-start.17) | collective-permute-done | bytes 262176 | tf_op jit(solution)/shard_map/ppermute | solution.py:451
  96.1 1.3 %collective-permute-done.18 = f32[128,256]{1,0:T(8,128)S(1)} collective-permute-done((f32[128,256]{1,0:T(8,128)S(1)}, f32[128,256]{1,0:T(8,128)S(1)}, u32[]{:S(2)}, u32[]{:S(2)}) %collective-permute-start.18) | collective-permute-done | bytes 131104 | tf_op jit(solution)/shard_map/ppermute | solution.py:451
  97.5 1.6 %collective-permute-start.19 = (f32[128,256]{1,0:T(8,128)S(1)}, f32[128,256]{1,0:T(8,128)S(1)}, u32[]{:S(2)}, u32[]{:S(2)}) collective-permute-start(f32[128,256]{1,0:T(8,128)S(1)} %add.28), channel_id=1, source_target_pairs={{0,1},{1,0},{2,3},{3,2},{4,5},{5,4},{6,7},{7,6},{8,9},{9,8},{10,11... | collective-permute-start | bytes 393224 | tf_op jit(solution)/shard_map/ppermute | solution.py:481
  99.1 4.0 %collective-permute-done.19 = f32[128,256]{1,0:T(8,128)S(1)} collective-permute-done((f32[128,256]{1,0:T(8,128)S(1)}, f32[128,256]{1,0:T(8,128)S(1)}, u32[]{:S(2)}, u32[]{:S(2)}) %collective-permute-start.19) | collective-permute-done | bytes 131104 | tf_op jit(solution)/shard_map/ppermute | solution.py:481
  104.3 3.8 %collective-permute-done.20 = f32[128,256]{1,0:T(8,128)S(1)} collective-permute-done((f32[128,256]{1,0:T(8,128)S(1)}, f32[128,256]{1,0:T(8,128)S(1)}, u32[]{:S(2)}, u32[]{:S(2)}) %collective-permute-start.20) | collective-permute-done | bytes 131104 | tf_op jit(solution)/shard_map/ppermute | solution.py:481
  108.1 2.4 %collective-permute-start.21 = (f32[128,256]{1,0:T(8,128)S(1)}, f32[128,256]{1,0:T(8,128)S(1)}, u32[]{:S(2)}, u32[]{:S(2)}) collective-permute-start(f32[128,256]{1,0:T(8,128)S(1)} %add.30), channel_id=1, source_target_pairs={{0,6},{1,7},{2,4},{3,5},{4,2},{5,3},{6,0},{7,1},{8,14},{9,15},{10,... | collective-permute-start | bytes 393224 | tf_op jit(solution)/shard_map/ppermute | solution.py:481
  110.6 4.5 %collective-permute-done.21 = f32[128,256]{1,0:T(8,128)S(1)} collective-permute-done((f32[128,256]{1,0:T(8,128)S(1)}, f32[128,256]{1,0:T(8,128)S(1)}, u32[]{:S(2)}, u32[]{:S(2)}) %collective-permute-start.21) | collective-permute-done | bytes 131104 | tf_op jit(solution)/shard_map/ppermute | solution.py:481
  116.5 2.4 %shard_map.70 = f32[2,64,512]{2,1,0:T(8,128)} custom-call(f32[128,256]{1,0:T(8,128)S(1)} %add.31.mine, f32[128,256]{1,0:T(8,128)S(1)} %collective-permute-done.22.theirs, bf16[2,2,256,256]{3,2,1,0:T(8,128)(2,1)S(1)} %get-tuple-element.61.q_high, bf16[2,2,256,256]{3,2,1,0:T(8,128)(2,1)S(1)} %get-tuple-element.62.q_low), custom_call_target="tpu_custom_call" | custom-call | flops 1610612736 | bytes 1048576 | tf_op jit(solution)/shard_map/pallas_call | solution.py:370
  (52 shorter events, 14.4 us)
Async XLA Ops:
  0.0 5.0 %copy-start = (f32[1,2,2,256,256]{4,3,2,1,0:T(8,128)S(1)}, f32[1,2,2,256,256]{4,3,2,1,0:T(8,128)}, u32[]{:S(2)}) copy-start(f32[1,2,2,256,256]{4,3,2,1,0:T(8,128)} %param.8) | copy-start | bytes 3145732
  0.0 1.3 %copy-start.1 = (f32[1,2,2,256,256]{4,3,2,1,0:T(8,128)S(1)}, f32[1,2,2,256,256]{4,3,2,1,0:T(8,128)}, u32[]{:S(2)}) copy-start(f32[1,2,2,256,256]{4,3,2,1,0:T(8,128)} %param.7) | copy-start | bytes 3145732
  1.9 21.4 %collective-permute-start = (f32[2,256,256]{2,1,0:T(8,128)S(1)}, f32[2,256,256]{2,1,0:T(8,128)S(1)}, u32[]{:S(2)}, u32[]{:S(2)}) collective-permute-start(f32[2,256,256]{2,1,0:T(8,128)S(1)} %shard_map.55.ahead.mine.a_mine), channel_id=1, source_target_pairs={{0,1},{1,0},{2,3},{3,2},{4,5},{5,4},{6,7},{7,6},{8,9},{9,8},{10,11... | collective-permute-start | bytes 1572872 | tf_op jit(solution)/shard_map/ppermute | solution.py:385
  5.0 1.2 %copy-start.4 = (f32[2,256,512]{2,1,0:T(8,128)S(1)}, f32[2,256,512]{2,1,0:T(8,128)}, u32[]{:S(2)}) copy-start(f32[2,256,512]{2,1,0:T(8,128)} %piece.1) | copy-start | bytes 3145732
  6.2 1.2 %copy-start.5 = (f32[1,2,2,256,256]{4,3,2,1,0:T(8,128)S(1)}, f32[1,2,2,256,256]{4,3,2,1,0:T(8,128)}, u32[]{:S(2)}) copy-start(f32[1,2,2,256,256]{4,3,2,1,0:T(8,128)} %param.6) | copy-start | bytes 3145732
  10.4 12.9 %collective-permute-start.1 = (f32[2,128,256]{2,1,0:T(8,128)S(1)}, f32[2,128,256]{2,1,0:T(8,128)S(1)}, u32[]{:S(2)}, u32[]{:S(2)}) collective-permute-start(f32[2,128,256]{2,1,0:T(8,128)S(1)} %get-tuple-element.36), channel_id=1, source_target_pairs={{0,1},{1,0},{2,3},{3,2},{4,5},{5,4},{6,7},{7,6},{8,9},{9,8},{10,11... | collective-permute-start | bytes 786440 | tf_op jit(solution)/shard_map/ppermute | solution.py:385
  10.5 24.1 %collective-permute-start.7 = (f32[2,256,256]{2,1,0:T(8,128)S(1)}, f32[2,256,256]{2,1,0:T(8,128)S(1)}, u32[]{:S(2)}, u32[]{:S(2)}) collective-permute-start(f32[2,256,256]{2,1,0:T(8,128)S(1)} %get-tuple-element.44.c_mine.mine), channel_id=1, source_target_pairs={{0,1},{1,0},{2,3},{3,2},{4,5},{5,4},{6,7},{7,6},{8,9},{9,8},{10,11... | collective-permute-start | bytes 1572872 | tf_op jit(solution)/shard_map/ppermute | solution.py:385
  24.2 7.9 %collective-permute-start.2 = (f32[2,128,256]{2,1,0:T(8,128)S(1)}, f32[2,128,256]{2,1,0:T(8,128)S(1)}, u32[]{:S(2)}, u32[]{:S(2)}) collective-permute-start(f32[2,128,256]{2,1,0:T(8,128)S(1)} %get-tuple-element.37.base), channel_id=1, source_target_pairs={{0,2},{1,3},{8,10},{9,11},{16,18},{17,19},{24,26},{25,27}} | collective-permute-start | bytes 786440 | tf_op jit(solution)/shard_map/ppermute | solution.py:388
  28.2 22.4 %collective-permute-start.6 = (f32[2,384,256]{2,1,0:T(8,128)S(1)}, f32[2,384,256]{2,1,0:T(8,128)S(1)}, u32[]{:S(2)}, u32[]{:S(2)}) collective-permute-start(f32[2,384,256]{2,1,0:T(8,128)S(1)} %get-tuple-element.43.late_mine), channel_id=1, source_target_pairs={{0,1},{1,0},{2,3},{3,2},{4,5},{5,4},{6,7},{7,6},{8,9},{9,8},{10,11... | collective-permute-start | bytes 2359304 | tf_op jit(solution)/shard_map/ppermute | solution.py:385
  32.5 3.4 %collective-permute-start.3 = (f32[2,128,256]{2,1,0:T(8,128)S(1)}, f32[2,128,256]{2,1,0:T(8,128)S(1)}, u32[]{:S(2)}, u32[]{:S(2)}) collective-permute-start(f32[2,128,256]{2,1,0:T(8,128)S(1)} %shard_map.58), channel_id=1, source_target_pairs={{2,4},{3,5},{10,12},{11,13},{18,20},{19,21},{26,28},{27,29}} | collective-permute-start | bytes 786440 | tf_op jit(solution)/shard_map/ppermute | solution.py:388
  35.2 17.9 %collective-permute-start.10 = (f32[2,256,256]{2,1,0:T(8,128)S(1)}, f32[2,256,256]{2,1,0:T(8,128)S(1)}, u32[]{:S(2)}, u32[]{:S(2)}) collective-permute-start(f32[2,256,256]{2,1,0:T(8,128)S(1)} %shard_map.63.c_mine), channel_id=1, source_target_pairs={{2,4},{3,5},{4,2},{5,3},{10,12},{11,13},{12,10},{13,11},{18,20},{1... | collective-permute-start | bytes 1572872 | tf_op jit(solution)/shard_map/ppermute | solution.py:388
  36.4 0.7 collective-permute-start.4
  51.7 1.4 %collective-permute-start.8 = (f32[2,64,256]{2,1,0:T(8,128)S(1)}, f32[2,64,256]{2,1,0:T(8,128)S(1)}, u32[]{:S(2)}, u32[]{:S(2)}) collective-permute-start(f32[2,64,256]{2,1,0:T(8,128)S(1)} %get-tuple-element.45.mine_a), channel_id=1, source_target_pairs={{6,4},{7,5},{4,2},{5,3},{14,12},{15,13},{12,10},{13,11},{22,20},{2... | collective-permute-start | bytes 393224 | tf_op jit(solution)/shard_map/ppermute | solution.py:388
  52.4 0.7 collective-permute-start.9
  53.9 20.4 %copy-start.2 = (f32[1,2,2,256,256]{4,3,2,1,0:T(8,128)S(1)}, f32[1,2,2,256,256]{4,3,2,1,0:T(8,128)}, u32[]{:S(2)}) copy-start(f32[1,2,2,256,256]{4,3,2,1,0:T(8,128)} %param.7) | copy-start | bytes 3145732
  53.9 16.6 %collective-permute-start.11 = (f32[2,64,256]{2,1,0:T(8,128)S(1)}, f32[2,64,256]{2,1,0:T(8,128)S(1)}, u32[]{:S(2)}, u32[]{:S(2)}) collective-permute-start(f32[2,64,256]{2,1,0:T(8,128)S(1)} %get-tuple-element.48), channel_id=1, source_target_pairs={{6,4},{7,5},{4,2},{5,3},{2,0},{3,1},{14,12},{15,13},{12,10},{13,11... | collective-permute-start | bytes 393224 | tf_op jit(solution)/shard_map/ppermute | solution.py:388
  55.3 16.9 %collective-permute-start.12 = (f32[2,64,256]{2,1,0:T(8,128)S(1)}, f32[2,64,256]{2,1,0:T(8,128)S(1)}, u32[]{:S(2)}, u32[]{:S(2)}) collective-permute-start(f32[2,64,256]{2,1,0:T(8,128)S(1)} %get-tuple-element.49), channel_id=1, source_target_pairs={{4,0},{5,1},{12,8},{13,9},{20,16},{21,17},{28,24},{29,25}} | collective-permute-start | bytes 393224 | tf_op jit(solution)/shard_map/ppermute | solution.py:388
  56.8 17.5 %collective-permute-start.5 = (f32[2,128,256]{2,1,0:T(8,128)S(1)}, f32[2,128,256]{2,1,0:T(8,128)S(1)}, u32[]{:S(2)}, u32[]{:S(2)}) collective-permute-start(f32[2,128,256]{2,1,0:T(8,128)S(1)} %get-tuple-element.40.in_other), channel_id=1, source_target_pairs={{0,1},{1,0},{2,3},{3,2},{4,5},{5,4},{6,7},{7,6},{8,9},{9,8},{10,11... | collective-permute-start | bytes 786440 | tf_op jit(solution)/shard_map/ppermute | solution.py:385
  72.7 6.4 %collective-permute-start.15 = (f32[2,128,256]{2,1,0:T(8,128)S(1)}, f32[2,128,256]{2,1,0:T(8,128)S(1)}, u32[]{:S(2)}, u32[]{:S(2)}) collective-permute-start(f32[2,128,256]{2,1,0:T(8,128)S(1)} %get-tuple-element.55), channel_id=1, source_target_pairs={{0,1},{1,0},{2,3},{3,2},{4,5},{5,4},{6,7},{7,6},{8,9},{9,8},{10,11... | collective-permute-start | bytes 786440 | tf_op jit(solution)/shard_map/ppermute | solution.py:385
  75.8 0.7 copy-start.3
  78.1 2.8 %collective-permute-start.13 = (f32[2,128,256]{2,1,0:T(8,128)S(1)}, f32[2,128,256]{2,1,0:T(8,128)S(1)}, u32[]{:S(2)}, u32[]{:S(2)}) collective-permute-start(f32[2,128,256]{2,1,0:T(8,128)S(1)} %get-tuple-element.53), channel_id=1, source_target_pairs={{0,8},{8,0},{16,24},{24,16},{1,9},{9,1},{17,25},{25,17},{2,10},{10... | collective-permute-start | bytes 786440 | tf_op jit(solution)/shard_map/ppermute | solution.py:451
  80.8 1.7 %collective-permute-start.16 = (f32[2,128,256]{2,1,0:T(8,128)S(1)}, f32[2,128,256]{2,1,0:T(8,128)S(1)}, u32[]{:S(2)}, u32[]{:S(2)}) collective-permute-start(f32[2,128,256]{2,1,0:T(8,128)S(1)} %get-tuple-element.57), channel_id=1, source_target_pairs={{0,8},{8,0},{16,24},{24,16},{1,9},{9,1},{17,25},{25,17},{2,10},{10... | collective-permute-start | bytes 786440 | tf_op jit(solution)/shard_map/ppermute | solution.py:451
  80.9 9.2 %collective-permute-start.14 = (f32[2,128,256]{2,1,0:T(8,128)S(1)}, f32[2,128,256]{2,1,0:T(8,128)S(1)}, u32[]{:S(2)}, u32[]{:S(2)}) collective-permute-start(f32[2,128,256]{2,1,0:T(8,128)S(1)} %add.26.own), channel_id=1, source_target_pairs={{0,16},{8,24},{16,0},{24,8},{1,17},{9,25},{17,1},{25,9},{2,18},{10... | collective-permute-start | bytes 786440 | tf_op jit(solution)/shard_map/ppermute | solution.py:451
  82.5 12.8 %collective-permute-start.17 = (f32[2,128,256]{2,1,0:T(8,128)S(1)}, f32[2,128,256]{2,1,0:T(8,128)S(1)}, u32[]{:S(2)}, u32[]{:S(2)}) collective-permute-start(f32[2,128,256]{2,1,0:T(8,128)S(1)} %add.27.theirs), channel_id=1, source_target_pairs={{0,16},{8,24},{16,0},{24,8},{1,17},{9,25},{17,1},{25,9},{2,18},{10... | collective-permute-start | bytes 786440 | tf_op jit(solution)/shard_map/ppermute | solution.py:451
  96.0 1.4 %collective-permute-start.18 = (f32[128,256]{1,0:T(8,128)S(1)}, f32[128,256]{1,0:T(8,128)S(1)}, u32[]{:S(2)}, u32[]{:S(2)}) collective-permute-start(f32[128,256]{1,0:T(8,128)S(1)} %get-tuple-element.59), channel_id=1, source_target_pairs={{0,8},{8,0},{16,24},{24,16},{1,9},{9,1},{17,25},{25,17},{2,10},{10... | collective-permute-start | bytes 393224 | tf_op jit(solution)/shard_map/ppermute | solution.py:451
  97.5 5.6 %collective-permute-start.19 = (f32[128,256]{1,0:T(8,128)S(1)}, f32[128,256]{1,0:T(8,128)S(1)}, u32[]{:S(2)}, u32[]{:S(2)}) collective-permute-start(f32[128,256]{1,0:T(8,128)S(1)} %add.28), channel_id=1, source_target_pairs={{0,1},{1,0},{2,3},{3,2},{4,5},{5,4},{6,7},{7,6},{8,9},{9,8},{10,11... | collective-permute-start | bytes 393224 | tf_op jit(solution)/shard_map/ppermute | solution.py:481
  99.1 16.1 %collective-permute-start.23 = (f32[2,256,256]{2,1,0:T(8,128)S(1)}, f32[2,256,256]{2,1,0:T(8,128)S(1)}, u32[]{:S(2)}, u32[]{:S(2)}) collective-permute-start(f32[2,256,256]{2,1,0:T(8,128)S(1)} %get-tuple-element.60.mine), channel_id=1, source_target_pairs={{0,8},{8,0},{16,24},{24,16},{1,9},{9,1},{17,25},{25,17},{2,10},{10... | collective-permute-start | bytes 1572872 | tf_op jit(solution)/shard_map/ppermute | solution.py:451
  103.1 5.0 %collective-permute-start.20 = (f32[128,256]{1,0:T(8,128)S(1)}, f32[128,256]{1,0:T(8,128)S(1)}, u32[]{:S(2)}, u32[]{:S(2)}) collective-permute-start(f32[128,256]{1,0:T(8,128)S(1)} %add.29), channel_id=1, source_target_pairs={{0,2},{1,3},{2,0},{3,1},{4,6},{5,7},{6,4},{7,5},{8,10},{9,11},{10,... | collective-permute-start | bytes 393224 | tf_op jit(solution)/shard_map/ppermute | solution.py:481
  108.1 6.9 %collective-permute-start.21 = (f32[128,256]{1,0:T(8,128)S(1)}, f32[128,256]{1,0:T(8,128)S(1)}, u32[]{:S(2)}, u32[]{:S(2)}) collective-permute-start(f32[128,256]{1,0:T(8,128)S(1)} %add.30), channel_id=1, source_target_pairs={{0,6},{1,7},{2,4},{3,5},{4,2},{5,3},{6,0},{7,1},{8,14},{9,15},{10,... | collective-permute-start | bytes 393224 | tf_op jit(solution)/shard_map/ppermute | solution.py:481
  115.1 1.4 %collective-permute-start.22 = (f32[128,256]{1,0:T(8,128)S(1)}, f32[128,256]{1,0:T(8,128)S(1)}, u32[]{:S(2)}, u32[]{:S(2)}) collective-permute-start(f32[128,256]{1,0:T(8,128)S(1)} %add.31.mine), channel_id=1, source_target_pairs={{0,8},{8,0},{16,24},{24,16},{1,9},{9,1},{17,25},{25,17},{2,10},{10... | collective-permute-start | bytes 393224 | tf_op jit(solution)/shard_map/ppermute | solution.py:451

commit v5 on v4

--- a/solution.py
+++ b/solution.py
@@ -257,7 +257,7 @@
     back_in(pair(work), mid, c_mine, c_theirs, own, other)
 
 
-def swept_kernel(states, in_own, in_theirs, lower, upper, out_own, out_theirs):
+def swept_kernel(states, in_own, in_theirs, lower, upper, weights, out_own, out_theirs):
     count = states.shape[0]
     half = in_own.shape[1]
     mine = jnp.where(side(), 0, half)
@@ -433,10 +433,14 @@
         last = between(last, [(2, 0)])
     else:
         back_inflow = prefix(ends[0], c_node, order[::-1])
-    swept_own, swept_theirs = call(
-        swept_kernel, [(count,) + strip] * 2, states, in_own, in_theirs, lower, upper,
-        products=count,
-    )
+    swept_own, swept_theirs = pl.pallas_call(
+        swept_kernel,
+        out_shape=[jax.ShapeDtypeStruct((count,) + strip, F32)] * 2,
+        in_specs=[pl.BlockSpec(memory_space=vmem)] * 5
+        + [pl.BlockSpec(memory_space=pltpu.SMEM)],
+        out_specs=[pl.BlockSpec(memory_space=vmem)] * 2,
+        compiler_params=pltpu.CompilerParams(vmem_limit_bytes=GRANT),
+    )(states, in_own, in_theirs, lower, upper, pole_weights)
     if short:
         x_own, x_other = scratch(
             back_in_parts_kernel, [strip] * 2, [strip], keep, came, last, mid, c_mine, c_theirs

time: 119 us -> 119 us (level)
    pallas_call x0 -> x1, Pallas kernels: none -> 2.04 us  [shards(): pl.pallas_call(swept_kernel, out_shape=[jax.ShapeDtypeStruct((count,) + s...]
    pallas_call x9 -> x8, Pallas kernels: 6.65 us -> 5.15 us  [call(): pl.pallas_call(body, out_shape=shapes, in_specs=[pl.BlockSpec(memory_spac...]
  transfers between devices with their start and end apart: 24 -> 24, of which waited for: 14 -> 14; matrix products, arithmetic and copies ran while one was open for 0% -> 0% of each run, Pallas kernels for 10% -> 11%
where the time goes in v5:
time: 119 us
  waiting for transfers between devices  68.7 us (58%)
  starting transfers between devices  28.7 us (24%)
  Pallas kernels  17.2 us (14%)
  local copies, waits for them, and re-layouts  3.78 us (3%)
    ppermute x6, waiting for transfers between devices, beside(): return lax.ppermute(value, 'rows', swap)  26.3 us
    ppermute x8, waiting for transfers between devices, between(): lax.ppermute(value, 'rows', [(2 * a + s, 2 * b + s) for a, b in moves for...  15.9 us
    ppermute x7, waiting for transfers between devices, over_poles(): lax.ppermute(value, 'pole', [(place, place ^ 1 << bit) for place in range...  13.8 us
    ppermute x3, waiting for transfers between devices, shards(): lax.ppermute(packed, 'rows', [(place, place ^ mask) for place in range(de...  12.6 us
    ppermute x8, starting transfers between devices, between(): lax.ppermute(value, 'rows', [(2 * a + s, 2 * b + s) for a, b in moves for...  10.3 us
    ppermute x6, starting transfers between devices, beside(): return lax.ppermute(value, 'rows', swap)  10.1 us
    pallas_call x4, Pallas kernels, scratch(): pl.pallas_call(body, out_shape=[jax.ShapeDtypeStruct(shape, F32) for shap...  6.54 us
    pallas_call x8, Pallas kernels, call(): pl.pallas_call(body, out_shape=shapes, in_specs=[pl.BlockSpec(memory_spac...  5.15 us
  transfers between devices with their start and end apart: 24, of which 14 were waited for; matrix products, arithmetic and copies ran while one was open for 0% of the time, Pallas kernels for 11%

profile of v5, /device:TPU:0, one launch (start us, length us, event | category | flops | bytes accessed | tf_op | source)
XLA Modules:
  0.0 118.9 jit_solution(8942479232686528377)
XLA Ops:
  0.0 1.3 %copy-done.1 = f32[1,2,2,256,256]{4,3,2,1,0:T(8,128)S(1)} copy-done((f32[1,2,2,256,256]{4,3,2,1,0:T(8,128)S(1)}, f32[1,2,2,256,256]{4,3,2,1,0:T(8,128)}, u32[]{:S(2)}) %copy-start.1) | copy-done | bytes 1048600
  1.9 3.0 %collective-permute-start = (f32[2,256,256]{2,1,0:T(8,128)S(1)}, f32[2,256,256]{2,1,0:T(8,128)S(1)}, u32[]{:S(2)}, u32[]{:S(2)}) collective-permute-start(f32[2,256,256]{2,1,0:T(8,128)S(1)} %shard_map.55.ahead.mine.a_mine), channel_id=1, source_target_pairs={{0,1},{1,0},{2,3},{3,2},{4,5},{5,4},{6,7},{7,6},{8,9},{9,8},{10,11... | collective-permute-start | bytes 1572872 | tf_op jit(solution)/shard_map/ppermute | solution.py:385
  5.0 1.2 %copy-done.4 = f32[2,256,512]{2,1,0:T(8,128)S(1)} copy-done((f32[2,256,512]{2,1,0:T(8,128)S(1)}, f32[2,256,512]{2,1,0:T(8,128)}, u32[]{:S(2)}) %copy-start.4) | copy-done | bytes 1048600
  6.2 1.2 %copy-done.5 = f32[1,2,2,256,256]{4,3,2,1,0:T(8,128)S(1)} copy-done((f32[1,2,2,256,256]{4,3,2,1,0:T(8,128)S(1)}, f32[1,2,2,256,256]{4,3,2,1,0:T(8,128)}, u32[]{:S(2)}) %copy-start.5) | copy-done | bytes 1048600
  7.4 3.0 %shard_map.56 = (f32[2,2,256,256]{3,2,1,0:T(8,128)S(1)}, f32[2,128,256]{2,1,0:T(8,128)S(1)}, f32[2,128,256]{2,1,0:T(8,128)S(1)}, f32[2,128,256]{2,1,0:T(8,128)S(...) custom-call(f32[2,256,512]{2,1,0:T(8,128)S(1)} %copy-done.4, f32[2,2,256,256]{3,2,1,0:T(8,128)S(1)} %bitcast.10, ...), custom_call_target="tpu_custom_call" | custom-call | flops 2818572288 | bytes 1048576 | tf_op jit(solution)/shard_map/pallas_call | solution.py:370
  10.5 2.0 %collective-permute-start.7 = (f32[2,256,256]{2,1,0:T(8,128)S(1)}, f32[2,256,256]{2,1,0:T(8,128)S(1)}, u32[]{:S(2)}, u32[]{:S(2)}) collective-permute-start(f32[2,256,256]{2,1,0:T(8,128)S(1)} %get-tuple-element.44.c_mine.mine), channel_id=1, source_target_pairs={{0,1},{1,0},{2,3},{3,2},{4,5},{5,4},{6,7},{7,6},{8,9},{9,8},{10,11... | collective-permute-start | bytes 1572872 | tf_op jit(solution)/shard_map/ppermute | solution.py:385
  12.5 10.8 %collective-permute-done.1.btheirs.b_theirs = f32[2,128,256]{2,1,0:T(8,128)S(1)} collective-permute-done((f32[2,128,256]{2,1,0:T(8,128)S(1)}, f32[2,128,256]{2,1,0:T(8,128)S(1)}, u32[]{:S(2)}, u32[]{:S(2)}) %collective-permute-start.1) | collective-permute-done | bytes 262176 | tf_op jit(solution)/shard_map/ppermute | solution.py:385
  24.2 4.0 %collective-permute-start.2 = (f32[2,128,256]{2,1,0:T(8,128)S(1)}, f32[2,128,256]{2,1,0:T(8,128)S(1)}, u32[]{:S(2)}, u32[]{:S(2)}) collective-permute-start(f32[2,128,256]{2,1,0:T(8,128)S(1)} %get-tuple-element.37.base), channel_id=1, source_target_pairs={{0,2},{1,3},{8,10},{9,11},{16,18},{17,19},{24,26},{25,27}} | collective-permute-start | bytes 786440 | tf_op jit(solution)/shard_map/ppermute | solution.py:388
  28.2 1.6 %collective-permute-start.6 = (f32[2,384,256]{2,1,0:T(8,128)S(1)}, f32[2,384,256]{2,1,0:T(8,128)S(1)}, u32[]{:S(2)}, u32[]{:S(2)}) collective-permute-start(f32[2,384,256]{2,1,0:T(8,128)S(1)} %get-tuple-element.43.late_mine), channel_id=1, source_target_pairs={{0,1},{1,0},{2,3},{3,2},{4,5},{5,4},{6,7},{7,6},{8,9},{9,8},{10,11... | collective-permute-start | bytes 2359304 | tf_op jit(solution)/shard_map/ppermute | solution.py:385
  29.8 2.3 %collective-permute-done.2.state = f32[2,128,256]{2,1,0:T(8,128)S(1)} collective-permute-done((f32[2,128,256]{2,1,0:T(8,128)S(1)}, f32[2,128,256]{2,1,0:T(8,128)S(1)}, u32[]{:S(2)}, u32[]{:S(2)}) %collective-permute-start.2) | collective-permute-done | bytes 262176 | tf_op jit(solution)/shard_map/ppermute | solution.py:388
  33.1 1.4 %collective-permute-done.7.c_theirs.theirs = f32[2,256,256]{2,1,0:T(8,128)S(1)} collective-permute-done((f32[2,256,256]{2,1,0:T(8,128)S(1)}, f32[2,256,256]{2,1,0:T(8,128)S(1)}, u32[]{:S(2)}, u32[]{:S(2)}) %collective-permute-start.7) | collective-permute-done | bytes 524320 | tf_op jit(solution)/shard_map/ppermute | solution.py:385
  37.5 13.0 %collective-permute-done.6.late_theirs = f32[2,384,256]{2,1,0:T(8,128)S(1)} collective-permute-done((f32[2,384,256]{2,1,0:T(8,128)S(1)}, f32[2,384,256]{2,1,0:T(8,128)S(1)}, u32[]{:S(2)}, u32[]{:S(2)}) %collective-permute-start.6) | collective-permute-done | bytes 786464 | tf_op jit(solution)/shard_map/ppermute | solution.py:385
  53.9 1.4 %collective-permute-start.11 = (f32[2,64,256]{2,1,0:T(8,128)S(1)}, f32[2,64,256]{2,1,0:T(8,128)S(1)}, u32[]{:S(2)}, u32[]{:S(2)}) collective-permute-start(f32[2,64,256]{2,1,0:T(8,128)S(1)} %get-tuple-element.48), channel_id=1, source_target_pairs={{6,4},{7,5},{4,2},{5,3},{2,0},{3,1},{14,12},{15,13},{12,10},{13,11... | collective-permute-start | bytes 393224 | tf_op jit(solution)/shard_map/ppermute | solution.py:388
  55.3 1.5 %collective-permute-start.12 = (f32[2,64,256]{2,1,0:T(8,128)S(1)}, f32[2,64,256]{2,1,0:T(8,128)S(1)}, u32[]{:S(2)}, u32[]{:S(2)}) collective-permute-start(f32[2,64,256]{2,1,0:T(8,128)S(1)} %get-tuple-element.49), channel_id=1, source_target_pairs={{4,0},{5,1},{12,8},{13,9},{20,16},{21,17},{28,24},{29,25}} | collective-permute-start | bytes 393224 | tf_op jit(solution)/shard_map/ppermute | solution.py:388
  56.8 1.8 %collective-permute-start.5 = (f32[2,128,256]{2,1,0:T(8,128)S(1)}, f32[2,128,256]{2,1,0:T(8,128)S(1)}, u32[]{:S(2)}, u32[]{:S(2)}) collective-permute-start(f32[2,128,256]{2,1,0:T(8,128)S(1)} %get-tuple-element.40.in_other), channel_id=1, source_target_pairs={{0,1},{1,0},{2,3},{3,2},{4,5},{5,4},{6,7},{7,6},{8,9},{9,8},{10,11... | collective-permute-start | bytes 786440 | tf_op jit(solution)/shard_map/ppermute | solution.py:385
  58.6 11.9 %collective-permute-done.11.came = f32[2,64,256]{2,1,0:T(8,128)S(1)} collective-permute-done((f32[2,64,256]{2,1,0:T(8,128)S(1)}, f32[2,64,256]{2,1,0:T(8,128)S(1)}, u32[]{:S(2)}, u32[]{:S(2)}) %collective-permute-start.11) | collective-permute-done | bytes 131104 | tf_op jit(solution)/shard_map/ppermute | solution.py:388
  70.5 1.7 %collective-permute-done.12.last = f32[2,64,256]{2,1,0:T(8,128)S(1)} collective-permute-done((f32[2,64,256]{2,1,0:T(8,128)S(1)}, f32[2,64,256]{2,1,0:T(8,128)S(1)}, u32[]{:S(2)}, u32[]{:S(2)}) %collective-permute-start.12) | collective-permute-done | bytes 131104 | tf_op jit(solution)/shard_map/ppermute | solution.py:388
  72.7 1.6 %collective-permute-start.15 = (f32[2,128,256]{2,1,0:T(8,128)S(1)}, f32[2,128,256]{2,1,0:T(8,128)S(1)}, u32[]{:S(2)}, u32[]{:S(2)}) collective-permute-start(f32[2,128,256]{2,1,0:T(8,128)S(1)} %get-tuple-element.55), channel_id=1, source_target_pairs={{0,1},{1,0},{2,3},{3,2},{4,5},{5,4},{6,7},{7,6},{8,9},{9,8},{10,11... | collective-permute-start | bytes 786440 | tf_op jit(solution)/shard_map/ppermute | solution.py:385
  74.3 2.0 %shard_map.61 = (f32[2,2,128,256]{3,2,1,0:T(8,128)S(1)}, f32[2,2,128,256]{3,2,1,0:T(8,128)S(1)}) custom-call(f32[2,2,256,256]{3,2,1,0:T(8,128)S(1)} %get-tuple-element.34.states, f32[2,128,256]{2,1,0:T(8,128)S(1)} %get-tuple-element.39.in_own, f32[2,128,256]{2,1,0:T(8,128)S(1)} %collective-permute-done.5.in_theirs, f32[2,2,256,256]{3,2,1,0:T(8,128)S(1)} %bitcast.9, ...), custom_call_target="tpu_custom_call" | custom-call | tf_op jit(solution)/shard_map/pallas_call | solution.py:436
  76.4 1.7 %shard_map.66 = (f32[2,128,256]{2,1,0:T(8,128)S(1)}, f32[2,128,256]{2,1,0:T(8,128)S(1)}) custom-call(f32[2,2,128,256]{3,2,1,0:T(8,128)S(1)} %get-tuple-element.41.swept, f32[2,128,256]{2,1,0:T(8,128)S(1)} %get-tuple-element.51.entering, f32[2,2,256,256]{3,2,1,0:T(8,128)S(1)} %bitcast.5, f32[1,2]{1,0:T(1,128)S(1)} %copy-done.3), custom_call_target="tpu_custom_call" | custom-call | tf_op jit(solution)/shard_map/pallas_call | solution.py:462
  79.1 1.7 %shard_map.67 = (f32[2,128,256]{2,1,0:T(8,128)S(1)}, f32[2,128,256]{2,1,0:T(8,128)S(1)}) custom-call(f32[2,2,128,256]{3,2,1,0:T(8,128)S(1)} %get-tuple-element.54.swept, f32[2,128,256]{2,1,0:T(8,128)S(1)} %collective-permute-done.15.entering, f32[2,2,256,256]{3,2,1,0:T(8,128)S(1)} %bitcast.6, f32[1,2]{1,0:T(1,128)S(1)} %copy-done.3), custom_call_target="tpu_custom_call" | custom-call | tf_op jit(solution)/shard_map/pallas_call | solution.py:462
  80.9 1.5 %collective-permute-start.14 = (f32[2,128,256]{2,1,0:T(8,128)S(1)}, f32[2,128,256]{2,1,0:T(8,128)S(1)}, u32[]{:S(2)}, u32[]{:S(2)}) collective-permute-start(f32[2,128,256]{2,1,0:T(8,128)S(1)} %add.26.own), channel_id=1, source_target_pairs={{0,16},{8,24},{16,0},{24,8},{1,17},{9,25},{17,1},{25,9},{2,18},{10... | collective-permute-start | bytes 786440 | tf_op jit(solution)/shard_map/ppermute | solution.py:455
  82.5 1.5 %collective-permute-start.17 = (f32[2,128,256]{2,1,0:T(8,128)S(1)}, f32[2,128,256]{2,1,0:T(8,128)S(1)}, u32[]{:S(2)}, u32[]{:S(2)}) collective-permute-start(f32[2,128,256]{2,1,0:T(8,128)S(1)} %add.27.theirs), channel_id=1, source_target_pairs={{0,16},{8,24},{16,0},{24,8},{1,17},{9,25},{17,1},{25,9},{2,18},{10... | collective-permute-start | bytes 786440 | tf_op jit(solution)/shard_map/ppermute | solution.py:455
  84.0 6.2 %collective-permute-done.14.own_more = f32[2,128,256]{2,1,0:T(8,128)S(1)} collective-permute-done((f32[2,128,256]{2,1,0:T(8,128)S(1)}, f32[2,128,256]{2,1,0:T(8,128)S(1)}, u32[]{:S(2)}, u32[]{:S(2)}) %collective-permute-start.14) | collective-permute-done | bytes 262176 | tf_op jit(solution)/shard_map/ppermute | solution.py:455
  90.2 5.1 %collective-permute-done.17.theirs_more = f32[2,128,256]{2,1,0:T(8,128)S(1)} collective-permute-done((f32[2,128,256]{2,1,0:T(8,128)S(1)}, f32[2,128,256]{2,1,0:T(8,128)S(1)}, u32[]{:S(2)}, u32[]{:S(2)}) %collective-permute-start.17) | collective-permute-done | bytes 262176 | tf_op jit(solution)/shard_map/ppermute | solution.py:455
  96.1 1.3 %collective-permute-done.18 = f32[128,256]{1,0:T(8,128)S(1)} collective-permute-done((f32[128,256]{1,0:T(8,128)S(1)}, f32[128,256]{1,0:T(8,128)S(1)}, u32[]{:S(2)}, u32[]{:S(2)}) %collective-permute-start.18) | collective-permute-done | bytes 131104 | tf_op jit(solution)/shard_map/ppermute | solution.py:455
  97.5 1.6 %collective-permute-start.19 = (f32[128,256]{1,0:T(8,128)S(1)}, f32[128,256]{1,0:T(8,128)S(1)}, u32[]{:S(2)}, u32[]{:S(2)}) collective-permute-start(f32[128,256]{1,0:T(8,128)S(1)} %add.28), channel_id=1, source_target_pairs={{0,1},{1,0},{2,3},{3,2},{4,5},{5,4},{6,7},{7,6},{8,9},{9,8},{10,11... | collective-permute-start | bytes 393224 | tf_op jit(solution)/shard_map/ppermute | solution.py:485
  99.1 4.0 %collective-permute-done.19 = f32[128,256]{1,0:T(8,128)S(1)} collective-permute-done((f32[128,256]{1,0:T(8,128)S(1)}, f32[128,256]{1,0:T(8,128)S(1)}, u32[]{:S(2)}, u32[]{:S(2)}) %collective-permute-start.19) | collective-permute-done | bytes 131104 | tf_op jit(solution)/shard_map/ppermute | solution.py:485
  104.2 4.0 %collective-permute-done.20 = f32[128,256]{1,0:T(8,128)S(1)} collective-permute-done((f32[128,256]{1,0:T(8,128)S(1)}, f32[128,256]{1,0:T(8,128)S(1)}, u32[]{:S(2)}, u32[]{:S(2)}) %collective-permute-start.20) | collective-permute-done | bytes 131104 | tf_op jit(solution)/shard_map/ppermute | solution.py:485
  108.2 2.3 %collective-permute-start.21 = (f32[128,256]{1,0:T(8,128)S(1)}, f32[128,256]{1,0:T(8,128)S(1)}, u32[]{:S(2)}, u32[]{:S(2)}) collective-permute-start(f32[128,256]{1,0:T(8,128)S(1)} %add.30), channel_id=1, source_target_pairs={{0,6},{1,7},{2,4},{3,5},{4,2},{5,3},{6,0},{7,1},{8,14},{9,15},{10,... | collective-permute-start | bytes 393224 | tf_op jit(solution)/shard_map/ppermute | solution.py:485
  110.5 4.6 %collective-permute-done.21 = f32[128,256]{1,0:T(8,128)S(1)} collective-permute-done((f32[128,256]{1,0:T(8,128)S(1)}, f32[128,256]{1,0:T(8,128)S(1)}, u32[]{:S(2)}, u32[]{:S(2)}) %collective-permute-start.21) | collective-permute-done | bytes 131104 | tf_op jit(solution)/shard_map/ppermute | solution.py:485
  116.5 2.4 %shard_map.70 = f32[2,64,512]{2,1,0:T(8,128)} custom-call(f32[128,256]{1,0:T(8,128)S(1)} %add.31.mine, f32[128,256]{1,0:T(8,128)S(1)} %collective-permute-done.22.theirs, bf16[2,2,256,256]{3,2,1,0:T(8,128)(2,1)S(1)} %get-tuple-element.61.q_high, bf16[2,2,256,256]{3,2,1,0:T(8,128)(2,1)S(1)} %get-tuple-element.62.q_low), custom_call_target="tpu_custom_call" | custom-call | flops 1610612736 | bytes 1048576 | tf_op jit(solution)/shard_map/pallas_call | solution.py:370
  (52 shorter events, 13.8 us)
Async XLA Ops:
  0.0 5.0 %copy-start = (f32[1,2,2,256,256]{4,3,2,1,0:T(8,128)S(1)}, f32[1,2,2,256,256]{4,3,2,1,0:T(8,128)}, u32[]{:S(2)}) copy-start(f32[1,2,2,256,256]{4,3,2,1,0:T(8,128)} %param.8) | copy-start | bytes 3145732
  0.0 1.3 %copy-start.1 = (f32[1,2,2,256,256]{4,3,2,1,0:T(8,128)S(1)}, f32[1,2,2,256,256]{4,3,2,1,0:T(8,128)}, u32[]{:S(2)}) copy-start(f32[1,2,2,256,256]{4,3,2,1,0:T(8,128)} %param.7) | copy-start | bytes 3145732
  1.9 21.4 %collective-permute-start = (f32[2,256,256]{2,1,0:T(8,128)S(1)}, f32[2,256,256]{2,1,0:T(8,128)S(1)}, u32[]{:S(2)}, u32[]{:S(2)}) collective-permute-start(f32[2,256,256]{2,1,0:T(8,128)S(1)} %shard_map.55.ahead.mine.a_mine), channel_id=1, source_target_pairs={{0,1},{1,0},{2,3},{3,2},{4,5},{5,4},{6,7},{7,6},{8,9},{9,8},{10,11... | collective-permute-start | bytes 1572872 | tf_op jit(solution)/shard_map/ppermute | solution.py:385
  5.0 1.2 %copy-start.4 = (f32[2,256,512]{2,1,0:T(8,128)S(1)}, f32[2,256,512]{2,1,0:T(8,128)}, u32[]{:S(2)}) copy-start(f32[2,256,512]{2,1,0:T(8,128)} %piece.1) | copy-start | bytes 3145732
  6.2 1.2 %copy-start.5 = (f32[1,2,2,256,256]{4,3,2,1,0:T(8,128)S(1)}, f32[1,2,2,256,256]{4,3,2,1,0:T(8,128)}, u32[]{:S(2)}) copy-start(f32[1,2,2,256,256]{4,3,2,1,0:T(8,128)} %param.6) | copy-start | bytes 3145732
  10.4 12.9 %collective-permute-start.1 = (f32[2,128,256]{2,1,0:T(8,128)S(1)}, f32[2,128,256]{2,1,0:T(8,128)S(1)}, u32[]{:S(2)}, u32[]{:S(2)}) collective-permute-start(f32[2,128,256]{2,1,0:T(8,128)S(1)} %get-tuple-element.36), channel_id=1, source_target_pairs={{0,1},{1,0},{2,3},{3,2},{4,5},{5,4},{6,7},{7,6},{8,9},{9,8},{10,11... | collective-permute-start | bytes 786440 | tf_op jit(solution)/shard_map/ppermute | solution.py:385
  10.5 24.1 %collective-permute-start.7 = (f32[2,256,256]{2,1,0:T(8,128)S(1)}, f32[2,256,256]{2,1,0:T(8,128)S(1)}, u32[]{:S(2)}, u32[]{:S(2)}) collective-permute-start(f32[2,256,256]{2,1,0:T(8,128)S(1)} %get-tuple-element.44.c_mine.mine), channel_id=1, source_target_pairs={{0,1},{1,0},{2,3},{3,2},{4,5},{5,4},{6,7},{7,6},{8,9},{9,8},{10,11... | collective-permute-start | bytes 1572872 | tf_op jit(solution)/shard_map/ppermute | solution.py:385
  24.2 7.9 %collective-permute-start.2 = (f32[2,128,256]{2,1,0:T(8,128)S(1)}, f32[2,128,256]{2,1,0:T(8,128)S(1)}, u32[]{:S(2)}, u32[]{:S(2)}) collective-permute-start(f32[2,128,256]{2,1,0:T(8,128)S(1)} %get-tuple-element.37.base), channel_id=1, source_target_pairs={{0,2},{1,3},{8,10},{9,11},{16,18},{17,19},{24,26},{25,27}} | collective-permute-start | bytes 786440 | tf_op jit(solution)/shard_map/ppermute | solution.py:388
  28.2 22.4 %collective-permute-start.6 = (f32[2,384,256]{2,1,0:T(8,128)S(1)}, f32[2,384,256]{2,1,0:T(8,128)S(1)}, u32[]{:S(2)}, u32[]{:S(2)}) collective-permute-start(f32[2,384,256]{2,1,0:T(8,128)S(1)} %get-tuple-element.43.late_mine), channel_id=1, source_target_pairs={{0,1},{1,0},{2,3},{3,2},{4,5},{5,4},{6,7},{7,6},{8,9},{9,8},{10,11... | collective-permute-start | bytes 2359304 | tf_op jit(solution)/shard_map/ppermute | solution.py:385
  32.5 3.4 %collective-permute-start.3 = (f32[2,128,256]{2,1,0:T(8,128)S(1)}, f32[2,128,256]{2,1,0:T(8,128)S(1)}, u32[]{:S(2)}, u32[]{:S(2)}) collective-permute-start(f32[2,128,256]{2,1,0:T(8,128)S(1)} %shard_map.58), channel_id=1, source_target_pairs={{2,4},{3,5},{10,12},{11,13},{18,20},{19,21},{26,28},{27,29}} | collective-permute-start | bytes 786440 | tf_op jit(solution)/shard_map/ppermute | solution.py:388
  35.2 17.9 %collective-permute-start.10 = (f32[2,256,256]{2,1,0:T(8,128)S(1)}, f32[2,256,256]{2,1,0:T(8,128)S(1)}, u32[]{:S(2)}, u32[]{:S(2)}) collective-permute-start(f32[2,256,256]{2,1,0:T(8,128)S(1)} %shard_map.63.c_mine), channel_id=1, source_target_pairs={{2,4},{3,5},{4,2},{5,3},{10,12},{11,13},{12,10},{13,11},{18,20},{1... | collective-permute-start | bytes 1572872 | tf_op jit(solution)/shard_map/ppermute | solution.py:388
  36.4 0.7 collective-permute-start.4
  51.7 1.4 %collective-permute-start.8 = (f32[2,64,256]{2,1,0:T(8,128)S(1)}, f32[2,64,256]{2,1,0:T(8,128)S(1)}, u32[]{:S(2)}, u32[]{:S(2)}) collective-permute-start(f32[2,64,256]{2,1,0:T(8,128)S(1)} %get-tuple-element.45.mine_a), channel_id=1, source_target_pairs={{6,4},{7,5},{4,2},{5,3},{14,12},{15,13},{12,10},{13,11},{22,20},{2... | collective-permute-start | bytes 393224 | tf_op jit(solution)/shard_map/ppermute | solution.py:388
  52.4 0.7 collective-permute-start.9
  53.9 20.4 %copy-start.2 = (f32[1,2,2,256,256]{4,3,2,1,0:T(8,128)S(1)}, f32[1,2,2,256,256]{4,3,2,1,0:T(8,128)}, u32[]{:S(2)}) copy-start(f32[1,2,2,256,256]{4,3,2,1,0:T(8,128)} %param.7) | copy-start | bytes 3145732
  53.9 16.6 %collective-permute-start.11 = (f32[2,64,256]{2,1,0:T(8,128)S(1)}, f32[2,64,256]{2,1,0:T(8,128)S(1)}, u32[]{:S(2)}, u32[]{:S(2)}) collective-permute-start(f32[2,64,256]{2,1,0:T(8,128)S(1)} %get-tuple-element.48), channel_id=1, source_target_pairs={{6,4},{7,5},{4,2},{5,3},{2,0},{3,1},{14,12},{15,13},{12,10},{13,11... | collective-permute-start | bytes 393224 | tf_op jit(solution)/shard_map/ppermute | solution.py:388
  55.3 16.9 %collective-permute-start.12 = (f32[2,64,256]{2,1,0:T(8,128)S(1)}, f32[2,64,256]{2,1,0:T(8,128)S(1)}, u32[]{:S(2)}, u32[]{:S(2)}) collective-permute-start(f32[2,64,256]{2,1,0:T(8,128)S(1)} %get-tuple-element.49), channel_id=1, source_target_pairs={{4,0},{5,1},{12,8},{13,9},{20,16},{21,17},{28,24},{29,25}} | collective-permute-start | bytes 393224 | tf_op jit(solution)/shard_map/ppermute | solution.py:388
  56.8 17.5 %collective-permute-start.5 = (f32[2,128,256]{2,1,0:T(8,128)S(1)}, f32[2,128,256]{2,1,0:T(8,128)S(1)}, u32[]{:S(2)}, u32[]{:S(2)}) collective-permute-start(f32[2,128,256]{2,1,0:T(8,128)S(1)} %get-tuple-element.40.in_other), channel_id=1, source_target_pairs={{0,1},{1,0},{2,3},{3,2},{4,5},{5,4},{6,7},{7,6},{8,9},{9,8},{10,11... | collective-permute-start | bytes 786440 | tf_op jit(solution)/shard_map/ppermute | solution.py:385
  72.7 1.6 %copy-start.3 = (f32[1,2]{1,0:T(1,128)S(1)}, f32[1,2]{1,0:T(1,128)}, u32[]{:S(2)}) copy-start(f32[1,2]{1,0:T(1,128)} %weights.5) | copy-start | bytes 28
  72.7 6.4 %collective-permute-start.15 = (f32[2,128,256]{2,1,0:T(8,128)S(1)}, f32[2,128,256]{2,1,0:T(8,128)S(1)}, u32[]{:S(2)}, u32[]{:S(2)}) collective-permute-start(f32[2,128,256]{2,1,0:T(8,128)S(1)} %get-tuple-element.55), channel_id=1, source_target_pairs={{0,1},{1,0},{2,3},{3,2},{4,5},{5,4},{6,7},{7,6},{8,9},{9,8},{10,11... | collective-permute-start | bytes 786440 | tf_op jit(solution)/shard_map/ppermute | solution.py:385
  78.0 2.9 %collective-permute-start.13 = (f32[2,128,256]{2,1,0:T(8,128)S(1)}, f32[2,128,256]{2,1,0:T(8,128)S(1)}, u32[]{:S(2)}, u32[]{:S(2)}) collective-permute-start(f32[2,128,256]{2,1,0:T(8,128)S(1)} %get-tuple-element.53), channel_id=1, source_target_pairs={{0,8},{8,0},{16,24},{24,16},{1,9},{9,1},{17,25},{25,17},{2,10},{10... | collective-permute-start | bytes 786440 | tf_op jit(solution)/shard_map/ppermute | solution.py:455
  80.8 1.7 %collective-permute-start.16 = (f32[2,128,256]{2,1,0:T(8,128)S(1)}, f32[2,128,256]{2,1,0:T(8,128)S(1)}, u32[]{:S(2)}, u32[]{:S(2)}) collective-permute-start(f32[2,128,256]{2,1,0:T(8,128)S(1)} %get-tuple-element.57), channel_id=1, source_target_pairs={{0,8},{8,0},{16,24},{24,16},{1,9},{9,1},{17,25},{25,17},{2,10},{10... | collective-permute-start | bytes 786440 | tf_op jit(solution)/shard_map/ppermute | solution.py:455
  80.9 9.2 %collective-permute-start.14 = (f32[2,128,256]{2,1,0:T(8,128)S(1)}, f32[2,128,256]{2,1,0:T(8,128)S(1)}, u32[]{:S(2)}, u32[]{:S(2)}) collective-permute-start(f32[2,128,256]{2,1,0:T(8,128)S(1)} %add.26.own), channel_id=1, source_target_pairs={{0,16},{8,24},{16,0},{24,8},{1,17},{9,25},{17,1},{25,9},{2,18},{10... | collective-permute-start | bytes 786440 | tf_op jit(solution)/shard_map/ppermute | solution.py:455
  82.5 12.8 %collective-permute-start.17 = (f32[2,128,256]{2,1,0:T(8,128)S(1)}, f32[2,128,256]{2,1,0:T(8,128)S(1)}, u32[]{:S(2)}, u32[]{:S(2)}) collective-permute-start(f32[2,128,256]{2,1,0:T(8,128)S(1)} %add.27.theirs), channel_id=1, source_target_pairs={{0,16},{8,24},{16,0},{24,8},{1,17},{9,25},{17,1},{25,9},{2,18},{10... | collective-permute-start | bytes 786440 | tf_op jit(solution)/shard_map/ppermute | solution.py:455
  96.0 1.4 %collective-permute-start.18 = (f32[128,256]{1,0:T(8,128)S(1)}, f32[128,256]{1,0:T(8,128)S(1)}, u32[]{:S(2)}, u32[]{:S(2)}) collective-permute-start(f32[128,256]{1,0:T(8,128)S(1)} %get-tuple-element.59), channel_id=1, source_target_pairs={{0,8},{8,0},{16,24},{24,16},{1,9},{9,1},{17,25},{25,17},{2,10},{10... | collective-permute-start | bytes 393224 | tf_op jit(solution)/shard_map/ppermute | solution.py:455
  97.5 5.6 %collective-permute-start.19 = (f32[128,256]{1,0:T(8,128)S(1)}, f32[128,256]{1,0:T(8,128)S(1)}, u32[]{:S(2)}, u32[]{:S(2)}) collective-permute-start(f32[128,256]{1,0:T(8,128)S(1)} %add.28), channel_id=1, source_target_pairs={{0,1},{1,0},{2,3},{3,2},{4,5},{5,4},{6,7},{7,6},{8,9},{9,8},{10,11... | collective-permute-start | bytes 393224 | tf_op jit(solution)/shard_map/ppermute | solution.py:485
  99.1 16.1 %collective-permute-start.23 = (f32[2,256,256]{2,1,0:T(8,128)S(1)}, f32[2,256,256]{2,1,0:T(8,128)S(1)}, u32[]{:S(2)}, u32[]{:S(2)}) collective-permute-start(f32[2,256,256]{2,1,0:T(8,128)S(1)} %get-tuple-element.60.mine), channel_id=1, source_target_pairs={{0,8},{8,0},{16,24},{24,16},{1,9},{9,1},{17,25},{25,17},{2,10},{10... | collective-permute-start | bytes 1572872 | tf_op jit(solution)/shard_map/ppermute | solution.py:455
  103.1 5.0 %collective-permute-start.20 = (f32[128,256]{1,0:T(8,128)S(1)}, f32[128,256]{1,0:T(8,128)S(1)}, u32[]{:S(2)}, u32[]{:S(2)}) collective-permute-start(f32[128,256]{1,0:T(8,128)S(1)} %add.29), channel_id=1, source_target_pairs={{0,2},{1,3},{2,0},{3,1},{4,6},{5,7},{6,4},{7,5},{8,10},{9,11},{10,... | collective-permute-start | bytes 393224 | tf_op jit(solution)/shard_map/ppermute | solution.py:485
  108.2 6.9 %collective-permute-start.21 = (f32[128,256]{1,0:T(8,128)S(1)}, f32[128,256]{1,0:T(8,128)S(1)}, u32[]{:S(2)}, u32[]{:S(2)}) collective-permute-start(f32[128,256]{1,0:T(8,128)S(1)} %add.30), channel_id=1, source_target_pairs={{0,6},{1,7},{2,4},{3,5},{4,2},{5,3},{6,0},{7,1},{8,14},{9,15},{10,... | collective-permute-start | bytes 393224 | tf_op jit(solution)/shard_map/ppermute | solution.py:485
  115.1 1.4 %collective-permute-start.22 = (f32[128,256]{1,0:T(8,128)S(1)}, f32[128,256]{1,0:T(8,128)S(1)}, u32[]{:S(2)}, u32[]{:S(2)}) collective-permute-start(f32[128,256]{1,0:T(8,128)S(1)} %add.31.mine), channel_id=1, source_target_pairs={{0,8},{8,0},{16,24},{24,16},{1,9},{9,1},{17,25},{25,17},{2,10},{10... | collective-permute-start | bytes 393224 | tf_op jit(solution)/shard_map/ppermute | solution.py:455

commit v6 on v5

--- a/solution.py
+++ b/solution.py
@@ -40,7 +40,10 @@
 
 
 def few(left, parts, dims):
-    left = stacked(left)
+    return few_stacked(stacked(left), parts, dims)
+
+
+def few_stacked(left, parts, dims):
     with_real, with_imag = against(left, parts[0], dims), against(left, parts[1], dims)
     return with_real[0] - with_imag[1], with_imag[0] + with_real[1]
 
@@ -120,7 +123,7 @@
     put(out, value)
 
 
-def local_kernel(piece, pivot, lower, upper, ahead, states, bkeep, bsend, gkeep, cmap, late, work):
+def local_kernel(piece, pivot, lower, upper, ahead, states, bkeep, bsend, gkeep, cmap, cmaps, late, work):
     count, width = pivot.shape[0], pivot.shape[-1]
     half = bkeep.shape[1]
     mine = jnp.where(side(), 0, half)
@@ -153,11 +156,11 @@
         value = minus(levels[number], plain(pair(upper, number), value))
     for part in range(2):
         late[part, :width, :] = value[part]
-    value = pair(upper, count - 1)
+    value = negative(pair(upper, count - 1))
+    put(cmaps.at[count - 1], value)
     for number in range(count - 2, -1, -1):
-        value = plain(pair(upper, number), value)
-    if count % 2:
-        value = negative(value)
+        value = negative(plain(pair(upper, number), value))
+        put(cmaps.at[number], value)
     put(cmap, value)
 
 
@@ -257,7 +260,8 @@
     back_in(pair(work), mid, c_mine, c_theirs, own, other)
 
 
-def swept_kernel(states, in_own, in_theirs, lower, upper, weights, out_own, out_theirs):
+def swept_kernel(states, in_own, in_theirs, lower, upper, c_maps, weights, out_own, out_theirs,
+                 high, low):
     count = states.shape[0]
     half = in_own.shape[1]
     mine = jnp.where(side(), 0, half)
@@ -265,20 +269,27 @@
         carry = pair(carry)
         for number in range(count):
             carry = negative(trans(carry, pair(lower, number)))
-            put(out.at[number], plus(rows_of(states.at[number], start, half), carry))
-
-
-def solved_kernel(swept, entering, upper, weights, keep, send):
+            value = plus(rows_of(states.at[number], start, half), carry)
+            put(out.at[number], value)
+        for number in range(count - 2, -1, -1):
+            value = minus(pair(out, number), trans(value, pair(upper, number)))
+            put(out.at[number], value)
+    for number in range(count):
+        for part in range(2):
+            high[number, part], low[number, part] = halves(c_maps[number, part])
+
+
+def solved_kernel(swept, entering, high, low, weights, keep, send):
     count, width = swept.shape[0], swept.shape[-1]
     wreal, wimag = weights[0, 0], weights[0, 1]
-    carry = pair(entering)
+    left = stacked(pair(entering))
     upward = lax.rem(lax.axis_index("pole"), 2) == 1
-    values = [None] * count
-    for number in range(count - 1, -1, -1):
-        carry = minus(pair(swept, number), trans(carry, pair(upper, number)))
-        values[number] = (
-            wreal * carry[0] - wimag * carry[1], wreal * carry[1] + wimag * carry[0]
-        )
+    values = []
+    for number in range(count):
+        parts = tuple((high[number, part], low[number, part]) for part in range(2))
+        product = few_stacked(left, parts, ((1,), (1,)))
+        value = plus(pair(swept, number), product)
+        values.append((wreal * value[0] - wimag * value[1], wreal * value[1] + wimag * value[0]))
     blocks = count // 2
     for number in range(blocks):
         columns = slice(number * width, (number + 1) * width)
@@ -401,9 +412,10 @@
 
     (a_mine,) = call(map_kernel, [square], lower)
     a_theirs = beside(a_mine)
-    states, b_mine, b_send, g_mine, c_mine, late_mine = scratch(
+    states, b_mine, b_send, g_mine, c_mine, c_maps, late_mine = scratch(
         local_kernel,
-        [(count,) + state, strip, strip, strip, square, (2, width + half, width)],
+        [(count,) + state, strip, strip, strip, square, (count,) + square,
+         (2, width + half, width)],
         [state], subspace, pivot, lower, upper, a_mine, products=2 * count + 3,
     )
     b_theirs = beside(b_send)
@@ -433,14 +445,15 @@
         last = between(last, [(2, 0)])
     else:
         back_inflow = prefix(ends[0], c_node, order[::-1])
-    swept_own, swept_theirs = pl.pallas_call(
+    swept_own, swept_theirs, c_high, c_low = pl.pallas_call(
         swept_kernel,
-        out_shape=[jax.ShapeDtypeStruct((count,) + strip, F32)] * 2,
-        in_specs=[pl.BlockSpec(memory_space=vmem)] * 5
+        out_shape=[jax.ShapeDtypeStruct((count,) + strip, F32)] * 2
+        + [jax.ShapeDtypeStruct((count,) + square, jnp.bfloat16)] * 2,
+        in_specs=[pl.BlockSpec(memory_space=vmem)] * 6
         + [pl.BlockSpec(memory_space=pltpu.SMEM)],
-        out_specs=[pl.BlockSpec(memory_space=vmem)] * 2,
+        out_specs=[pl.BlockSpec(memory_space=vmem)] * 4,
         compiler_params=pltpu.CompilerParams(vmem_limit_bytes=GRANT),
-    )(states, in_own, in_theirs, lower, upper, pole_weights)
+    )(states, in_own, in_theirs, lower, upper, c_maps, pole_weights)
     if short:
         x_own, x_other = scratch(
             back_in_parts_kernel, [strip] * 2, [strip], keep, came, last, mid, c_mine, c_theirs
@@ -462,11 +475,11 @@
         keep, send = pl.pallas_call(
             solved_kernel,
             out_shape=[jax.ShapeDtypeStruct(block, F32)] * 2,
-            in_specs=[pl.BlockSpec(memory_space=vmem)] * 3
+            in_specs=[pl.BlockSpec(memory_space=vmem)] * 4
             + [pl.BlockSpec(memory_space=pltpu.SMEM)],
             out_specs=[pl.BlockSpec(memory_space=vmem)] * 2,
             compiler_params=pltpu.CompilerParams(vmem_limit_bytes=GRANT),
-        )(swept, entering, upper, pole_weights)
+        )(swept, entering, c_high, c_low, pole_weights)
         value, more = keep, over_poles(send, 0)
         for bit in range(1, levels):
             value = value + more

time: 119 us -> 119 us (level)
  waiting for transfers between devices: 68.7 us -> 65.8 us
  starting transfers between devices: 28.7 us -> 30.5 us
    ppermute x3, starting transfers between devices: 5 us -> 6.69 us  [shards(): lax.ppermute(packed, 'rows', [(place, place ^ mask) for place in range(de...]
    ppermute x3, waiting for transfers between devices: 12.6 us -> 10.9 us  [shards(): lax.ppermute(packed, 'rows', [(place, place ^ mask) for place in range(de...]
  transfers between devices with their start and end apart: 24 -> 24, of which waited for: 14 -> 13; matrix products, arithmetic and copies ran while one was open for 0% -> 0% of each run, Pallas kernels for 11% -> 11%
where the time goes in v6:
time: 119 us
  waiting for transfers between devices  65.8 us (55%)
  starting transfers between devices  30.5 us (26%)
  Pallas kernels  17.5 us (15%)
  local copies, waits for them, and re-layouts  4.34 us (4%)
    ppermute x6, waiting for transfers between devices, beside(): return lax.ppermute(value, 'rows', swap)  25.3 us
    ppermute x8, waiting for transfers between devices, between(): lax.ppermute(value, 'rows', [(2 * a + s, 2 * b + s) for a, b in moves for...  15.9 us
    ppermute x7, waiting for transfers between devices, over_poles(): lax.ppermute(value, 'pole', [(place, place ^ 1 << bit) for place in range...  13.7 us
    ppermute x3, waiting for transfers between devices, shards(): lax.ppermute(packed, 'rows', [(place, place ^ mask) for place in range(de...  10.9 us
    ppermute x8, starting transfers between devices, between(): lax.ppermute(value, 'rows', [(2 * a + s, 2 * b + s) for a, b in moves for...  10.3 us
    ppermute x6, starting transfers between devices, beside(): return lax.ppermute(value, 'rows', swap)  10.1 us
    ppermute x3, starting transfers between devices, shards(): lax.ppermute(packed, 'rows', [(place, place ^ mask) for place in range(de...  6.69 us
    pallas_call x4, Pallas kernels, scratch(): pl.pallas_call(body, out_shape=[jax.ShapeDtypeStruct(shape, F32) for shap...  6.54 us
  transfers between devices with their start and end apart: 24, of which 13 were waited for; matrix products, arithmetic and copies ran while one was open for 0% of the time, Pallas kernels for 11%

profile of v6, /device:TPU:0, one launch (start us, length us, event | category | flops | bytes accessed | tf_op | source)
XLA Modules:
  0.0 118.7 jit_solution(16812520176819513083)
XLA Ops:
  0.0 1.2 %copy-done = f32[1,2,2,256,256]{4,3,2,1,0:T(8,128)S(1)} copy-done((f32[1,2,2,256,256]{4,3,2,1,0:T(8,128)S(1)}, f32[1,2,2,256,256]{4,3,2,1,0:T(8,128)}, u32[]{:S(2)}) %copy-start) | copy-done | bytes 1048600
  1.8 3.1 %collective-permute-start = (f32[2,256,256]{2,1,0:T(8,128)S(1)}, f32[2,256,256]{2,1,0:T(8,128)S(1)}, u32[]{:S(2)}, u32[]{:S(2)}) collective-permute-start(f32[2,256,256]{2,1,0:T(8,128)S(1)} %shard_map.55.ahead.mine.a_mine), channel_id=1, source_target_pairs={{0,1},{1,0},{2,3},{3,2},{4,5},{5,4},{6,7},{7,6},{8,9},{9,8},{10,11... | collective-permute-start | bytes 1572872 | tf_op jit(solution)/shard_map/ppermute | solution.py:396
  4.9 1.2 %copy-done.4 = f32[2,256,512]{2,1,0:T(8,128)S(1)} copy-done((f32[2,256,512]{2,1,0:T(8,128)S(1)}, f32[2,256,512]{2,1,0:T(8,128)}, u32[]{:S(2)}) %copy-start.4) | copy-done | bytes 1048600
  6.1 1.2 %copy-done.5 = f32[1,2,2,256,256]{4,3,2,1,0:T(8,128)S(1)} copy-done((f32[1,2,2,256,256]{4,3,2,1,0:T(8,128)S(1)}, f32[1,2,2,256,256]{4,3,2,1,0:T(8,128)}, u32[]{:S(2)}) %copy-start.5) | copy-done | bytes 1048600
  7.3 3.0 %shard_map.56 = (f32[2,2,256,256]{3,2,1,0:T(8,128)S(1)}, f32[2,128,256]{2,1,0:T(8,128)S(1)}, f32[2,128,256]{2,1,0:T(8,128)S(1)}, f32[2,128,256]{2,1,0:T(8,128)S(...) custom-call(f32[2,256,512]{2,1,0:T(8,128)S(1)} %copy-done.4, ...), custom_call_target="tpu_custom_call" | custom-call | flops 2818572288 | bytes 1048576 | tf_op jit(solution)/shard_map/pallas_call | solution.py:381
  11.0 1.5 %collective-permute-start.7 = (f32[2,256,256]{2,1,0:T(8,128)S(1)}, f32[2,256,256]{2,1,0:T(8,128)S(1)}, u32[]{:S(2)}, u32[]{:S(2)}) collective-permute-start(f32[2,256,256]{2,1,0:T(8,128)S(1)} %get-tuple-element.48.c_mine.mine), channel_id=1, source_target_pairs={{0,1},{1,0},{2,3},{3,2},{4,5},{5,4},{6,7},{7,6},{8,9},{9,8},{10,11... | collective-permute-start | bytes 1572872 | tf_op jit(solution)/shard_map/ppermute | solution.py:396
  12.5 10.8 %collective-permute-done.1.btheirs.b_theirs = f32[2,128,256]{2,1,0:T(8,128)S(1)} collective-permute-done((f32[2,128,256]{2,1,0:T(8,128)S(1)}, f32[2,128,256]{2,1,0:T(8,128)S(1)}, u32[]{:S(2)}, u32[]{:S(2)}) %collective-permute-start.1) | collective-permute-done | bytes 262176 | tf_op jit(solution)/shard_map/ppermute | solution.py:396
  24.1 4.0 %collective-permute-start.2 = (f32[2,128,256]{2,1,0:T(8,128)S(1)}, f32[2,128,256]{2,1,0:T(8,128)S(1)}, u32[]{:S(2)}, u32[]{:S(2)}) collective-permute-start(f32[2,128,256]{2,1,0:T(8,128)S(1)} %get-tuple-element.40.base), channel_id=1, source_target_pairs={{0,2},{1,3},{8,10},{9,11},{16,18},{17,19},{24,26},{25,27}} | collective-permute-start | bytes 786440 | tf_op jit(solution)/shard_map/ppermute | solution.py:399
  28.1 1.6 %collective-permute-start.6 = (f32[2,384,256]{2,1,0:T(8,128)S(1)}, f32[2,384,256]{2,1,0:T(8,128)S(1)}, u32[]{:S(2)}, u32[]{:S(2)}) collective-permute-start(f32[2,384,256]{2,1,0:T(8,128)S(1)} %get-tuple-element.47.late_mine), channel_id=1, source_target_pairs={{0,1},{1,0},{2,3},{3,2},{4,5},{5,4},{6,7},{7,6},{8,9},{9,8},{10,11... | collective-permute-start | bytes 2359304 | tf_op jit(solution)/shard_map/ppermute | solution.py:396
  29.7 2.3 %collective-permute-done.2.state = f32[2,128,256]{2,1,0:T(8,128)S(1)} collective-permute-done((f32[2,128,256]{2,1,0:T(8,128)S(1)}, f32[2,128,256]{2,1,0:T(8,128)S(1)}, u32[]{:S(2)}, u32[]{:S(2)}) %collective-permute-start.2) | collective-permute-done | bytes 262176 | tf_op jit(solution)/shard_map/ppermute | solution.py:399
  33.1 1.4 %collective-permute-done.7.c_theirs.theirs = f32[2,256,256]{2,1,0:T(8,128)S(1)} collective-permute-done((f32[2,256,256]{2,1,0:T(8,128)S(1)}, f32[2,256,256]{2,1,0:T(8,128)S(1)}, u32[]{:S(2)}, u32[]{:S(2)}) %collective-permute-start.7) | collective-permute-done | bytes 524320 | tf_op jit(solution)/shard_map/ppermute | solution.py:396
  37.5 13.0 %collective-permute-done.6.late_theirs = f32[2,384,256]{2,1,0:T(8,128)S(1)} collective-permute-done((f32[2,384,256]{2,1,0:T(8,128)S(1)}, f32[2,384,256]{2,1,0:T(8,128)S(1)}, u32[]{:S(2)}, u32[]{:S(2)}) %collective-permute-start.6) | collective-permute-done | bytes 786464 | tf_op jit(solution)/shard_map/ppermute | solution.py:396
  53.8 1.4 %collective-permute-start.11 = (f32[2,64,256]{2,1,0:T(8,128)S(1)}, f32[2,64,256]{2,1,0:T(8,128)S(1)}, u32[]{:S(2)}, u32[]{:S(2)}) collective-permute-start(f32[2,64,256]{2,1,0:T(8,128)S(1)} %get-tuple-element.52), channel_id=1, source_target_pairs={{6,4},{7,5},{4,2},{5,3},{2,0},{3,1},{14,12},{15,13},{12,10},{13,11... | collective-permute-start | bytes 393224 | tf_op jit(solution)/shard_map/ppermute | solution.py:399
  55.2 1.5 %collective-permute-start.12 = (f32[2,64,256]{2,1,0:T(8,128)S(1)}, f32[2,64,256]{2,1,0:T(8,128)S(1)}, u32[]{:S(2)}, u32[]{:S(2)}) collective-permute-start(f32[2,64,256]{2,1,0:T(8,128)S(1)} %get-tuple-element.53), channel_id=1, source_target_pairs={{4,0},{5,1},{12,8},{13,9},{20,16},{21,17},{28,24},{29,25}} | collective-permute-start | bytes 393224 | tf_op jit(solution)/shard_map/ppermute | solution.py:399
  56.7 1.8 %collective-permute-start.5 = (f32[2,128,256]{2,1,0:T(8,128)S(1)}, f32[2,128,256]{2,1,0:T(8,128)S(1)}, u32[]{:S(2)}, u32[]{:S(2)}) collective-permute-start(f32[2,128,256]{2,1,0:T(8,128)S(1)} %get-tuple-element.43.in_other), channel_id=1, source_target_pairs={{0,1},{1,0},{2,3},{3,2},{4,5},{5,4},{6,7},{7,6},{8,9},{9,8},{10,11... | collective-permute-start | bytes 786440 | tf_op jit(solution)/shard_map/ppermute | solution.py:396
  58.5 11.9 %collective-permute-done.11.came = f32[2,64,256]{2,1,0:T(8,128)S(1)} collective-permute-done((f32[2,64,256]{2,1,0:T(8,128)S(1)}, f32[2,64,256]{2,1,0:T(8,128)S(1)}, u32[]{:S(2)}, u32[]{:S(2)}) %collective-permute-start.11) | collective-permute-done | bytes 131104 | tf_op jit(solution)/shard_map/ppermute | solution.py:399
  70.4 1.7 %collective-permute-done.12.last = f32[2,64,256]{2,1,0:T(8,128)S(1)} collective-permute-done((f32[2,64,256]{2,1,0:T(8,128)S(1)}, f32[2,64,256]{2,1,0:T(8,128)S(1)}, u32[]{:S(2)}, u32[]{:S(2)}) %collective-permute-start.12) | collective-permute-done | bytes 131104 | tf_op jit(solution)/shard_map/ppermute | solution.py:399
  72.6 1.6 %collective-permute-start.15 = (f32[2,128,256]{2,1,0:T(8,128)S(1)}, f32[2,128,256]{2,1,0:T(8,128)S(1)}, u32[]{:S(2)}, u32[]{:S(2)}) collective-permute-start(f32[2,128,256]{2,1,0:T(8,128)S(1)} %get-tuple-element.61), channel_id=1, source_target_pairs={{0,1},{1,0},{2,3},{3,2},{4,5},{5,4},{6,7},{7,6},{8,9},{9,8},{10,11... | collective-permute-start | bytes 786440 | tf_op jit(solution)/shard_map/ppermute | solution.py:396
  74.8 3.2 %shard_map.61 = (f32[2,2,128,256]{3,2,1,0:T(8,128)S(1)}, f32[2,2,128,256]{3,2,1,0:T(8,128)S(1)}, bf16[2,2,256,256]{3,2,1,0:T(8,128)(2,1)S(1)}, bf16[2,2,256,256]{3,2,1,0:T(8,128)(2,1)S(1)}) custom-call(f32[2,2,256,256]{3,2,1,0:T(8,128)S(1)} %get-tuple-element.37.states, f32[2,128,256]{2,1,0:T(8,128)S(1)} %get-tuple-element.42.in_own, ...), custom_call_target="tpu_custom_call" | custom-call | tf_op jit(solution)/shard_map/pallas_call | solution.py:448
  78.0 1.2 %shard_map.66 = (f32[2,128,256]{2,1,0:T(8,128)S(1)}, f32[2,128,256]{2,1,0:T(8,128)S(1)}) custom-call(f32[2,2,128,256]{3,2,1,0:T(8,128)S(1)} %get-tuple-element.45.swept, f32[2,128,256]{2,1,0:T(8,128)S(1)} %get-tuple-element.55.entering, bf16[2,2,256,256]{3,2,1,0:T(8,128)(2,1)S(1)} %get-tuple-element.56.high, ...), custom_call_target="tpu_custom_call" | custom-call | tf_op jit(solution)/shard_map/pallas_call | solution.py:475
  79.3 1.2 %shard_map.67 = (f32[2,128,256]{2,1,0:T(8,128)S(1)}, f32[2,128,256]{2,1,0:T(8,128)S(1)}) custom-call(f32[2,2,128,256]{3,2,1,0:T(8,128)S(1)} %get-tuple-element.60.swept, f32[2,128,256]{2,1,0:T(8,128)S(1)} %collective-permute-done.15.entering, bf16[2,2,256,256]{3,2,1,0:T(8,128)(2,1)S(1)} %get-tuple-element.56.high, ...), custom_call_target="tpu_custom_call" | custom-call | tf_op jit(solution)/shard_map/pallas_call | solution.py:475
  81.1 1.5 %collective-permute-start.14 = (f32[2,128,256]{2,1,0:T(8,128)S(1)}, f32[2,128,256]{2,1,0:T(8,128)S(1)}, u32[]{:S(2)}, u32[]{:S(2)}) collective-permute-start(f32[2,128,256]{2,1,0:T(8,128)S(1)} %add.26.own), channel_id=1, source_target_pairs={{0,16},{8,24},{16,0},{24,8},{1,17},{9,25},{17,1},{25,9},{2,18},{10... | collective-permute-start | bytes 786440 | tf_op jit(solution)/shard_map/ppermute | solution.py:468
  83.8 6.5 %collective-permute-done.14.own_more = f32[2,128,256]{2,1,0:T(8,128)S(1)} collective-permute-done((f32[2,128,256]{2,1,0:T(8,128)S(1)}, f32[2,128,256]{2,1,0:T(8,128)S(1)}, u32[]{:S(2)}, u32[]{:S(2)}) %collective-permute-start.14) | collective-permute-done | bytes 262176 | tf_op jit(solution)/shard_map/ppermute | solution.py:468
  90.4 4.7 %collective-permute-done.17.theirs_more = f32[2,128,256]{2,1,0:T(8,128)S(1)} collective-permute-done((f32[2,128,256]{2,1,0:T(8,128)S(1)}, f32[2,128,256]{2,1,0:T(8,128)S(1)}, u32[]{:S(2)}, u32[]{:S(2)}) %collective-permute-start.17) | collective-permute-done | bytes 262176 | tf_op jit(solution)/shard_map/ppermute | solution.py:468
  95.9 1.3 %collective-permute-done.18 = f32[128,256]{1,0:T(8,128)S(1)} collective-permute-done((f32[128,256]{1,0:T(8,128)S(1)}, f32[128,256]{1,0:T(8,128)S(1)}, u32[]{:S(2)}, u32[]{:S(2)}) %collective-permute-start.18) | collective-permute-done | bytes 131104 | tf_op jit(solution)/shard_map/ppermute | solution.py:468
  97.2 1.3 %collective-permute-start.19 = (f32[128,256]{1,0:T(8,128)S(1)}, f32[128,256]{1,0:T(8,128)S(1)}, u32[]{:S(2)}, u32[]{:S(2)}) collective-permute-start(f32[128,256]{1,0:T(8,128)S(1)} %add.28), channel_id=1, source_target_pairs={{0,1},{1,0},{2,3},{3,2},{4,5},{5,4},{6,7},{7,6},{8,9},{9,8},{10,11... | collective-permute-start | bytes 393224 | tf_op jit(solution)/shard_map/ppermute | solution.py:498
  98.5 4.4 %collective-permute-done.19 = f32[128,256]{1,0:T(8,128)S(1)} collective-permute-done((f32[128,256]{1,0:T(8,128)S(1)}, f32[128,256]{1,0:T(8,128)S(1)}, u32[]{:S(2)}, u32[]{:S(2)}) %collective-permute-start.19) | collective-permute-done | bytes 131104 | tf_op jit(solution)/shard_map/ppermute | solution.py:498
  102.9 2.1 %collective-permute-start.20 = (f32[128,256]{1,0:T(8,128)S(1)}, f32[128,256]{1,0:T(8,128)S(1)}, u32[]{:S(2)}, u32[]{:S(2)}) collective-permute-start(f32[128,256]{1,0:T(8,128)S(1)} %add.29), channel_id=1, source_target_pairs={{0,2},{1,3},{2,0},{3,1},{4,6},{5,7},{6,4},{7,5},{8,10},{9,11},{10,... | collective-permute-start | bytes 393224 | tf_op jit(solution)/shard_map/ppermute | solution.py:498
  105.0 3.0 %collective-permute-done.20 = f32[128,256]{1,0:T(8,128)S(1)} collective-permute-done((f32[128,256]{1,0:T(8,128)S(1)}, f32[128,256]{1,0:T(8,128)S(1)}, u32[]{:S(2)}, u32[]{:S(2)}) %collective-permute-start.20) | collective-permute-done | bytes 131104 | tf_op jit(solution)/shard_map/ppermute | solution.py:498
  108.0 3.3 %collective-permute-start.21 = (f32[128,256]{1,0:T(8,128)S(1)}, f32[128,256]{1,0:T(8,128)S(1)}, u32[]{:S(2)}, u32[]{:S(2)}) collective-permute-start(f32[128,256]{1,0:T(8,128)S(1)} %add.30), channel_id=1, source_target_pairs={{0,6},{1,7},{2,4},{3,5},{4,2},{5,3},{6,0},{7,1},{8,14},{9,15},{10,... | collective-permute-start | bytes 393224 | tf_op jit(solution)/shard_map/ppermute | solution.py:498
  111.3 3.6 %collective-permute-done.21 = f32[128,256]{1,0:T(8,128)S(1)} collective-permute-done((f32[128,256]{1,0:T(8,128)S(1)}, f32[128,256]{1,0:T(8,128)S(1)}, u32[]{:S(2)}, u32[]{:S(2)}) %collective-permute-start.21) | collective-permute-done | bytes 131104 | tf_op jit(solution)/shard_map/ppermute | solution.py:498
  116.3 2.4 %shard_map.70 = f32[2,64,512]{2,1,0:T(8,128)} custom-call(f32[128,256]{1,0:T(8,128)S(1)} %add.31.mine, f32[128,256]{1,0:T(8,128)S(1)} %collective-permute-done.22.theirs, bf16[2,2,256,256]{3,2,1,0:T(8,128)(2,1)S(1)} %get-tuple-element.67.q_high, bf16[2,2,256,256]{3,2,1,0:T(8,128)(2,1)S(1)} %get-tuple-element.68.q_low), custom_call_target="tpu_custom_call" | custom-call | flops 1610612736 | bytes 1048576 | tf_op jit(solution)/shard_map/pallas_call | solution.py:381
  (52 shorter events, 14.4 us)
Async XLA Ops:
  0.0 1.2 %copy-start = (f32[1,2,2,256,256]{4,3,2,1,0:T(8,128)S(1)}, f32[1,2,2,256,256]{4,3,2,1,0:T(8,128)}, u32[]{:S(2)}) copy-start(f32[1,2,2,256,256]{4,3,2,1,0:T(8,128)} %param.7) | copy-start | bytes 3145732
  1.2 3.7 %copy-start.2 = (f32[1,2,2,256,256]{4,3,2,1,0:T(8,128)S(1)}, f32[1,2,2,256,256]{4,3,2,1,0:T(8,128)}, u32[]{:S(2)}) copy-start(f32[1,2,2,256,256]{4,3,2,1,0:T(8,128)} %param.8) | copy-start | bytes 3145732
  1.8 21.5 %collective-permute-start = (f32[2,256,256]{2,1,0:T(8,128)S(1)}, f32[2,256,256]{2,1,0:T(8,128)S(1)}, u32[]{:S(2)}, u32[]{:S(2)}) collective-permute-start(f32[2,256,256]{2,1,0:T(8,128)S(1)} %shard_map.55.ahead.mine.a_mine), channel_id=1, source_target_pairs={{0,1},{1,0},{2,3},{3,2},{4,5},{5,4},{6,7},{7,6},{8,9},{9,8},{10,11... | collective-permute-start | bytes 1572872 | tf_op jit(solution)/shard_map/ppermute | solution.py:396
  4.9 1.2 %copy-start.4 = (f32[2,256,512]{2,1,0:T(8,128)S(1)}, f32[2,256,512]{2,1,0:T(8,128)}, u32[]{:S(2)}) copy-start(f32[2,256,512]{2,1,0:T(8,128)} %piece.1) | copy-start | bytes 3145732
  6.1 1.2 %copy-start.5 = (f32[1,2,2,256,256]{4,3,2,1,0:T(8,128)S(1)}, f32[1,2,2,256,256]{4,3,2,1,0:T(8,128)}, u32[]{:S(2)}) copy-start(f32[1,2,2,256,256]{4,3,2,1,0:T(8,128)} %param.6) | copy-start | bytes 3145732
  10.4 12.9 %collective-permute-start.1 = (f32[2,128,256]{2,1,0:T(8,128)S(1)}, f32[2,128,256]{2,1,0:T(8,128)S(1)}, u32[]{:S(2)}, u32[]{:S(2)}) collective-permute-start(f32[2,128,256]{2,1,0:T(8,128)S(1)} %get-tuple-element.39), channel_id=1, source_target_pairs={{0,1},{1,0},{2,3},{3,2},{4,5},{5,4},{6,7},{7,6},{8,9},{9,8},{10,11... | collective-permute-start | bytes 786440 | tf_op jit(solution)/shard_map/ppermute | solution.py:396
  11.0 23.5 %collective-permute-start.7 = (f32[2,256,256]{2,1,0:T(8,128)S(1)}, f32[2,256,256]{2,1,0:T(8,128)S(1)}, u32[]{:S(2)}, u32[]{:S(2)}) collective-permute-start(f32[2,256,256]{2,1,0:T(8,128)S(1)} %get-tuple-element.48.c_mine.mine), channel_id=1, source_target_pairs={{0,1},{1,0},{2,3},{3,2},{4,5},{5,4},{6,7},{7,6},{8,9},{9,8},{10,11... | collective-permute-start | bytes 1572872 | tf_op jit(solution)/shard_map/ppermute | solution.py:396
  24.1 7.9 %collective-permute-start.2 = (f32[2,128,256]{2,1,0:T(8,128)S(1)}, f32[2,128,256]{2,1,0:T(8,128)S(1)}, u32[]{:S(2)}, u32[]{:S(2)}) collective-permute-start(f32[2,128,256]{2,1,0:T(8,128)S(1)} %get-tuple-element.40.base), channel_id=1, source_target_pairs={{0,2},{1,3},{8,10},{9,11},{16,18},{17,19},{24,26},{25,27}} | collective-permute-start | bytes 786440 | tf_op jit(solution)/shard_map/ppermute | solution.py:399
  28.1 22.4 %collective-permute-start.6 = (f32[2,384,256]{2,1,0:T(8,128)S(1)}, f32[2,384,256]{2,1,0:T(8,128)S(1)}, u32[]{:S(2)}, u32[]{:S(2)}) collective-permute-start(f32[2,384,256]{2,1,0:T(8,128)S(1)} %get-tuple-element.47.late_mine), channel_id=1, source_target_pairs={{0,1},{1,0},{2,3},{3,2},{4,5},{5,4},{6,7},{7,6},{8,9},{9,8},{10,11... | collective-permute-start | bytes 2359304 | tf_op jit(solution)/shard_map/ppermute | solution.py:396
  32.4 3.4 %collective-permute-start.3 = (f32[2,128,256]{2,1,0:T(8,128)S(1)}, f32[2,128,256]{2,1,0:T(8,128)S(1)}, u32[]{:S(2)}, u32[]{:S(2)}) collective-permute-start(f32[2,128,256]{2,1,0:T(8,128)S(1)} %shard_map.58), channel_id=1, source_target_pairs={{2,4},{3,5},{10,12},{11,13},{18,20},{19,21},{26,28},{27,29}} | collective-permute-start | bytes 786440 | tf_op jit(solution)/shard_map/ppermute | solution.py:399
  35.1 17.9 %collective-permute-start.10 = (f32[2,256,256]{2,1,0:T(8,128)S(1)}, f32[2,256,256]{2,1,0:T(8,128)S(1)}, u32[]{:S(2)}, u32[]{:S(2)}) collective-permute-start(f32[2,256,256]{2,1,0:T(8,128)S(1)} %shard_map.63.c_mine), channel_id=1, source_target_pairs={{2,4},{3,5},{4,2},{5,3},{10,12},{11,13},{12,10},{13,11},{18,20},{1... | collective-permute-start | bytes 1572872 | tf_op jit(solution)/shard_map/ppermute | solution.py:399
  36.3 0.7 collective-permute-start.4
  51.6 1.4 %collective-permute-start.8 = (f32[2,64,256]{2,1,0:T(8,128)S(1)}, f32[2,64,256]{2,1,0:T(8,128)S(1)}, u32[]{:S(2)}, u32[]{:S(2)}) collective-permute-start(f32[2,64,256]{2,1,0:T(8,128)S(1)} %get-tuple-element.49.mine_a), channel_id=1, source_target_pairs={{6,4},{7,5},{4,2},{5,3},{14,12},{15,13},{12,10},{13,11},{22,20},{2... | collective-permute-start | bytes 393224 | tf_op jit(solution)/shard_map/ppermute | solution.py:399
  52.3 0.7 collective-permute-start.9
  53.8 20.4 %copy-start.1 = (f32[1,2,2,256,256]{4,3,2,1,0:T(8,128)S(1)}, f32[1,2,2,256,256]{4,3,2,1,0:T(8,128)}, u32[]{:S(2)}) copy-start(f32[1,2,2,256,256]{4,3,2,1,0:T(8,128)} %param.7) | copy-start | bytes 3145732
  53.8 16.6 %collective-permute-start.11 = (f32[2,64,256]{2,1,0:T(8,128)S(1)}, f32[2,64,256]{2,1,0:T(8,128)S(1)}, u32[]{:S(2)}, u32[]{:S(2)}) collective-permute-start(f32[2,64,256]{2,1,0:T(8,128)S(1)} %get-tuple-element.52), channel_id=1, source_target_pairs={{6,4},{7,5},{4,2},{5,3},{2,0},{3,1},{14,12},{15,13},{12,10},{13,11... | collective-permute-start | bytes 393224 | tf_op jit(solution)/shard_map/ppermute | solution.py:399
  55.2 16.9 %collective-permute-start.12 = (f32[2,64,256]{2,1,0:T(8,128)S(1)}, f32[2,64,256]{2,1,0:T(8,128)S(1)}, u32[]{:S(2)}, u32[]{:S(2)}) collective-permute-start(f32[2,64,256]{2,1,0:T(8,128)S(1)} %get-tuple-element.53), channel_id=1, source_target_pairs={{4,0},{5,1},{12,8},{13,9},{20,16},{21,17},{28,24},{29,25}} | collective-permute-start | bytes 393224 | tf_op jit(solution)/shard_map/ppermute | solution.py:399
  56.7 17.5 %collective-permute-start.5 = (f32[2,128,256]{2,1,0:T(8,128)S(1)}, f32[2,128,256]{2,1,0:T(8,128)S(1)}, u32[]{:S(2)}, u32[]{:S(2)}) collective-permute-start(f32[2,128,256]{2,1,0:T(8,128)S(1)} %get-tuple-element.43.in_other), channel_id=1, source_target_pairs={{0,1},{1,0},{2,3},{3,2},{4,5},{5,4},{6,7},{7,6},{8,9},{9,8},{10,11... | collective-permute-start | bytes 786440 | tf_op jit(solution)/shard_map/ppermute | solution.py:396
  72.6 6.8 %collective-permute-start.15 = (f32[2,128,256]{2,1,0:T(8,128)S(1)}, f32[2,128,256]{2,1,0:T(8,128)S(1)}, u32[]{:S(2)}, u32[]{:S(2)}) collective-permute-start(f32[2,128,256]{2,1,0:T(8,128)S(1)} %get-tuple-element.61), channel_id=1, source_target_pairs={{0,1},{1,0},{2,3},{3,2},{4,5},{5,4},{6,7},{7,6},{8,9},{9,8},{10,11... | collective-permute-start | bytes 786440 | tf_op jit(solution)/shard_map/ppermute | solution.py:396
  74.2 0.7 copy-start.3
  79.2 1.9 %collective-permute-start.13 = (f32[2,128,256]{2,1,0:T(8,128)S(1)}, f32[2,128,256]{2,1,0:T(8,128)S(1)}, u32[]{:S(2)}, u32[]{:S(2)}) collective-permute-start(f32[2,128,256]{2,1,0:T(8,128)S(1)} %get-tuple-element.59), channel_id=1, source_target_pairs={{0,8},{8,0},{16,24},{24,16},{1,9},{9,1},{17,25},{25,17},{2,10},{10... | collective-permute-start | bytes 786440 | tf_op jit(solution)/shard_map/ppermute | solution.py:468
  80.5 2.1 %collective-permute-start.16 = (f32[2,128,256]{2,1,0:T(8,128)S(1)}, f32[2,128,256]{2,1,0:T(8,128)S(1)}, u32[]{:S(2)}, u32[]{:S(2)}) collective-permute-start(f32[2,128,256]{2,1,0:T(8,128)S(1)} %get-tuple-element.63), channel_id=1, source_target_pairs={{0,8},{8,0},{16,24},{24,16},{1,9},{9,1},{17,25},{25,17},{2,10},{10... | collective-permute-start | bytes 786440 | tf_op jit(solution)/shard_map/ppermute | solution.py:468
  81.1 9.2 %collective-permute-start.14 = (f32[2,128,256]{2,1,0:T(8,128)S(1)}, f32[2,128,256]{2,1,0:T(8,128)S(1)}, u32[]{:S(2)}, u32[]{:S(2)}) collective-permute-start(f32[2,128,256]{2,1,0:T(8,128)S(1)} %add.26.own), channel_id=1, source_target_pairs={{0,16},{8,24},{16,0},{24,8},{1,17},{9,25},{17,1},{25,9},{2,18},{10... | collective-permute-start | bytes 786440 | tf_op jit(solution)/shard_map/ppermute | solution.py:468
  82.7 12.3 %collective-permute-start.17 = (f32[2,128,256]{2,1,0:T(8,128)S(1)}, f32[2,128,256]{2,1,0:T(8,128)S(1)}, u32[]{:S(2)}, u32[]{:S(2)}) collective-permute-start(f32[2,128,256]{2,1,0:T(8,128)S(1)} %add.27.theirs), channel_id=1, source_target_pairs={{0,16},{8,24},{16,0},{24,8},{1,17},{9,25},{17,1},{25,9},{2,18},{10... | collective-permute-start | bytes 786440 | tf_op jit(solution)/shard_map/ppermute | solution.py:468
  95.8 1.4 %collective-permute-start.18 = (f32[128,256]{1,0:T(8,128)S(1)}, f32[128,256]{1,0:T(8,128)S(1)}, u32[]{:S(2)}, u32[]{:S(2)}) collective-permute-start(f32[128,256]{1,0:T(8,128)S(1)} %get-tuple-element.65), channel_id=1, source_target_pairs={{0,8},{8,0},{16,24},{24,16},{1,9},{9,1},{17,25},{25,17},{2,10},{10... | collective-permute-start | bytes 393224 | tf_op jit(solution)/shard_map/ppermute | solution.py:468
  97.2 5.6 %collective-permute-start.19 = (f32[128,256]{1,0:T(8,128)S(1)}, f32[128,256]{1,0:T(8,128)S(1)}, u32[]{:S(2)}, u32[]{:S(2)}) collective-permute-start(f32[128,256]{1,0:T(8,128)S(1)} %add.28), channel_id=1, source_target_pairs={{0,1},{1,0},{2,3},{3,2},{4,5},{5,4},{6,7},{7,6},{8,9},{9,8},{10,11... | collective-permute-start | bytes 393224 | tf_op jit(solution)/shard_map/ppermute | solution.py:498
  98.5 16.5 %collective-permute-start.23 = (f32[2,256,256]{2,1,0:T(8,128)S(1)}, f32[2,256,256]{2,1,0:T(8,128)S(1)}, u32[]{:S(2)}, u32[]{:S(2)}) collective-permute-start(f32[2,256,256]{2,1,0:T(8,128)S(1)} %get-tuple-element.66.mine), channel_id=1, source_target_pairs={{0,8},{8,0},{16,24},{24,16},{1,9},{9,1},{17,25},{25,17},{2,10},{10... | collective-permute-start | bytes 1572872 | tf_op jit(solution)/shard_map/ppermute | solution.py:468
  102.9 5.1 %collective-permute-start.20 = (f32[128,256]{1,0:T(8,128)S(1)}, f32[128,256]{1,0:T(8,128)S(1)}, u32[]{:S(2)}, u32[]{:S(2)}) collective-permute-start(f32[128,256]{1,0:T(8,128)S(1)} %add.29), channel_id=1, source_target_pairs={{0,2},{1,3},{2,0},{3,1},{4,6},{5,7},{6,4},{7,5},{8,10},{9,11},{10,... | collective-permute-start | bytes 393224 | tf_op jit(solution)/shard_map/ppermute | solution.py:498
  108.0 6.9 %collective-permute-start.21 = (f32[128,256]{1,0:T(8,128)S(1)}, f32[128,256]{1,0:T(8,128)S(1)}, u32[]{:S(2)}, u32[]{:S(2)}) collective-permute-start(f32[128,256]{1,0:T(8,128)S(1)} %add.30), channel_id=1, source_target_pairs={{0,6},{1,7},{2,4},{3,5},{4,2},{5,3},{6,0},{7,1},{8,14},{9,15},{10,... | collective-permute-start | bytes 393224 | tf_op jit(solution)/shard_map/ppermute | solution.py:498
  114.9 1.4 %collective-permute-start.22 = (f32[128,256]{1,0:T(8,128)S(1)}, f32[128,256]{1,0:T(8,128)S(1)}, u32[]{:S(2)}, u32[]{:S(2)}) collective-permute-start(f32[128,256]{1,0:T(8,128)S(1)} %add.31.mine), channel_id=1, source_target_pairs={{0,8},{8,0},{16,24},{24,16},{1,9},{9,1},{17,25},{25,17},{2,10},{10... | collective-permute-start | bytes 393224 | tf_op jit(solution)/shard_map/ppermute | solution.py:468

commit v7 on v6

--- a/solution.py
+++ b/solution.py
@@ -260,8 +260,7 @@
     back_in(pair(work), mid, c_mine, c_theirs, own, other)
 
 
-def swept_kernel(states, in_own, in_theirs, lower, upper, c_maps, weights, out_own, out_theirs,
-                 high, low):
+def swept_kernel(states, in_own, in_theirs, lower, upper, c_maps, weights, out_own, out_theirs):
     count = states.shape[0]
     half = in_own.shape[1]
     mine = jnp.where(side(), 0, half)
@@ -274,20 +273,17 @@
         for number in range(count - 2, -1, -1):
             value = minus(pair(out, number), trans(value, pair(upper, number)))
             put(out.at[number], value)
-    for number in range(count):
-        for part in range(2):
-            high[number, part], low[number, part] = halves(c_maps[number, part])
-
-
-def solved_kernel(swept, entering, high, low, weights, keep, send):
+
+
+def solved_kernel(swept, entering, c_maps, weights, keep, send):
     count, width = swept.shape[0], swept.shape[-1]
     wreal, wimag = weights[0, 0], weights[0, 1]
     left = stacked(pair(entering))
     upward = lax.rem(lax.axis_index("pole"), 2) == 1
     values = []
     for number in range(count):
-        parts = tuple((high[number, part], low[number, part]) for part in range(2))
-        product = few_stacked(left, parts, ((1,), (1,)))
+        maps = pair(c_maps, number)
+        product = few_stacked(left, (halves(maps[0]), halves(maps[1])), ((1,), (1,)))
         value = plus(pair(swept, number), product)
         values.append((wreal * value[0] - wimag * value[1], wreal * value[1] + wimag * value[0]))
     blocks = count // 2
@@ -445,13 +441,12 @@
         last = between(last, [(2, 0)])
     else:
         back_inflow = prefix(ends[0], c_node, order[::-1])
-    swept_own, swept_theirs, c_high, c_low = pl.pallas_call(
+    swept_own, swept_theirs = pl.pallas_call(
         swept_kernel,
-        out_shape=[jax.ShapeDtypeStruct((count,) + strip, F32)] * 2
-        + [jax.ShapeDtypeStruct((count,) + square, jnp.bfloat16)] * 2,
+        out_shape=[jax.ShapeDtypeStruct((count,) + strip, F32)] * 2,
         in_specs=[pl.BlockSpec(memory_space=vmem)] * 6
         + [pl.BlockSpec(memory_space=pltpu.SMEM)],
-        out_specs=[pl.BlockSpec(memory_space=vmem)] * 4,
+        out_specs=[pl.BlockSpec(memory_space=vmem)] * 2,
         compiler_params=pltpu.CompilerParams(vmem_limit_bytes=GRANT),
     )(states, in_own, in_theirs, lower, upper, c_maps, pole_weights)
     if short:
@@ -475,11 +470,11 @@
         keep, send = pl.pallas_call(
             solved_kernel,
             out_shape=[jax.ShapeDtypeStruct(block, F32)] * 2,
-            in_specs=[pl.BlockSpec(memory_space=vmem)] * 4
+            in_specs=[pl.BlockSpec(memory_space=vmem)] * 3
             + [pl.BlockSpec(memory_space=pltpu.SMEM)],
             out_specs=[pl.BlockSpec(memory_space=vmem)] * 2,
             compiler_params=pltpu.CompilerParams(vmem_limit_bytes=GRANT),
-        )(swept, entering, c_high, c_low, pole_weights)
+        )(swept, entering, c_maps, pole_weights)
         value, more = keep, over_poles(send, 0)
         for bit in range(1, levels):
             value = value + more
@@ -494,7 +489,7 @@
     )
     packed = packed + over_poles(packed_send, 0)
     for bit in range(devices.bit_length() - 1):
-        mask = (2 << bit) - 2 if bit else 1
+        mask = 1 << bit
         packed = packed + lax.ppermute(
             packed, "rows", [(place, place ^ mask) for place in range(devices)]
         )

time: 119 us -> 120 us (level)
  no operation moved by 1% of the time
where the time goes in v7:
time: 120 us
  waiting for transfers between devices  66.7 us (56%)
  starting transfers between devices  31.2 us (26%)
  Pallas kernels  17.3 us (14%)
  local copies, waits for them, and re-layouts  4.34 us (4%)
    ppermute x6, waiting for transfers between devices, beside(): return lax.ppermute(value, 'rows', swap)  25.3 us
    ppermute x8, waiting for transfers between devices, between(): lax.ppermute(value, 'rows', [(2 * a + s, 2 * b + s) for a, b in moves for...  15.9 us
    ppermute x7, waiting for transfers between devices, over_poles(): lax.ppermute(value, 'pole', [(place, place ^ 1 << bit) for place in range...  13.7 us
    ppermute x3, waiting for transfers between devices, shards(): lax.ppermute(packed, 'rows', [(place, place ^ mask) for place in range(de...  11.7 us
    ppermute x8, starting transfers between devices, between(): lax.ppermute(value, 'rows', [(2 * a + s, 2 * b + s) for a, b in moves for...  10.3 us
    ppermute x6, starting transfers between devices, beside(): return lax.ppermute(value, 'rows', swap)  10.1 us
    ppermute x3, starting transfers between devices, shards(): lax.ppermute(packed, 'rows', [(place, place ^ mask) for place in range(de...  7.34 us
    pallas_call x4, Pallas kernels, scratch(): pl.pallas_call(body, out_shape=[jax.ShapeDtypeStruct(shape, F32) for shap...  6.54 us
  transfers between devices with their start and end apart: 24, of which 13 were waited for; matrix products, arithmetic and copies ran while one was open for 0% of the time, Pallas kernels for 11%

profile of v7, /device:TPU:0, one launch (start us, length us, event | category | flops | bytes accessed | tf_op | source)
XLA Modules:
  0.0 120.0 jit_solution(13307643751964681332)
XLA Ops:
  0.0 1.2 %copy-done = f32[1,2,2,256,256]{4,3,2,1,0:T(8,128)S(1)} copy-done((f32[1,2,2,256,256]{4,3,2,1,0:T(8,128)S(1)}, f32[1,2,2,256,256]{4,3,2,1,0:T(8,128)}, u32[]{:S(2)}) %copy-start) | copy-done | bytes 1048600
  1.8 3.1 %collective-permute-start = (f32[2,256,256]{2,1,0:T(8,128)S(1)}, f32[2,256,256]{2,1,0:T(8,128)S(1)}, u32[]{:S(2)}, u32[]{:S(2)}) collective-permute-start(f32[2,256,256]{2,1,0:T(8,128)S(1)} %shard_map.55.ahead.mine.a_mine), channel_id=1, source_target_pairs={{0,1},{1,0},{2,3},{3,2},{4,5},{5,4},{6,7},{7,6},{8,9},{9,8},{10,11... | collective-permute-start | bytes 1572872 | tf_op jit(solution)/shard_map/ppermute | solution.py:392
  4.9 1.2 %copy-done.4 = f32[2,256,512]{2,1,0:T(8,128)S(1)} copy-done((f32[2,256,512]{2,1,0:T(8,128)S(1)}, f32[2,256,512]{2,1,0:T(8,128)}, u32[]{:S(2)}) %copy-start.4) | copy-done | bytes 1048600
  6.1 1.2 %copy-done.5 = f32[1,2,2,256,256]{4,3,2,1,0:T(8,128)S(1)} copy-done((f32[1,2,2,256,256]{4,3,2,1,0:T(8,128)S(1)}, f32[1,2,2,256,256]{4,3,2,1,0:T(8,128)}, u32[]{:S(2)}) %copy-start.5) | copy-done | bytes 1048600
  7.3 3.0 %shard_map.56 = (f32[2,2,256,256]{3,2,1,0:T(8,128)S(1)}, f32[2,128,256]{2,1,0:T(8,128)S(1)}, f32[2,128,256]{2,1,0:T(8,128)S(1)}, f32[2,128,256]{2,1,0:T(8,128)S(...) custom-call(f32[2,256,512]{2,1,0:T(8,128)S(1)} %copy-done.4, ...), custom_call_target="tpu_custom_call" | custom-call | flops 2818572288 | bytes 1048576 | tf_op jit(solution)/shard_map/pallas_call | solution.py:377
  11.0 1.5 %collective-permute-start.7 = (f32[2,256,256]{2,1,0:T(8,128)S(1)}, f32[2,256,256]{2,1,0:T(8,128)S(1)}, u32[]{:S(2)}, u32[]{:S(2)}) collective-permute-start(f32[2,256,256]{2,1,0:T(8,128)S(1)} %get-tuple-element.46.c_mine.mine), channel_id=1, source_target_pairs={{0,1},{1,0},{2,3},{3,2},{4,5},{5,4},{6,7},{7,6},{8,9},{9,8},{10,11... | collective-permute-start | bytes 1572872 | tf_op jit(solution)/shard_map/ppermute | solution.py:392
  12.5 10.8 %collective-permute-done.1.btheirs.b_theirs = f32[2,128,256]{2,1,0:T(8,128)S(1)} collective-permute-done((f32[2,128,256]{2,1,0:T(8,128)S(1)}, f32[2,128,256]{2,1,0:T(8,128)S(1)}, u32[]{:S(2)}, u32[]{:S(2)}) %collective-permute-start.1) | collective-permute-done | bytes 262176 | tf_op jit(solution)/shard_map/ppermute | solution.py:392
  24.1 4.0 %collective-permute-start.2 = (f32[2,128,256]{2,1,0:T(8,128)S(1)}, f32[2,128,256]{2,1,0:T(8,128)S(1)}, u32[]{:S(2)}, u32[]{:S(2)}) collective-permute-start(f32[2,128,256]{2,1,0:T(8,128)S(1)} %get-tuple-element.38.base), channel_id=1, source_target_pairs={{0,2},{1,3},{8,10},{9,11},{16,18},{17,19},{24,26},{25,27}} | collective-permute-start | bytes 786440 | tf_op jit(solution)/shard_map/ppermute | solution.py:395
  28.1 1.6 %collective-permute-start.6 = (f32[2,384,256]{2,1,0:T(8,128)S(1)}, f32[2,384,256]{2,1,0:T(8,128)S(1)}, u32[]{:S(2)}, u32[]{:S(2)}) collective-permute-start(f32[2,384,256]{2,1,0:T(8,128)S(1)} %get-tuple-element.45.late_mine), channel_id=1, source_target_pairs={{0,1},{1,0},{2,3},{3,2},{4,5},{5,4},{6,7},{7,6},{8,9},{9,8},{10,11... | collective-permute-start | bytes 2359304 | tf_op jit(solution)/shard_map/ppermute | solution.py:392
  29.7 2.3 %collective-permute-done.2.state = f32[2,128,256]{2,1,0:T(8,128)S(1)} collective-permute-done((f32[2,128,256]{2,1,0:T(8,128)S(1)}, f32[2,128,256]{2,1,0:T(8,128)S(1)}, u32[]{:S(2)}, u32[]{:S(2)}) %collective-permute-start.2) | collective-permute-done | bytes 262176 | tf_op jit(solution)/shard_map/ppermute | solution.py:395
  33.1 1.4 %collective-permute-done.7.c_theirs.theirs = f32[2,256,256]{2,1,0:T(8,128)S(1)} collective-permute-done((f32[2,256,256]{2,1,0:T(8,128)S(1)}, f32[2,256,256]{2,1,0:T(8,128)S(1)}, u32[]{:S(2)}, u32[]{:S(2)}) %collective-permute-start.7) | collective-permute-done | bytes 524320 | tf_op jit(solution)/shard_map/ppermute | solution.py:392
  37.5 13.0 %collective-permute-done.6.late_theirs = f32[2,384,256]{2,1,0:T(8,128)S(1)} collective-permute-done((f32[2,384,256]{2,1,0:T(8,128)S(1)}, f32[2,384,256]{2,1,0:T(8,128)S(1)}, u32[]{:S(2)}, u32[]{:S(2)}) %collective-permute-start.6) | collective-permute-done | bytes 786464 | tf_op jit(solution)/shard_map/ppermute | solution.py:392
  53.8 1.4 %collective-permute-start.11 = (f32[2,64,256]{2,1,0:T(8,128)S(1)}, f32[2,64,256]{2,1,0:T(8,128)S(1)}, u32[]{:S(2)}, u32[]{:S(2)}) collective-permute-start(f32[2,64,256]{2,1,0:T(8,128)S(1)} %get-tuple-element.50), channel_id=1, source_target_pairs={{6,4},{7,5},{4,2},{5,3},{2,0},{3,1},{14,12},{15,13},{12,10},{13,11... | collective-permute-start | bytes 393224 | tf_op jit(solution)/shard_map/ppermute | solution.py:395
  55.2 1.5 %collective-permute-start.12 = (f32[2,64,256]{2,1,0:T(8,128)S(1)}, f32[2,64,256]{2,1,0:T(8,128)S(1)}, u32[]{:S(2)}, u32[]{:S(2)}) collective-permute-start(f32[2,64,256]{2,1,0:T(8,128)S(1)} %get-tuple-element.51), channel_id=1, source_target_pairs={{4,0},{5,1},{12,8},{13,9},{20,16},{21,17},{28,24},{29,25}} | collective-permute-start | bytes 393224 | tf_op jit(solution)/shard_map/ppermute | solution.py:395
  56.7 1.8 %collective-permute-start.5 = (f32[2,128,256]{2,1,0:T(8,128)S(1)}, f32[2,128,256]{2,1,0:T(8,128)S(1)}, u32[]{:S(2)}, u32[]{:S(2)}) collective-permute-start(f32[2,128,256]{2,1,0:T(8,128)S(1)} %get-tuple-element.41.in_other), channel_id=1, source_target_pairs={{0,1},{1,0},{2,3},{3,2},{4,5},{5,4},{6,7},{7,6},{8,9},{9,8},{10,11... | collective-permute-start | bytes 786440 | tf_op jit(solution)/shard_map/ppermute | solution.py:392
  58.5 11.9 %collective-permute-done.11.came = f32[2,64,256]{2,1,0:T(8,128)S(1)} collective-permute-done((f32[2,64,256]{2,1,0:T(8,128)S(1)}, f32[2,64,256]{2,1,0:T(8,128)S(1)}, u32[]{:S(2)}, u32[]{:S(2)}) %collective-permute-start.11) | collective-permute-done | bytes 131104 | tf_op jit(solution)/shard_map/ppermute | solution.py:395
  70.4 1.7 %collective-permute-done.12.last = f32[2,64,256]{2,1,0:T(8,128)S(1)} collective-permute-done((f32[2,64,256]{2,1,0:T(8,128)S(1)}, f32[2,64,256]{2,1,0:T(8,128)S(1)}, u32[]{:S(2)}, u32[]{:S(2)}) %collective-permute-start.12) | collective-permute-done | bytes 131104 | tf_op jit(solution)/shard_map/ppermute | solution.py:395
  72.6 1.6 %collective-permute-start.15 = (f32[2,128,256]{2,1,0:T(8,128)S(1)}, f32[2,128,256]{2,1,0:T(8,128)S(1)}, u32[]{:S(2)}, u32[]{:S(2)}) collective-permute-start(f32[2,128,256]{2,1,0:T(8,128)S(1)} %get-tuple-element.57), channel_id=1, source_target_pairs={{0,1},{1,0},{2,3},{3,2},{4,5},{5,4},{6,7},{7,6},{8,9},{9,8},{10,11... | collective-permute-start | bytes 786440 | tf_op jit(solution)/shard_map/ppermute | solution.py:392
  74.8 3.0 %shard_map.61 = (f32[2,2,128,256]{3,2,1,0:T(8,128)S(1)}, f32[2,2,128,256]{3,2,1,0:T(8,128)S(1)}) custom-call(f32[2,2,256,256]{3,2,1,0:T(8,128)S(1)} %get-tuple-element.35.states, f32[2,128,256]{2,1,0:T(8,128)S(1)} %get-tuple-element.40.in_own, f32[2,128,256]{2,1,0:T(8,128)S(1)} %collective-permute-done.5.in_theirs, f32[2,2,256,256]{3,2,1,0:T(8,128)S(1)} %bitcast.5, ...), custom_call_target="tpu_custom_call" | custom-call | tf_op jit(solution)/shard_map/pallas_call | solution.py:444
  77.9 1.2 %shard_map.66 = (f32[2,128,256]{2,1,0:T(8,128)S(1)}, f32[2,128,256]{2,1,0:T(8,128)S(1)}) custom-call(f32[2,2,128,256]{3,2,1,0:T(8,128)S(1)} %get-tuple-element.43.swept, f32[2,128,256]{2,1,0:T(8,128)S(1)} %get-tuple-element.53.entering, f32[2,2,256,256]{3,2,1,0:T(8,128)S(1)} %get-tuple-element.42.c_maps, f32[1,2]{1,0:T(1,128)S(1)} %copy-done.3), custom_call_target="tpu_custom_call" | custom-call | tf_op jit(solution)/shard_map/pallas_call | solution.py:470
  79.2 1.2 %shard_map.67 = (f32[2,128,256]{2,1,0:T(8,128)S(1)}, f32[2,128,256]{2,1,0:T(8,128)S(1)}) custom-call(f32[2,2,128,256]{3,2,1,0:T(8,128)S(1)} %get-tuple-element.56.swept, f32[2,128,256]{2,1,0:T(8,128)S(1)} %collective-permute-done.15.entering, f32[2,2,256,256]{3,2,1,0:T(8,128)S(1)} %get-tuple-element.42.c_maps, f32[1,2]{1,0:T(1,128)S(1)} %copy-done.3), custom_call_target="tpu_custom_call" | custom-call | tf_op jit(solution)/shard_map/pallas_call | solution.py:470
  81.0 1.5 %collective-permute-start.14 = (f32[2,128,256]{2,1,0:T(8,128)S(1)}, f32[2,128,256]{2,1,0:T(8,128)S(1)}, u32[]{:S(2)}, u32[]{:S(2)}) collective-permute-start(f32[2,128,256]{2,1,0:T(8,128)S(1)} %add.26.own), channel_id=1, source_target_pairs={{0,16},{8,24},{16,0},{24,8},{1,17},{9,25},{17,1},{25,9},{2,18},{10... | collective-permute-start | bytes 786440 | tf_op jit(solution)/shard_map/ppermute | solution.py:463
  83.7 6.5 %collective-permute-done.14.own_more = f32[2,128,256]{2,1,0:T(8,128)S(1)} collective-permute-done((f32[2,128,256]{2,1,0:T(8,128)S(1)}, f32[2,128,256]{2,1,0:T(8,128)S(1)}, u32[]{:S(2)}, u32[]{:S(2)}) %collective-permute-start.14) | collective-permute-done | bytes 262176 | tf_op jit(solution)/shard_map/ppermute | solution.py:463
  90.2 4.7 %collective-permute-done.17.theirs_more = f32[2,128,256]{2,1,0:T(8,128)S(1)} collective-permute-done((f32[2,128,256]{2,1,0:T(8,128)S(1)}, f32[2,128,256]{2,1,0:T(8,128)S(1)}, u32[]{:S(2)}, u32[]{:S(2)}) %collective-permute-start.17) | collective-permute-done | bytes 262176 | tf_op jit(solution)/shard_map/ppermute | solution.py:463
  95.7 1.3 %collective-permute-done.18 = f32[128,256]{1,0:T(8,128)S(1)} collective-permute-done((f32[128,256]{1,0:T(8,128)S(1)}, f32[128,256]{1,0:T(8,128)S(1)}, u32[]{:S(2)}, u32[]{:S(2)}) %collective-permute-start.18) | collective-permute-done | bytes 131104 | tf_op jit(solution)/shard_map/ppermute | solution.py:463
  97.1 1.4 %collective-permute-start.19 = (f32[128,256]{1,0:T(8,128)S(1)}, f32[128,256]{1,0:T(8,128)S(1)}, u32[]{:S(2)}, u32[]{:S(2)}) collective-permute-start(f32[128,256]{1,0:T(8,128)S(1)} %add.28), channel_id=1, source_target_pairs={{0,1},{1,0},{2,3},{3,2},{4,5},{5,4},{6,7},{7,6},{8,9},{9,8},{10,11... | collective-permute-start | bytes 393224 | tf_op jit(solution)/shard_map/ppermute | solution.py:493
  98.5 4.2 %collective-permute-done.19 = f32[128,256]{1,0:T(8,128)S(1)} collective-permute-done((f32[128,256]{1,0:T(8,128)S(1)}, f32[128,256]{1,0:T(8,128)S(1)}, u32[]{:S(2)}, u32[]{:S(2)}) %collective-permute-start.19) | collective-permute-done | bytes 131104 | tf_op jit(solution)/shard_map/ppermute | solution.py:493
  102.7 2.1 %collective-permute-start.20 = (f32[128,256]{1,0:T(8,128)S(1)}, f32[128,256]{1,0:T(8,128)S(1)}, u32[]{:S(2)}, u32[]{:S(2)}) collective-permute-start(f32[128,256]{1,0:T(8,128)S(1)} %add.29), channel_id=1, source_target_pairs={{0,2},{1,3},{2,0},{3,1},{4,6},{5,7},{6,4},{7,5},{8,10},{9,11},{10,... | collective-permute-start | bytes 393224 | tf_op jit(solution)/shard_map/ppermute | solution.py:493
  104.8 3.0 %collective-permute-done.20 = f32[128,256]{1,0:T(8,128)S(1)} collective-permute-done((f32[128,256]{1,0:T(8,128)S(1)}, f32[128,256]{1,0:T(8,128)S(1)}, u32[]{:S(2)}, u32[]{:S(2)}) %collective-permute-start.20) | collective-permute-done | bytes 131104 | tf_op jit(solution)/shard_map/ppermute | solution.py:493
  107.8 3.8 %collective-permute-start.21 = (f32[128,256]{1,0:T(8,128)S(1)}, f32[128,256]{1,0:T(8,128)S(1)}, u32[]{:S(2)}, u32[]{:S(2)}) collective-permute-start(f32[128,256]{1,0:T(8,128)S(1)} %add.30), channel_id=1, source_target_pairs={{0,4},{1,5},{2,6},{3,7},{4,0},{5,1},{6,2},{7,3},{8,12},{9,13},{10,... | collective-permute-start | bytes 393224 | tf_op jit(solution)/shard_map/ppermute | solution.py:493
  111.6 4.6 %collective-permute-done.21 = f32[128,256]{1,0:T(8,128)S(1)} collective-permute-done((f32[128,256]{1,0:T(8,128)S(1)}, f32[128,256]{1,0:T(8,128)S(1)}, u32[]{:S(2)}, u32[]{:S(2)}) %collective-permute-start.21) | collective-permute-done | bytes 131104 | tf_op jit(solution)/shard_map/ppermute | solution.py:493
  117.6 2.4 %shard_map.70 = f32[2,64,512]{2,1,0:T(8,128)} custom-call(f32[128,256]{1,0:T(8,128)S(1)} %add.31.mine, f32[128,256]{1,0:T(8,128)S(1)} %collective-permute-done.22.theirs, bf16[2,2,256,256]{3,2,1,0:T(8,128)(2,1)S(1)} %get-tuple-element.63.q_high, bf16[2,2,256,256]{3,2,1,0:T(8,128)(2,1)S(1)} %get-tuple-element.64.q_low), custom_call_target="tpu_custom_call" | custom-call | flops 1610612736 | bytes 1048576 | tf_op jit(solution)/shard_map/pallas_call | solution.py:377
  (52 shorter events, 14.4 us)
Async XLA Ops:
  0.0 1.2 %copy-start = (f32[1,2,2,256,256]{4,3,2,1,0:T(8,128)S(1)}, f32[1,2,2,256,256]{4,3,2,1,0:T(8,128)}, u32[]{:S(2)}) copy-start(f32[1,2,2,256,256]{4,3,2,1,0:T(8,128)} %param.7) | copy-start | bytes 3145732
  1.2 3.7 %copy-start.2 = (f32[1,2,2,256,256]{4,3,2,1,0:T(8,128)S(1)}, f32[1,2,2,256,256]{4,3,2,1,0:T(8,128)}, u32[]{:S(2)}) copy-start(f32[1,2,2,256,256]{4,3,2,1,0:T(8,128)} %param.8) | copy-start | bytes 3145732
  1.8 21.5 %collective-permute-start = (f32[2,256,256]{2,1,0:T(8,128)S(1)}, f32[2,256,256]{2,1,0:T(8,128)S(1)}, u32[]{:S(2)}, u32[]{:S(2)}) collective-permute-start(f32[2,256,256]{2,1,0:T(8,128)S(1)} %shard_map.55.ahead.mine.a_mine), channel_id=1, source_target_pairs={{0,1},{1,0},{2,3},{3,2},{4,5},{5,4},{6,7},{7,6},{8,9},{9,8},{10,11... | collective-permute-start | bytes 1572872 | tf_op jit(solution)/shard_map/ppermute | solution.py:392
  4.9 1.2 %copy-start.4 = (f32[2,256,512]{2,1,0:T(8,128)S(1)}, f32[2,256,512]{2,1,0:T(8,128)}, u32[]{:S(2)}) copy-start(f32[2,256,512]{2,1,0:T(8,128)} %piece.1) | copy-start | bytes 3145732
  6.1 1.2 %copy-start.5 = (f32[1,2,2,256,256]{4,3,2,1,0:T(8,128)S(1)}, f32[1,2,2,256,256]{4,3,2,1,0:T(8,128)}, u32[]{:S(2)}) copy-start(f32[1,2,2,256,256]{4,3,2,1,0:T(8,128)} %param.6) | copy-start | bytes 3145732
  10.4 12.9 %collective-permute-start.1 = (f32[2,128,256]{2,1,0:T(8,128)S(1)}, f32[2,128,256]{2,1,0:T(8,128)S(1)}, u32[]{:S(2)}, u32[]{:S(2)}) collective-permute-start(f32[2,128,256]{2,1,0:T(8,128)S(1)} %get-tuple-element.37), channel_id=1, source_target_pairs={{0,1},{1,0},{2,3},{3,2},{4,5},{5,4},{6,7},{7,6},{8,9},{9,8},{10,11... | collective-permute-start | bytes 786440 | tf_op jit(solution)/shard_map/ppermute | solution.py:392
  11.0 23.5 %collective-permute-start.7 = (f32[2,256,256]{2,1,0:T(8,128)S(1)}, f32[2,256,256]{2,1,0:T(8,128)S(1)}, u32[]{:S(2)}, u32[]{:S(2)}) collective-permute-start(f32[2,256,256]{2,1,0:T(8,128)S(1)} %get-tuple-element.46.c_mine.mine), channel_id=1, source_target_pairs={{0,1},{1,0},{2,3},{3,2},{4,5},{5,4},{6,7},{7,6},{8,9},{9,8},{10,11... | collective-permute-start | bytes 1572872 | tf_op jit(solution)/shard_map/ppermute | solution.py:392
  24.1 7.9 %collective-permute-start.2 = (f32[2,128,256]{2,1,0:T(8,128)S(1)}, f32[2,128,256]{2,1,0:T(8,128)S(1)}, u32[]{:S(2)}, u32[]{:S(2)}) collective-permute-start(f32[2,128,256]{2,1,0:T(8,128)S(1)} %get-tuple-element.38.base), channel_id=1, source_target_pairs={{0,2},{1,3},{8,10},{9,11},{16,18},{17,19},{24,26},{25,27}} | collective-permute-start | bytes 786440 | tf_op jit(solution)/shard_map/ppermute | solution.py:395
  28.1 22.4 %collective-permute-start.6 = (f32[2,384,256]{2,1,0:T(8,128)S(1)}, f32[2,384,256]{2,1,0:T(8,128)S(1)}, u32[]{:S(2)}, u32[]{:S(2)}) collective-permute-start(f32[2,384,256]{2,1,0:T(8,128)S(1)} %get-tuple-element.45.late_mine), channel_id=1, source_target_pairs={{0,1},{1,0},{2,3},{3,2},{4,5},{5,4},{6,7},{7,6},{8,9},{9,8},{10,11... | collective-permute-start | bytes 2359304 | tf_op jit(solution)/shard_map/ppermute | solution.py:392
  32.4 3.4 %collective-permute-start.3 = (f32[2,128,256]{2,1,0:T(8,128)S(1)}, f32[2,128,256]{2,1,0:T(8,128)S(1)}, u32[]{:S(2)}, u32[]{:S(2)}) collective-permute-start(f32[2,128,256]{2,1,0:T(8,128)S(1)} %shard_map.58), channel_id=1, source_target_pairs={{2,4},{3,5},{10,12},{11,13},{18,20},{19,21},{26,28},{27,29}} | collective-permute-start | bytes 786440 | tf_op jit(solution)/shard_map/ppermute | solution.py:395
  35.1 17.9 %collective-permute-start.10 = (f32[2,256,256]{2,1,0:T(8,128)S(1)}, f32[2,256,256]{2,1,0:T(8,128)S(1)}, u32[]{:S(2)}, u32[]{:S(2)}) collective-permute-start(f32[2,256,256]{2,1,0:T(8,128)S(1)} %shard_map.63.c_mine), channel_id=1, source_target_pairs={{2,4},{3,5},{4,2},{5,3},{10,12},{11,13},{12,10},{13,11},{18,20},{1... | collective-permute-start | bytes 1572872 | tf_op jit(solution)/shard_map/ppermute | solution.py:395
  36.3 0.7 collective-permute-start.4
  51.6 1.4 %collective-permute-start.8 = (f32[2,64,256]{2,1,0:T(8,128)S(1)}, f32[2,64,256]{2,1,0:T(8,128)S(1)}, u32[]{:S(2)}, u32[]{:S(2)}) collective-permute-start(f32[2,64,256]{2,1,0:T(8,128)S(1)} %get-tuple-element.47.mine_a), channel_id=1, source_target_pairs={{6,4},{7,5},{4,2},{5,3},{14,12},{15,13},{12,10},{13,11},{22,20},{2... | collective-permute-start | bytes 393224 | tf_op jit(solution)/shard_map/ppermute | solution.py:395
  52.3 0.7 collective-permute-start.9
  53.8 20.4 %copy-start.1 = (f32[1,2,2,256,256]{4,3,2,1,0:T(8,128)S(1)}, f32[1,2,2,256,256]{4,3,2,1,0:T(8,128)}, u32[]{:S(2)}) copy-start(f32[1,2,2,256,256]{4,3,2,1,0:T(8,128)} %param.7) | copy-start | bytes 3145732
  53.8 16.6 %collective-permute-start.11 = (f32[2,64,256]{2,1,0:T(8,128)S(1)}, f32[2,64,256]{2,1,0:T(8,128)S(1)}, u32[]{:S(2)}, u32[]{:S(2)}) collective-permute-start(f32[2,64,256]{2,1,0:T(8,128)S(1)} %get-tuple-element.50), channel_id=1, source_target_pairs={{6,4},{7,5},{4,2},{5,3},{2,0},{3,1},{14,12},{15,13},{12,10},{13,11... | collective-permute-start | bytes 393224 | tf_op jit(solution)/shard_map/ppermute | solution.py:395
  55.2 16.9 %collective-permute-start.12 = (f32[2,64,256]{2,1,0:T(8,128)S(1)}, f32[2,64,256]{2,1,0:T(8,128)S(1)}, u32[]{:S(2)}, u32[]{:S(2)}) collective-permute-start(f32[2,64,256]{2,1,0:T(8,128)S(1)} %get-tuple-element.51), channel_id=1, source_target_pairs={{4,0},{5,1},{12,8},{13,9},{20,16},{21,17},{28,24},{29,25}} | collective-permute-start | bytes 393224 | tf_op jit(solution)/shard_map/ppermute | solution.py:395
  56.7 17.5 %collective-permute-start.5 = (f32[2,128,256]{2,1,0:T(8,128)S(1)}, f32[2,128,256]{2,1,0:T(8,128)S(1)}, u32[]{:S(2)}, u32[]{:S(2)}) collective-permute-start(f32[2,128,256]{2,1,0:T(8,128)S(1)} %get-tuple-element.41.in_other), channel_id=1, source_target_pairs={{0,1},{1,0},{2,3},{3,2},{4,5},{5,4},{6,7},{7,6},{8,9},{9,8},{10,11... | collective-permute-start | bytes 786440 | tf_op jit(solution)/shard_map/ppermute | solution.py:392
  72.6 6.6 %collective-permute-start.15 = (f32[2,128,256]{2,1,0:T(8,128)S(1)}, f32[2,128,256]{2,1,0:T(8,128)S(1)}, u32[]{:S(2)}, u32[]{:S(2)}) collective-permute-start(f32[2,128,256]{2,1,0:T(8,128)S(1)} %get-tuple-element.57), channel_id=1, source_target_pairs={{0,1},{1,0},{2,3},{3,2},{4,5},{5,4},{6,7},{7,6},{8,9},{9,8},{10,11... | collective-permute-start | bytes 786440 | tf_op jit(solution)/shard_map/ppermute | solution.py:392
  74.2 0.7 copy-start.3
  79.1 1.9 %collective-permute-start.13 = (f32[2,128,256]{2,1,0:T(8,128)S(1)}, f32[2,128,256]{2,1,0:T(8,128)S(1)}, u32[]{:S(2)}, u32[]{:S(2)}) collective-permute-start(f32[2,128,256]{2,1,0:T(8,128)S(1)} %get-tuple-element.55), channel_id=1, source_target_pairs={{0,8},{8,0},{16,24},{24,16},{1,9},{9,1},{17,25},{25,17},{2,10},{10... | collective-permute-start | bytes 786440 | tf_op jit(solution)/shard_map/ppermute | solution.py:463
  80.4 2.1 %collective-permute-start.16 = (f32[2,128,256]{2,1,0:T(8,128)S(1)}, f32[2,128,256]{2,1,0:T(8,128)S(1)}, u32[]{:S(2)}, u32[]{:S(2)}) collective-permute-start(f32[2,128,256]{2,1,0:T(8,128)S(1)} %get-tuple-element.59), channel_id=1, source_target_pairs={{0,8},{8,0},{16,24},{24,16},{1,9},{9,1},{17,25},{25,17},{2,10},{10... | collective-permute-start | bytes 786440 | tf_op jit(solution)/shard_map/ppermute | solution.py:463
  81.0 9.2 %collective-permute-start.14 = (f32[2,128,256]{2,1,0:T(8,128)S(1)}, f32[2,128,256]{2,1,0:T(8,128)S(1)}, u32[]{:S(2)}, u32[]{:S(2)}) collective-permute-start(f32[2,128,256]{2,1,0:T(8,128)S(1)} %add.26.own), channel_id=1, source_target_pairs={{0,16},{8,24},{16,0},{24,8},{1,17},{9,25},{17,1},{25,9},{2,18},{10... | collective-permute-start | bytes 786440 | tf_op jit(solution)/shard_map/ppermute | solution.py:463
  82.6 12.3 %collective-permute-start.17 = (f32[2,128,256]{2,1,0:T(8,128)S(1)}, f32[2,128,256]{2,1,0:T(8,128)S(1)}, u32[]{:S(2)}, u32[]{:S(2)}) collective-permute-start(f32[2,128,256]{2,1,0:T(8,128)S(1)} %add.27.theirs), channel_id=1, source_target_pairs={{0,16},{8,24},{16,0},{24,8},{1,17},{9,25},{17,1},{25,9},{2,18},{10... | collective-permute-start | bytes 786440 | tf_op jit(solution)/shard_map/ppermute | solution.py:463
  95.6 1.4 %collective-permute-start.18 = (f32[128,256]{1,0:T(8,128)S(1)}, f32[128,256]{1,0:T(8,128)S(1)}, u32[]{:S(2)}, u32[]{:S(2)}) collective-permute-start(f32[128,256]{1,0:T(8,128)S(1)} %get-tuple-element.61), channel_id=1, source_target_pairs={{0,8},{8,0},{16,24},{24,16},{1,9},{9,1},{17,25},{25,17},{2,10},{10... | collective-permute-start | bytes 393224 | tf_op jit(solution)/shard_map/ppermute | solution.py:463
  97.1 5.6 %collective-permute-start.19 = (f32[128,256]{1,0:T(8,128)S(1)}, f32[128,256]{1,0:T(8,128)S(1)}, u32[]{:S(2)}, u32[]{:S(2)}) collective-permute-start(f32[128,256]{1,0:T(8,128)S(1)} %add.28), channel_id=1, source_target_pairs={{0,1},{1,0},{2,3},{3,2},{4,5},{5,4},{6,7},{7,6},{8,9},{9,8},{10,11... | collective-permute-start | bytes 393224 | tf_op jit(solution)/shard_map/ppermute | solution.py:493
  98.5 17.8 %collective-permute-start.23 = (f32[2,256,256]{2,1,0:T(8,128)S(1)}, f32[2,256,256]{2,1,0:T(8,128)S(1)}, u32[]{:S(2)}, u32[]{:S(2)}) collective-permute-start(f32[2,256,256]{2,1,0:T(8,128)S(1)} %get-tuple-element.62.mine), channel_id=1, source_target_pairs={{0,8},{8,0},{16,24},{24,16},{1,9},{9,1},{17,25},{25,17},{2,10},{10... | collective-permute-start | bytes 1572872 | tf_op jit(solution)/shard_map/ppermute | solution.py:463
  102.7 5.1 %collective-permute-start.20 = (f32[128,256]{1,0:T(8,128)S(1)}, f32[128,256]{1,0:T(8,128)S(1)}, u32[]{:S(2)}, u32[]{:S(2)}) collective-permute-start(f32[128,256]{1,0:T(8,128)S(1)} %add.29), channel_id=1, source_target_pairs={{0,2},{1,3},{2,0},{3,1},{4,6},{5,7},{6,4},{7,5},{8,10},{9,11},{10,... | collective-permute-start | bytes 393224 | tf_op jit(solution)/shard_map/ppermute | solution.py:493
  107.8 8.4 %collective-permute-start.21 = (f32[128,256]{1,0:T(8,128)S(1)}, f32[128,256]{1,0:T(8,128)S(1)}, u32[]{:S(2)}, u32[]{:S(2)}) collective-permute-start(f32[128,256]{1,0:T(8,128)S(1)} %add.30), channel_id=1, source_target_pairs={{0,4},{1,5},{2,6},{3,7},{4,0},{5,1},{6,2},{7,3},{8,12},{9,13},{10,... | collective-permute-start | bytes 393224 | tf_op jit(solution)/shard_map/ppermute | solution.py:493
  116.2 1.4 %collective-permute-start.22 = (f32[128,256]{1,0:T(8,128)S(1)}, f32[128,256]{1,0:T(8,128)S(1)}, u32[]{:S(2)}, u32[]{:S(2)}) collective-permute-start(f32[128,256]{1,0:T(8,128)S(1)} %add.31.mine), channel_id=1, source_target_pairs={{0,8},{8,0},{16,24},{24,16},{1,9},{9,1},{17,25},{25,17},{2,10},{10... | collective-permute-start | bytes 393224 | tf_op jit(solution)/shard_map/ppermute | solution.py:463
